TPU v7x, 32 devices: a whole 2x2x4 slice. The times are simulated.
32 devices in a mesh: fsdp: 32 (over z, y, x, core).
Axes of the slice: x: 2, y: 2, z: 4, core: 2. Of those that a mesh axis runs over, the one named last changes fastest.
Arguments:
- tokens: bfloat16 [2, 128, 128, 1536], P(None, 'fsdp'), may hold values from -6 to 6
- in_weight: bfloat16 [1536, 6448], P('fsdp'), may hold values from -0.15625 to 0.15625
- conv_weight: bfloat16 [3328, 4], P('fsdp'), may hold values from -3 to 3
- conv_bias: bfloat16 [3328], P('fsdp'), may hold values from -3 to 3
- dt_bias: float32 [48], replicated, may hold values from -6.5 to -4.5
- a_log: float32 [48], replicated, may hold values from 0 to 2.8
- skip_d: float32 [48], replicated, may hold values from 0.5 to 1.5
- norm_scale: bfloat16 [1536], P('fsdp'), may hold values from 0.5 to 1.5
- gate_scale: bfloat16 [3072], P('fsdp'), may hold values from 0.5 to 1.5
- out_weight: bfloat16 [3072, 1536], P('fsdp'), may hold values from -0.109375 to 0.109375
- grad_out: bfloat16 [2, 128, 128, 1536], P(None, 'fsdp'), may hold values from -6 to 6
Outputs:
- output: bfloat16 [2, 128, 128, 1536], P(None, 'fsdp')
- d_tokens: float32 [2, 128, 128, 1536], P(None, 'fsdp')
- d_in_weight: float32 [1536, 6448], P('fsdp')
- d_conv_weight: float32 [3328, 4], P('fsdp')
- d_conv_bias: float32 [3328], P('fsdp')
- d_dt_bias: float32 [48], replicated
- d_a_log: float32 [48], replicated
- d_skip_d: float32 [48], replicated
- d_norm_scale: float32 [1536], P('fsdp')
- d_gate_scale: float32 [3072], P('fsdp')
- d_out_weight: float32 [3072, 1536], P('fsdp')
All inputs are finite; a program needn't handle non-finite values.
Results may differ from a plain program's by a relative error of at most 0.0093.
Values may be sent and summed in bfloat16 or wider, within the bound.
A program may use at most 320 MiB of HBM per device.

v0:
```python
import jax
import jax.numpy as jnp
from jax import lax
from jax.sharding import PartitionSpec as P

epsilon = 1e-05


def batched(form, left, right):
    return jnp.einsum(form, left, right, preferred_element_type=jnp.float32)


def silu_grad(value):
    sigma = jax.nn.sigmoid(value)
    return sigma * (1.0 + value * (1.0 - sigma))


def rows_product(left, right):
    return lax.dot_general(
        left, right, (((0,), (0,)), ((), ())), preferred_element_type=jnp.float32
    )


def layer_forward(block, weights, params):
    in_weight, conv_weight, conv_bias, norm_scale, gate_scale, out_weight = weights
    dt_bias, a_log, skip_d = params
    seq_count, seq_length, width = block.shape
    inner_width = out_weight.shape[0]
    head_count = a_log.shape[0]
    head_dim = inner_width // head_count
    channels = conv_weight.shape[0]
    state_width = (channels - inner_width) // 2
    kernel_width = conv_weight.shape[1]
    row_count = seq_count * seq_length
    u_full = block.astype(jnp.float32)
    rstd_in = lax.rsqrt(jnp.mean(u_full * u_full, axis=-1, keepdims=True) + epsilon)
    u_hat = u_full * rstd_in
    normed = (u_hat * norm_scale.astype(jnp.float32)).astype(jnp.bfloat16).reshape(row_count, width)
    projected = jnp.dot(normed, in_weight, preferred_element_type=jnp.float32).astype(jnp.bfloat16)
    gate_in = (
        projected[:, :inner_width].astype(jnp.float32).reshape(seq_count, seq_length, inner_width)
    )
    conv_in = projected[:, inner_width : inner_width + channels].reshape(
        seq_count, seq_length, channels
    )
    dt_raw = (
        projected[:, inner_width + channels :]
        .astype(jnp.float32)
        .reshape(seq_count, seq_length, head_count)
    )
    conv_pad = jnp.pad(conv_in, ((0, 0), (kernel_width - 1, 0), (0, 0))).astype(jnp.float32)
    taps = conv_weight.astype(jnp.float32)
    conv_out = jnp.zeros((seq_count, seq_length, channels), jnp.float32) + conv_bias.astype(
        jnp.float32
    )
    for offset in range(kernel_width):
        conv_out = conv_out + conv_pad[:, offset : offset + seq_length, :] * taps[:, offset]
    active = jax.nn.silu(conv_out).astype(jnp.bfloat16)
    x_heads = active[..., :inner_width].reshape(seq_count, seq_length, head_count, head_dim)
    b_mat = active[..., inner_width : inner_width + state_width]
    c_mat = active[..., inner_width + state_width :]
    dt_pre = dt_raw + dt_bias
    step_size = jax.nn.softplus(dt_pre)
    decay_rate = -jnp.exp(a_log)
    step_heads = jnp.transpose(step_size, (0, 2, 1))
    log_decay = jnp.cumsum(step_heads * decay_rate[:, None], axis=-1)
    causal = jnp.arange(seq_length)[:, None] >= jnp.arange(seq_length)[None, :]
    spread = log_decay[..., :, None] - log_decay[..., None, :]
    decay = jnp.where(causal, jnp.exp(jnp.minimum(spread, 0.0)), 0.0)
    scores = batched("sln,smn->slm", c_mat, b_mat)
    mixing = (scores[:, None] * decay * step_heads[:, :, None, :]).astype(jnp.bfloat16)
    ssd = batched("shtr,srhp->sthp", mixing, x_heads) + skip_d[:, None] * x_heads.astype(
        jnp.float32
    )
    ssd = ssd.reshape(seq_count, seq_length, inner_width)
    gate_act = jax.nn.silu(gate_in)
    gated = ssd * gate_act
    rstd_gate = lax.rsqrt(jnp.mean(gated * gated, axis=-1, keepdims=True) + epsilon)
    gated_hat = gated * rstd_gate
    mixed = (
        (gated_hat * gate_scale.astype(jnp.float32))
        .astype(jnp.bfloat16)
        .reshape(row_count, inner_width)
    )
    branch = jnp.dot(mixed, out_weight, preferred_element_type=jnp.float32)
    output = (
        (u_full.reshape(row_count, width) + branch)
        .astype(jnp.bfloat16)
        .reshape(seq_count, seq_length, width)
    )
    saved = (
        u_hat,
        rstd_in,
        normed,
        gate_in,
        conv_pad,
        conv_out,
        x_heads,
        b_mat,
        c_mat,
        dt_pre,
        step_heads,
        decay_rate,
        decay,
        scores,
        mixing,
        ssd,
        gate_act,
        gated_hat,
        rstd_gate,
        mixed,
    )
    return (output, saved)


def layer_backward(grad_block, saved, weights, params):
    in_weight, conv_weight, conv_bias, norm_scale, gate_scale, out_weight = weights
    dt_bias, a_log, skip_d = params
    (
        u_hat,
        rstd_in,
        normed,
        gate_in,
        conv_pad,
        conv_out,
        x_heads,
        b_mat,
        c_mat,
        dt_pre,
        step_heads,
        decay_rate,
        decay,
        scores,
        mixing,
        ssd,
        gate_act,
        gated_hat,
        rstd_gate,
        mixed,
    ) = saved
    seq_count, seq_length, width = grad_block.shape
    inner_width = out_weight.shape[0]
    head_count = a_log.shape[0]
    head_dim = inner_width // head_count
    kernel_width = conv_weight.shape[1]
    row_count = seq_count * seq_length
    grad_rows = grad_block.reshape(row_count, width)
    d_out_weight = rows_product(mixed, grad_rows)
    d_mixed = lax.dot_general(
        grad_rows, out_weight, (((1,), (1,)), ((), ())), preferred_element_type=jnp.float32
    ).reshape(seq_count, seq_length, inner_width)
    d_gate_scale = jnp.sum(d_mixed * gated_hat, axis=(0, 1))
    d_hat = d_mixed * gate_scale.astype(jnp.float32)
    d_gated = rstd_gate * (d_hat - gated_hat * jnp.mean(d_hat * gated_hat, axis=-1, keepdims=True))
    d_ssd = d_gated * gate_act
    d_gate_in = d_gated * ssd * silu_grad(gate_in)
    d_ssd_heads = d_ssd.reshape(seq_count, seq_length, head_count, head_dim)
    d_ssd_low = d_ssd_heads.astype(jnp.bfloat16)
    d_skip = jnp.sum(d_ssd_heads * x_heads.astype(jnp.float32), axis=(0, 1, 3))
    d_x_heads = batched("shtr,sthp->srhp", mixing, d_ssd_low) + skip_d[:, None] * d_ssd_heads
    d_mixing = batched("sthp,srhp->shtr", d_ssd_low, x_heads)
    path = d_mixing * decay
    d_scores = jnp.sum(path * step_heads[:, :, None, :], axis=1).astype(jnp.bfloat16)
    through = path * scores[:, None]
    weighted = through * step_heads[:, :, None, :]
    d_log = jnp.sum(weighted, axis=3) - jnp.sum(weighted, axis=2)
    d_steps = lax.cumsum(d_log, axis=2, reverse=True)
    d_step_heads = jnp.sum(through, axis=2) + d_steps * decay_rate[:, None]
    d_a_log = jnp.sum(d_steps * step_heads, axis=(0, 2)) * decay_rate
    d_dt_raw = jnp.transpose(d_step_heads, (0, 2, 1)) * jax.nn.sigmoid(dt_pre)
    d_dt_bias = jnp.sum(d_dt_raw, axis=(0, 1))
    d_c_mat = batched("slm,smn->sln", d_scores, b_mat)
    d_b_mat = batched("slm,sln->smn", d_scores, c_mat)
    d_active = jnp.concatenate(
        [d_x_heads.reshape(seq_count, seq_length, inner_width), d_b_mat, d_c_mat], axis=-1
    )
    d_conv_out = d_active * silu_grad(conv_out)
    d_conv_bias = jnp.sum(d_conv_out, axis=(0, 1))
    taps = conv_weight.astype(jnp.float32)
    d_conv_weight = jnp.stack(
        [
            jnp.sum(d_conv_out * conv_pad[:, offset : offset + seq_length, :], axis=(0, 1))
            for offset in range(kernel_width)
        ],
        axis=1,
    )
    d_pad = jnp.pad(d_conv_out, ((0, 0), (0, kernel_width - 1), (0, 0)))
    d_conv_in = jnp.zeros_like(d_conv_out)
    for offset in range(kernel_width):
        begin = kernel_width - 1 - offset
        d_conv_in = d_conv_in + taps[:, offset] * d_pad[:, begin : begin + seq_length, :]
    d_projected = (
        jnp.concatenate([d_gate_in, d_conv_in, d_dt_raw], axis=-1)
        .astype(jnp.bfloat16)
        .reshape(row_count, -1)
    )
    d_in_weight = rows_product(normed, d_projected)
    d_normed = lax.dot_general(
        d_projected, in_weight, (((1,), (1,)), ((), ())), preferred_element_type=jnp.float32
    ).reshape(seq_count, seq_length, width)
    d_norm_scale = jnp.sum(d_normed * u_hat, axis=(0, 1))
    d_uhat = d_normed * norm_scale.astype(jnp.float32)
    d_input = grad_block.astype(jnp.float32) + rstd_in * (
        d_uhat - u_hat * jnp.mean(d_uhat * u_hat, axis=-1, keepdims=True)
    )
    grads = (d_in_weight, d_conv_weight, d_conv_bias, d_norm_scale, d_gate_scale, d_out_weight)
    return (d_input, grads, (d_dt_bias, d_a_log, d_skip))


def local(
    tokens,
    in_weight,
    conv_weight,
    conv_bias,
    dt_bias,
    a_log,
    skip_d,
    norm_scale,
    gate_scale,
    out_weight,
    grad_out,
):
    micro_count = tokens.shape[0]
    params = (dt_bias, a_log, skip_d)

    def gather_weights():
        return (
            lax.all_gather(in_weight, "fsdp", axis=0, tiled=True),
            lax.all_gather(conv_weight, "fsdp", axis=0, tiled=True),
            lax.all_gather(conv_bias, "fsdp", axis=0, tiled=True),
            lax.all_gather(norm_scale, "fsdp", axis=0, tiled=True),
            lax.all_gather(gate_scale, "fsdp", axis=0, tiled=True),
            lax.all_gather(out_weight, "fsdp", axis=0, tiled=True),
        )

    outputs = []
    d_inputs = []
    totals = None
    head_totals = None
    for micro_index in range(micro_count):
        forward_set = gather_weights()
        output, saved = layer_forward(tokens[micro_index], forward_set, params)
        backward_set = gather_weights()
        d_input, grads, head_grads = layer_backward(
            grad_out[micro_index], saved, backward_set, params
        )
        outputs.append(output)
        d_inputs.append(d_input)
        if totals is None:
            totals = grads
            head_totals = head_grads
        else:
            totals = jax.tree.map(jnp.add, totals, grads)
            head_totals = jax.tree.map(jnp.add, head_totals, head_grads)
    grad_shards = (
        lax.psum_scatter(totals[0], "fsdp", scatter_dimension=0, tiled=True),
        lax.psum_scatter(totals[1], "fsdp", scatter_dimension=0, tiled=True),
        lax.psum_scatter(totals[2], "fsdp", scatter_dimension=0, tiled=True),
        lax.psum_scatter(totals[3], "fsdp", scatter_dimension=0, tiled=True),
        lax.psum_scatter(totals[4], "fsdp", scatter_dimension=0, tiled=True),
        lax.psum_scatter(totals[5], "fsdp", scatter_dimension=0, tiled=True),
    )
    head_sums = lax.psum((head_totals[0], head_totals[1], head_totals[2]), "fsdp")
    return (
        jnp.stack(outputs),
        jnp.stack(d_inputs),
        grad_shards[0],
        grad_shards[1],
        grad_shards[2],
        head_sums[0],
        head_sums[1],
        head_sums[2],
        grad_shards[3],
        grad_shards[4],
        grad_shards[5],
    )


def solution(mesh):
    placed = (
        P(None, "fsdp", None, None),
        P("fsdp", None),
        P("fsdp", None),
        P("fsdp"),
        P(),
        P(),
        P(),
        P("fsdp"),
        P("fsdp"),
        P("fsdp", None),
        P(None, "fsdp", None, None),
    )
    return jax.shard_map(
        local,
        mesh=mesh,
        in_specs=placed,
        out_specs=(
            P(None, "fsdp", None, None),
            P(None, "fsdp", None, None),
            P("fsdp", None),
            P("fsdp", None),
            P("fsdp"),
            P(),
            P(),
            P(),
            P("fsdp"),
            P("fsdp"),
            P("fsdp", None),
        ),
        check_vma=False,
    )
```

profile of v0, /device:TPU:0, one launch (start us, length us, event | category | flops | bytes accessed | tf_op | source)
XLA Modules:
  0.0 1369.5 jit_solution(9758379837161499685)
XLA Ops:
  11.3 43.6 %all-reduce.12 = (bf16[1536]{0:T(1024)(128)(2,1)S(1)}, bf16[3328]{0:T(1024)(128)(2,1)S(1)}, bf16[3072]{0:T(1024)(128)(2,1)S(1)}) all-reduce(bf16[1536]{0:T(1024)(128)(2,1)S(1)} %dynamic-update-slice.1, bf16[3328]{0:T(1024)(128)(2,1)S(1)} %dynamic-update-slice, bf16[3072]{0:T(1024)(128)(2,1)S(1)} %dynamic-update-slice.2), channel_id=1, replica_groups=mesh['fsdp'=32] {'fsdp'}, use_global_device_ids=true, to_apply=%add.5 | all-reduce | flops 7936 | bytes 31744
  54.9 41.2 %all-gather = bf16[32,104,4]{1,2,0:T(4,128)(2,1)S(1)} all-gather(bf16[1,104,4]{1,2,0:T(4,128)(2,1)} %bitcast.237), channel_id=1, replica_groups=mesh['fsdp'=32] {'fsdp'}, dimensions={0}, use_global_device_ids=true | all-gather | bytes 27456 | tf_op jit(solution)/shard_map/all_gather | solution.py:229
  107.1 9.9 fusion.6
  117.0 109.5 %all-gather.4.cloned.1.call-done = bf16[1536,6448]{1,0:T(8,128)(2,1)} async-done(((bf16[48,6448]{1,0:T(8,128)(2,1)}), bf16[1536,6448]{1,0:T(8,128)(2,1)}) %all-gather.4.cloned.1.call-update) | async-done | bytes 19808272 | tf_op jit(solution)/shard_map/all_gather | solution.py:228
  226.5 16.6 %convolution_convert_fusion = bf16[512,6448]{0,1:T(8,128)(2,1)} fusion(bf16[512,1536]{1,0:T(8,128)(2,1)S(1)} %copy-done.19, bf16[1536,6448]{1,0:T(8,128)(2,1)} %all-gather.4.cloned.1.call-done), kind=kOutput, calls=%fused_computation.20 | convolution fusion | flops 10145128448 | bytes 27983872 | tf_op jit(solution)/shard_map/dot_general | solution.py:39
  250.7 16.8 %convolution_convert_fusion.1 = bf16[512,6448]{0,1:T(8,128)(2,1)} fusion(bf16[512,1536]{1,0:T(8,128)(2,1)S(1)} %copy-done.18, bf16[1536,6448]{1,0:T(8,128)(2,1)} %all-gather.4.cloned.1.call-done), kind=kOutput, calls=%fused_computation.21 | convolution fusion | flops 10145128448 | bytes 27983872 | tf_op jit(solution)/shard_map/dot_general | solution.py:39
  287.6 10.8 multiply_convert_fusion.3
  312.0 7.6 reshape.235
  326.1 8.0 reshape.241
  350.3 9.5 multiply_reduce_fusion.22
  359.8 8.6 copy.276
  376.9 9.8 multiply_reduce_fusion.23
  386.7 8.5 copy.270
  408.9 27.0 %multiply_reduce_fusion.17 = (f32[3072]{0:T(1024)}, f32[4,128]{1,0:T(4,128)S(1)}, f32[4,128]{1,0:T(4,128)S(1)}, f32[3072]{0:T(1024)}, f32[4,128,3072]{2,1,0:T(8,128)}) fusion(f32[4,128]{1,0:T(4,128)S(1)} %get-tuple-element.96, f32[4,128,3072]{2,1,0:T(8,128)} %copy.281, f32[512,3072]{1,0:T(8,128)} %copy.327, f32[4,128,3072]{2,1,0:T(8,128)} %bitcast.209, ...), kind=kOutput, calls=%fused_computation.64 | convolution fusion | flops 4885308416 | bytes 61386752 | tf_op jit(solution)/shard_map/dot_general | solution.py:149
  435.9 22.0 %multiply_reduce_fusion.19 = (f32[3072]{0:T(1024)}, f32[4,128,3072]{2,1,0:T(8,128)}, bf16[4,128,3072]{2,1,0:T(8,128)(2,1)}, bf16[4,128,3072]{2,1,0:T(8,128)(2,1)}, f32[3072]{0:T(1024)}, /*index=5*/f32[4,128,3072]{2,1,0:T(8,128)}) fusion(bf16[4,128,3328]{2,1,0:T(8,128)(2,1)} %get-tuple-element.67, f32[4,128]{1,0:T(4,128)S(1)} %broadcast_multiply_fusion.3, ...), kind=kLoop, calls=%fused_computation.66 | loop fusion | flops 66054144 | bytes 62959616 | tf_op jit(solution)/shard_map/reduce_sum | solution.py:159
  464.5 13.5 multiply_reduce_fusion.4
  494.7 13.6 multiply_reduce_fusion.2
  535.3 6.7 copy.300
  542.2 21.4 %multiply_reduce_fusion.15 = (f32[3328]{0:T(1024)S(1)}, f32[3328]{0:T(1024)S(1)}, f32[3328]{0:T(1024)S(1)}, f32[3328]{0:T(1024)S(1)}, f32[3328]{0:T(1024)S(1)}, /*index=5*/f32[4,128,3328]{2,1,0:T(8,128)}) fusion(f32[4,131,3328]{2,1,0:T(8,128)} %pad_convert_fusion.1, f32[4,128,3328]{2,1,0:T(8,128)} %get-tuple-element.68, f32[4,128,128]{2,1,0:T(8,128)S(1)} %copy-done.22, ...), kind=kLoop, calls=%fused_computation.35 | loop fusion | flops 32358144 | bytes 47776768 | tf_op jit(solution)/shard_map/reduce_sum | solution.py:182
  563.8 6.9 multiply_reduce_fusion.11
  571.9 22.9 %add_convert_fusion.1 = (bf16[4,128,3328]{2,1,0:T(8,128)(2,1)}, bf16[4,128,3328]{2,1,0:T(8,128)(2,1)S(1)}) fusion(f32[4,128,3328]{2,1,0:T(8,128)} %get-tuple-element.64, f32[3328]{0:T(1024)S(1)} %copy-done.33, f32[3328]{0:T(1024)S(1)} %copy-done.35, f32[3328]{0:T(1024)S(1)} %copy-done.37, f32[3328]{0:T(1024)S(1)} %copy-done.31, ...), kind=kLoop, calls=%fused_computation.39 | loop fusion | flops 27262976 | bytes 20500480 | tf_op jit(solution)/shard_map/convert.10
  597.4 17.2 %fusion = f32[4,128,1536]{2,1,0:T(8,128)} fusion(bf16[1536,6448]{1,0:T(8,128)(2,1)} %all-gather.4.cloned.1.call-done, bf16[4,128,48]{2,1,0:T(8,128)(2,1)S(1)} %copy.303, bf16[4,128,3328]{2,1,0:T(8,128)(2,1)S(1)} %get-tuple-element.86, bf16[4,128,3072]{2,1,0:T(8,128)(2,1)S(1)} %copy-done.9), kind=kOutput, calls=%fused_computation.1 | convolution fusion | flops 10161635328 | bytes 29556736 | tf_op jit(solution)/shard_map/dot_general | solution.py:198
  614.7 20.2 %multiply_reduce_fusion.25 = (f32[1536]{0:T(1024)S(1)}, f32[4,128]{1,0:T(4,128)}, f32[4,128]{1,0:T(4,128)}, f32[1536]{0:T(1024)S(1)}, f32[4,128,1536]{2,1,0:T(8,128)}) fusion(f32[4,128]{1,0:T(4,128)S(1)} %copy-done.25, bf16[2,4,128,1536]{3,2,1,0:T(8,128)(2,1)S(1)} %copy-done.2, f32[1536]{0:T(1024)S(1)} %copy-done.16, f32[4,128]{1,0:T(4,128)S(1)} %copy-done.24, ...), kind=kOutput, calls=%fused_computation.105 | convolution fusion | flops 10172641280 | bytes 35874816 | tf_op jit(solution)/shard_map/dot_general | solution.py:198
  636.9 12.8 fusion.83
  650.5 16.8 %convolution_add_fusion = f32[3072,1536]{1,0:T(8,128)} fusion(f32[3072,1536]{1,0:T(8,128)} %fusion.83, bf16[512,1536]{1,0:T(8,128)(2,1)} %bitcast.233, f32[384,8,4,128]{3,2,1,0:T(4,128)} %bitcast.215, f32[512]{0:T(512)S(1)} %copy-done.52, f32[3072]{0:T(1024)} %convert_element_type.164, bf16[512,6448]{0,1:T(8,128)(2,1)} %convolution_convert_fusion), kind=kOutput, calls=%fused_computation.19 | convolution fusion | flops 4850712576 | bytes 48773120 | tf_op jit(solution)/shard_map/dot_general | solution.py:19
  667.7 21.4 %fusion.32 = f32[1536,6448,1]{1,0,2:T(8,128)} fusion(bf16[4,128,48]{2,1,0:T(8,128)(2,1)S(1)} %copy.290, bf16[4,128,3328]{2,1,0:T(8,128)(2,1)} %get-tuple-element.85, bf16[4,128,3072]{2,1,0:T(8,128)(2,1)} %get-tuple-element.73, f32[1536]{0:T(1024)S(1)} %copy-done.16, f32[4,128]{1,0:T(4,128)S(1)} %copy-done.25, bf16[2,4,128,1536]{3,2,1,0:T(8,128)(2,1)S(1)} %copy-done.2), kind=kOutput, calls=%fused_computation.114 | convolution fusion | flops 10164781056 | bytes 47884288 | tf_op jit(solution)/shard_map/dot_general | solution.py:19
  689.0 29.6 %bitcast_add_fusion = f32[1536,6448]{1,0:T(8,128)} fusion(f32[1536,6448,1]{1,0,2:T(8,128)} %fusion.32, bf16[4,128,48]{2,1,0:T(8,128)(2,1)S(1)} %copy.303, bf16[4,128,3328]{2,1,0:T(8,128)(2,1)} %copy-done.8, bf16[4,128,3072]{2,1,0:T(8,128)(2,1)} %get-tuple-element.87, f32[4,128]{1,0:T(4,128)S(1)} %copy-done.24, f32[1536]{0:T(1024)S(1)} %copy-done.16, ...), kind=kOutput, calls=%fused_computation | convolution fusion | flops 10174685184 | bytes 87500800 | tf_op jit(solution)/shard_map/dot_general | solution.py:19
  721.0 13.8 %fusion.31 = bf16[512,1536]{1,0:T(8,128)(2,1)S(1)} fusion(f32[512,1536]{1,0:T(8,128)} %bitcast.232, bf16[3072,1536]{1,0:T(8,128)(2,1)} %all-gather.6.cloned.1.call-done, f32[384,8,4,128]{3,2,1,0:T(4,128)} %bitcast.216, f32[512]{0:T(512)S(1)} %copy-done.52, f32[3072]{0:T(1024)S(1)} %copy-done.49, bf16[512,6448]{0,1:T(8,128)(2,1)} %convolution_convert_fusion), kind=kOutput, calls=%fused_computation.113 | convolution fusion | flops 4847566848 | bytes 23607296 | tf_op jit(solution)/shard_map/dot_general | solution.py:85
  734.9 10.8 fusion.30
  756.7 18.0 %all-reduce.15.cloned.1.call-done = (f32[3328,4]{0,1:T(4,128)}, f32[3328]{0:T(1024)}, f32[48]{0:T(128)}, f32[48]{0:T(128)}, f32[48]{0:T(128)}, /*index=5*/f32[1536]{0:T(1024)}, f32[3072]{0:T(1024)}) async-done(((f32[3328,4]{0,1:T(4,128)}, f32[3328]{0:T(1024)}, f32[48]{0:T(128)}, f32[48]{0:T(128)}, f32[48]{0:T(128)}, /*index=5*/f32[1536]{0:T(1024)}, f32[3072]{0:T(1024)}), (f32[3328,4]{0,1:T(4,128)}, ...) | async-done | bytes 85584
  779.8 209.5 %reduce-scatter.6.cloned.1.call-done = f32[96,1536]{1,0:T(8,128)} async-done(((f32[3072,1536]{1,0:T(8,128)}), f32[96,1536]{1,0:T(8,128)}) %reduce-scatter.6.cloned.1.call-update) | async-done | bytes 589840 | tf_op jit(solution)/shard_map/reduce_scatter | solution.py:261
  989.3 369.7 %reduce-scatter.4.cloned.1.call-done = f32[48,6448]{1,0:T(8,128)} async-done(((f32[1536,6448]{1,0:T(8,128)}), f32[48,6448]{1,0:T(8,128)}) %reduce-scatter.4.cloned.1.call-update) | async-done | bytes 1238032 | tf_op jit(solution)/shard_map/reduce_scatter | solution.py:256
  (254 shorter events, 180.1 us)
Async XLA Ops:
  7.2 97.5 %copy-start.1 = (bf16[2,4,128,1536]{3,2,1,0:T(8,128)(2,1)S(1)}, bf16[2,4,128,1536]{3,2,1,0:T(8,128)(2,1)}, u32[]{:S(2)}) copy-start(bf16[2,4,128,1536]{3,2,1,0:T(8,128)(2,1)} %param.11) | copy-start | bytes 9437188
  7.2 99.9 %all-gather.6.cloned.1.call-start = ((), (), s32[]{:S(2)}) async-start(), calls=%async_computation.3 | async-start | bytes 9732096 | tf_op jit(solution)/shard_map/all_gather | solution.py:233
  7.9 218.6 %all-gather.4.cloned.1.call-start = ((), (), s32[]{:S(2)}) async-start(), calls=%async_computation.2 | async-start | bytes 20680704 | tf_op jit(solution)/shard_map/all_gather | solution.py:228
  8.7 766.0 %all-reduce.15.cloned.1.call-start = ((), (), s32[]{:S(2)}) async-start(), calls=%async_computation.6 | async-start | bytes 183296
  54.9 52.2 %copy-start.15 = (f32[1536]{0:T(1024)}, f32[1536]{0:T(1024)S(1)}, u32[]{:S(2)}) copy-start(f32[1536]{0:T(1024)S(1)} %convert_element_type.155) | copy-start | bytes 18436
  97.1 190.2 %copy-start.30 = (f32[3328]{0:T(1024)}, f32[3328]{0:T(1024)S(1)}, u32[]{:S(2)}) copy-start(f32[3328]{0:T(1024)S(1)} %get-tuple-element.41) | copy-start | bytes 39940
  97.1 190.2 %copy-start.32 = (f32[3328]{0:T(1024)}, f32[3328]{0:T(1024)S(1)}, u32[]{:S(2)}) copy-start(f32[3328]{0:T(1024)S(1)} %get-tuple-element.42) | copy-start | bytes 39940
  97.1 190.2 %copy-start.34 = (f32[3328]{0:T(1024)}, f32[3328]{0:T(1024)S(1)}, u32[]{:S(2)}) copy-start(f32[3328]{0:T(1024)S(1)} %get-tuple-element.43) | copy-start | bytes 39940
  97.1 190.2 %copy-start.36 = (f32[3328]{0:T(1024)}, f32[3328]{0:T(1024)S(1)}, u32[]{:S(2)}) copy-start(f32[3328]{0:T(1024)S(1)} %get-tuple-element.44) | copy-start | bytes 39940
  97.8 247.5 %copy-start.58 = (f32[48]{0:T(128)}, f32[48]{0:T(128)S(1)}, u32[]{:S(2)}) copy-start(f32[48]{0:T(128)S(1)} %exponential_negate_fusion) | copy-start | bytes 580
  107.1 119.4 %copy-start.19 = (bf16[512,1536]{1,0:T(8,128)(2,1)S(1)}, bf16[512,1536]{1,0:T(8,128)(2,1)}, u32[]{:S(2)}) copy-start(bf16[512,1536]{1,0:T(8,128)(2,1)} %get-tuple-element.78) | copy-start | bytes 4718596
  510.2 17.3 %copy-start.38 = (f32[4,48,128]{2,1,0:T(8,128)S(1)}, f32[4,48,128]{2,1,0:T(8,128)}, u32[]{:S(2)}) copy-start(f32[4,48,128]{2,1,0:T(8,128)} %get-tuple-element.23) | copy-start | bytes 294916
  510.2 17.3 %copy-start.39 = (f32[4,48,128]{2,1,0:T(8,128)S(1)}, f32[4,48,128]{2,1,0:T(8,128)}, u32[]{:S(2)}) copy-start(f32[4,48,128]{2,1,0:T(8,128)} %get-tuple-element.24) | copy-start | bytes 294916
  510.2 17.3 %copy-start.57 = (f32[48]{0:T(128)S(1)}, f32[48]{0:T(128)}, u32[]{:S(2)}) copy-start(f32[48]{0:T(128)} %param.15) | copy-start | bytes 580
  535.3 28.4 %slice-start.4 = ((s8[6815744]{0:T(1024)(128)(4,1)}), s8[2621440]{0:T(1024)(128)(4,1)S(1)}, s32[]{:S(2)}) async-start(s8[6815744]{0:T(1024)(128)(4,1)} %bitcast.205), calls=%async_computation.11 | async-start | bytes 5242880
  542.1 21.6 %slice-start = ((s8[7241728]{0:T(1024)(128)(4,1)}), s8[4194304]{0:T(1024)(128)(4,1)S(1)}, s32[]{:S(2)}) async-start(s8[7241728]{0:T(1024)(128)(4,1)} %bitcast.201), calls=%async_computation.7 | async-start | bytes 8388608
  542.1 21.6 %slice-start.1 = ((s8[7241728]{0:T(1024)(128)(4,1)}), s8[3047424]{0:T(1024)(128)(4,1)S(1)}, s32[]{:S(2)}) async-start(s8[7241728]{0:T(1024)(128)(4,1)} %bitcast.201), calls=%async_computation.8 | async-start | bytes 6094848
  542.1 21.6 %slice-start.5 = ((s8[6815744]{0:T(1024)(128)(4,1)}), s8[4194304]{0:T(1024)(128)(4,1)S(1)}, s32[]{:S(2)}) async-start(s8[6815744]{0:T(1024)(128)(4,1)} %bitcast.205), calls=%async_computation.12 | async-start | bytes 8388608
  542.1 21.6 %copy-start.7 = (f32[4,128,3072]{2,1,0:T(8,128)S(1)}, f32[4,128,3072]{2,1,0:T(8,128)}, u32[]{:S(2)}) copy-start(f32[4,128,3072]{2,1,0:T(8,128)} %copy.300) | copy-start | bytes 18874372
  542.2 21.6 %copy-start.20 = (f32[4,128,128]{2,1,0:T(8,128)S(1)}, f32[4,128,128]{2,1,0:T(8,128)}, u32[]{:S(2)}) copy-start(f32[4,128,128]{2,1,0:T(8,128)} %fusion.47) | copy-start | bytes 786436
  542.2 21.6 %copy-start.21 = (f32[4,128,128]{2,1,0:T(8,128)S(1)}, f32[4,128,128]{2,1,0:T(8,128)}, u32[]{:S(2)}) copy-start(f32[4,128,128]{2,1,0:T(8,128)} %fusion.51) | copy-start | bytes 786436
  571.9 24.5 %copy-start.60 = (f32[48]{0:T(128)S(1)}, f32[48]{0:T(128)}, u32[]{:S(2)}) copy-start(f32[48]{0:T(128)} %param.16) | copy-start | bytes 580
  571.9 25.6 %copy-start.9 = (bf16[4,128,3072]{2,1,0:T(8,128)(2,1)S(1)}, bf16[4,128,3072]{2,1,0:T(8,128)(2,1)}, u32[]{:S(2)}) copy-start(bf16[4,128,3072]{2,1,0:T(8,128)(2,1)} %get-tuple-element.87) | copy-start | bytes 9437188
  594.7 19.9 %copy-start.8 = (bf16[4,128,3328]{2,1,0:T(8,128)(2,1)}, bf16[4,128,3328]{2,1,0:T(8,128)(2,1)S(1)}, u32[]{:S(2)}) copy-start(bf16[4,128,3328]{2,1,0:T(8,128)(2,1)S(1)} %get-tuple-element.86) | copy-start | bytes 10223620
  597.4 17.3 %copy-start.2 = (bf16[2,4,128,1536]{3,2,1,0:T(8,128)(2,1)S(1)}, bf16[2,4,128,1536]{3,2,1,0:T(8,128)(2,1)}, u32[]{:S(2)}) copy-start(bf16[2,4,128,1536]{3,2,1,0:T(8,128)(2,1)} %param.11) | copy-start | bytes 9437188
  597.4 17.3 %copy-start.16 = (f32[1536]{0:T(1024)S(1)}, f32[1536]{0:T(1024)}, u32[]{:S(2)}) copy-start(f32[1536]{0:T(1024)} %copy-done.15) | copy-start | bytes 18436
  597.4 17.3 %copy-start.24 = (f32[4,128]{1,0:T(4,128)S(1)}, f32[4,128]{1,0:T(4,128)}, u32[]{:S(2)}) copy-start(f32[4,128]{1,0:T(4,128)} %get-tuple-element.92) | copy-start | bytes 6148
  597.4 17.3 %copy-start.25 = (f32[4,128]{1,0:T(4,128)S(1)}, f32[4,128]{1,0:T(4,128)}, u32[]{:S(2)}) copy-start(f32[4,128]{1,0:T(4,128)} %get-tuple-element.111) | copy-start | bytes 6148
  614.7 22.2 %copy-start.17 = (bf16[1,4,128,1536]{3,2,1,0:T(8,128)(2,1)S(1)}, bf16[1,4,128,1536]{3,2,1,0:T(8,128)(2,1)}, u32[]{:S(2)}) copy-start(bf16[1,4,128,1536]{3,2,1,0:T(8,128)(2,1)} %get-tuple-element.80) | copy-start | bytes 4718596
  614.7 22.2 %copy-start.48 = (f32[3072]{0:T(1024)S(1)}, f32[3072]{0:T(1024)}, u32[]{:S(2)}) copy-start(f32[3072]{0:T(1024)} %convert_element_type.164) | copy-start | bytes 36868
  650.5 338.8 %reduce-scatter.6.cloned.1.call-start = ((), (), s32[]{:S(2)}) async-start(), calls=%async_computation.5 | async-start | bytes 19464192 | tf_op jit(solution)/shard_map/reduce_scatter | solution.py:261
  667.4 691.6 %reduce-scatter.4.cloned.1.call-start = ((), (), s32[]{:S(2)}) async-start(), calls=%async_computation.4 | async-start | bytes 41361408 | tf_op jit(solution)/shard_map/reduce_scatter | solution.py:256
  (46 other events, 448.9 us)
Sparse Core Ops, SparseCore 0:
  10.9 84.6 all-gather.5
  98.5 127.9 all-gather.3
  650.6 124.0 all-reduce.14
  781.5 207.7 reduce-scatter.5
  996.1 362.8 reduce-scatter.3
where the time goes:
time: 1380 us; the launch traced here: 1370 us
  waiting for transfers between devices  708 us (51%)
  matrix products  280 us (20%)
  other arithmetic  150 us (11%)
  local copies, waits for them, and re-layouts  132 us (10%)
  blocking collectives  84.9 us (6%)
  between operations  15.1 us (1%)
    reduce_scatter x1, waiting for transfers between devices, local(): lax.psum_scatter(totals[0], 'fsdp', scatter_dimension=0, tiled=True)  370 us
    reduce_scatter x1, waiting for transfers between devices, local(): lax.psum_scatter(totals[5], 'fsdp', scatter_dimension=0, tiled=True)  209 us
    all_gather x1, waiting for transfers between devices, gather_weights(): lax.all_gather(in_weight, 'fsdp', axis=0, tiled=True)  109 us
    dot_general x4, matrix products, rows_product(): lax.dot_general(left, right, (((0,), (0,)), ((), ())), preferred_element_...  80.6 us
    dot_general x12, matrix products, batched(): return jnp.einsum(form, left, right, preferred_element_type=jnp.float32)  66.7 us
    unnamed x1, blocking collectives  43.6 us
    all_gather x1, blocking collectives, gather_weights(): lax.all_gather(conv_weight, 'fsdp', axis=0, tiled=True)  41.2 us
    dot_general x2, matrix products, layer_backward(): lax.dot_general(d_projected, in_weight, (((1,), (1,)), ((), ())), preferr...  37.5 us
  transfers between devices with their start and end apart: 5, of which 4 were waited for; matrix products, arithmetic and copies ran while one was open for 10% of the time, Pallas kernels for 0%

commit v1 on v0

v1 whole, which is shorter than its diff:
```python
import functools

import jax
import jax.numpy as jnp
from jax import lax
from jax.experimental import pallas as pl
from jax.experimental.pallas import tpu as pltpu
from jax.sharding import PartitionSpec as P

epsilon = 1e-05
LOG2E = 1.4426950408889634
BIG = 3.0e38
LANES = 128
FRONT = 8
f32 = jnp.float32
bf16 = jnp.bfloat16
UNROLL_F = 2
UNROLL_B = 2


def sigmoid(v):
    return 0.5 * jnp.tanh(0.5 * v) + 0.5


def sum8(v):
    rows, lanes = v.shape
    return jnp.sum(v.reshape(rows // 8, 8, lanes), axis=0)


def iotas(rows, lanes):
    return (
        lax.broadcasted_iota(jnp.int32, (rows, lanes), 0),
        lax.broadcasted_iota(jnp.int32, (rows, lanes), 1),
    )


def step_stage(dims, proj, hpar, dtp):
    T, DI, C, H = dims["T"], dims["DI"], dims["C"], dims["H"]
    dtp[...] = jnp.zeros_like(dtp)
    dtp[:, 0:H] = proj[:, DI + C : DI + C + H].astype(f32)
    v = dtp[...] + hpar[0:1, :]
    e = jnp.exp(-jnp.abs(v))
    step = jnp.maximum(v, 0.0) + jnp.log1p(e)
    row, col = iotas(T, T)
    tri = (row >= col).astype(f32)
    ld = jnp.dot(
        tri, step * (hpar[1:2, :] * LOG2E), precision=lax.Precision.HIGHEST,
        preferred_element_type=f32,
    )
    return v, e, step, ld, ld - jnp.log2(step)


def conv_tile(dims, proj, cpar, pad, c0):
    T, DI, KW = dims["T"], dims["DI"], dims["KW"]
    lanes = pl.ds(c0, LANES)
    cin = proj[:, pl.ds(DI + c0, LANES)].astype(f32)
    pad[FRONT : FRONT + T, :] = cin
    out = cpar[KW : KW + 1, lanes] + cin * cpar[KW - 1 : KW, lanes]
    for k in range(KW - 1):
        out = out + pad[FRONT - KW + 1 + k : FRONT - KW + 1 + k + T, :] * cpar[k : k + 1, lanes]
    return out


def stack_heads(dims, v):
    T, HD = dims["T"], dims["HD"]
    _, lane = iotas(T, LANES)
    zero = jnp.zeros_like(v)
    return jnp.concatenate(
        [jnp.where(lane // HD == a, v, zero) for a in range(LANES // HD)], axis=0
    )


def mix_forward(dims, proj, cpar, hpar, dpar, mixed, ssd, rstd,
                pad, gated, colb, rowb, mask, scores, acc, dtp):
    T, DI, H, HD, ST = dims["T"], dims["DI"], dims["H"], dims["HD"], dims["ST"]
    HP = LANES // HD
    tiles = DI // LANES
    pad[:, 0:FRONT, :] = jnp.zeros((pad.shape[0], FRONT, LANES), f32)
    _, _, _, ld, ld2 = step_stage(dims, proj, hpar, dtp)
    row, col = iotas(T, T)
    mask[...] = jnp.where(col <= row, BIG, -BIG)
    rowb[...] = ld2.T
    for h in range(H):
        colb[h] = jnp.broadcast_to(ld[:, h : h + 1], (T, LANES))
    bc = []
    for a in range(2):
        conv = conv_tile(dims, proj, cpar, pad.at[a], DI + a * ST)
        bc.append((conv * sigmoid(conv)).astype(bf16))
    scores[...] = lax.dot_general(
        bc[1], bc[0], (((1,), (1,)), ((), ())), preferred_element_type=f32
    )
    acc[...] = jnp.zeros_like(acc)

    def tile(j, u):
        c0 = pl.multiple_of(j * LANES, LANES)
        lanes = pl.ds(c0, LANES)
        conv = conv_tile(dims, proj, cpar, pad.at[u], c0)
        x = (conv * sigmoid(conv)).astype(bf16)
        mix = []
        for a in range(HP):
            h = j * HP + a
            expo = jnp.minimum(colb[h] - rowb[pl.ds(h, 1), :], mask[...])
            mix.append((jnp.exp2(expo) * scores[...]).astype(bf16))
        core = jnp.dot(
            jnp.concatenate(mix, axis=1), stack_heads(dims, x), preferred_element_type=f32
        )
        out = core + dpar[1:2, lanes] * x.astype(f32)
        ssd[:, lanes] = out
        gate = proj[:, lanes].astype(f32)
        g = out * (gate * sigmoid(gate))
        gated[:, lanes] = g
        return g * g

    def body(j, _):
        total = tile(j * UNROLL_F, 0)
        for u in range(1, UNROLL_F):
            total = total + tile(j * UNROLL_F + u, u)
        acc[...] += total
        return 0

    lax.fori_loop(0, tiles // UNROLL_F, body, 0)
    r = lax.rsqrt(jnp.sum(acc[...], axis=1, keepdims=True) * (1.0 / DI) + epsilon)
    rb = jnp.broadcast_to(r, (T, LANES))
    rstd[...] = rb

    def finish(j, _):
        lanes = pl.ds(pl.multiple_of(j * LANES, LANES), LANES)
        mixed[:, lanes] = (gated[:, lanes] * rb * dpar[0:1, lanes]).astype(bf16)
        return 0

    lax.fori_loop(0, tiles, finish, 0)


def mix_backward(dims, proj, dmixed, ssd, rstd, cpar, hpar, dpar, dproj, cacc, dacc, hacc,
                 pad, dpad, colb, rowb, mask, scores, acc, dtp, dscores, dlog, csum, bcs):
    T, DI, C, H, HD, ST, KW = (dims[k] for k in ("T", "DI", "C", "H", "HD", "ST", "KW"))
    HP = LANES // HD
    tiles = DI // LANES

    @pl.when(pl.program_id(0) == 0)
    def _():
        cacc[...] = jnp.zeros_like(cacc)
        dacc[...] = jnp.zeros_like(dacc)
        hacc[...] = jnp.zeros_like(hacc)

    pad[:, 0:FRONT, :] = jnp.zeros((pad.shape[0], FRONT, LANES), f32)
    dpad[:, T:, :] = jnp.zeros((dpad.shape[0], FRONT, LANES), f32)
    v, e, step, ld, ld2 = step_stage(dims, proj, hpar, dtp)
    row, col = iotas(T, T)
    mask[...] = jnp.where(row <= col, BIG, -BIG)
    rowb[...] = ld.T
    for h in range(H):
        colb[h] = jnp.broadcast_to(ld2[:, h : h + 1], (T, LANES))
    for a in range(2):
        conv = conv_tile(dims, proj, cpar, pad.at[a], DI + a * ST)
        bcs[a] = (conv * sigmoid(conv)).astype(bf16)
    scores[...] = lax.dot_general(
        bcs[0], bcs[1], (((1,), (1,)), ((), ())), preferred_element_type=f32
    )
    acc[...] = jnp.zeros_like(acc)
    dscores[...] = jnp.zeros_like(dscores)
    dlog[...] = jnp.zeros_like(dlog)
    csum[...] = jnp.zeros_like(csum)
    rb = rstd[...]

    def first(j, _):
        lanes = pl.ds(pl.multiple_of(j * LANES, LANES), LANES)
        gate = proj[:, lanes].astype(f32)
        p = dmixed[:, lanes] * (ssd[:, lanes] * (gate * sigmoid(gate)))
        acc[...] += p * dpar[0:1, lanes]
        dacc[0:8, lanes] += sum8(p * rb)
        return 0

    lax.fori_loop(0, tiles, first, 0)
    mean = jnp.sum(acc[...], axis=1, keepdims=True) * (1.0 / DI)
    mb = jnp.broadcast_to(mean, (T, LANES)) * rb * rb * rb
    acc[...] = mb

    def conv_back(c0, dact, conv, sig, u):
        lanes = pl.ds(c0, LANES)
        dconv = dact * (sig * (1.0 + conv * (1.0 - sig)))
        dpad[u, 0:T, :] = dconv
        dcin = dconv * cpar[KW - 1 : KW, lanes]
        for k in range(KW - 1):
            dcin = dcin + dpad[u, KW - 1 - k : KW - 1 - k + T, :] * cpar[k : k + 1, lanes]
        dproj[:, pl.ds(DI + c0, LANES)] = dcin.astype(bf16)
        for k in range(KW):
            start = FRONT - KW + 1 + k
            cacc[8 * k : 8 * k + 8, lanes] += sum8(dconv * pad[u, start : start + T, :])
        cacc[8 * KW : 8 * KW + 8, lanes] += sum8(dconv)

    def tile(j, u):
        c0 = pl.multiple_of(j * LANES, LANES)
        lanes = pl.ds(c0, LANES)
        conv = conv_tile(dims, proj, cpar, pad.at[u], c0)
        sig = sigmoid(conv)
        x = (conv * sig).astype(bf16)
        xf = x.astype(f32)
        gate = proj[:, lanes].astype(f32)
        gs = sigmoid(gate)
        act = gate * gs
        out = ssd[:, lanes]
        r = rstd[...]
        dgated = r * (dmixed[:, lanes] * dpar[0:1, lanes]) - (out * act) * acc[...]
        dssd = dgated * act
        dproj[:, lanes] = (dgated * out * (gs * (1.0 + gate * (1.0 - gs)))).astype(bf16)
        low = dssd.astype(bf16)
        dacc[8:16, lanes] += sum8(dssd * xf)
        lows = stack_heads(dims, low)
        dmix = lax.dot_general(
            x, lows, (((1,), (1,)), ((), ())), preferred_element_type=f32
        )
        mix = []
        part = None
        for a in range(HP):
            h = j * HP + a
            decay = jnp.exp2(jnp.minimum(rowb[pl.ds(h, 1), :] - colb[h], mask[...]))
            mix.append((decay * scores[...]).astype(bf16))
            term = dmix[:, a * T : (a + 1) * T] * decay
            part = term if part is None else part + term
        core = jnp.dot(jnp.concatenate(mix, axis=1), lows, preferred_element_type=f32)
        skip = dpar[1:2, lanes]
        from_cols = xf * core
        diff = low.astype(f32) * (out - skip * xf) - from_cols
        prow, pcol = iotas(LANES, LANES)
        place = (pcol == j * HP + prow // HD).astype(bf16)
        place = jnp.concatenate([place, place], axis=0)

        def by_head(w):
            hi = w.astype(bf16)
            lo = (w - hi.astype(f32)).astype(bf16)
            return jnp.dot(
                jnp.concatenate([hi, lo], axis=1), place, preferred_element_type=f32
            )

        conv_back(c0, core + skip * dssd, conv, sig, u)
        return part, by_head(diff), by_head(from_cols)

    def body(j, _):
        sums = tile(j * UNROLL_B, 0)
        for u in range(1, UNROLL_B):
            sums = tuple(p + q for p, q in zip(sums, tile(j * UNROLL_B + u, u)))
        dscores[...] += sums[0]
        dlog[...] += sums[1]
        csum[...] += sums[2]
        return 0

    lax.fori_loop(0, tiles // UNROLL_B, body, 0)
    ds = dscores[...].astype(bf16)
    dst = dscores[...].T.astype(bf16)
    dact = (
        jnp.dot(ds, bcs[1], preferred_element_type=f32),
        jnp.dot(dst, bcs[0], preferred_element_type=f32),
    )
    for a in range(2):
        conv = conv_tile(dims, proj, cpar, pad.at[a], DI + a * ST)
        conv_back(DI + a * ST, dact[a], conv, sigmoid(conv), a)
    dsteps = jnp.dot(
        (row <= col).astype(f32), dlog[...], precision=lax.Precision.HIGHEST,
        preferred_element_type=f32,
    )
    sg = jnp.where(v >= 0.0, 1.0, e) / (1.0 + e)
    ratio = jnp.where(step > 1e-30, sg / jnp.maximum(step, 1e-30), 1.0)
    ddt = csum[...] * ratio + dsteps * hpar[1:2, :] * sg
    dproj[:, DI + C : DI + C + H] = ddt[:, 0:H].astype(bf16)
    hacc[0:8, :] += sum8(ddt)
    hacc[8:16, :] += sum8(dsteps * step)


def run_forward(dims, proj, cpar, hpar, dpar):
    T, DI, C, H, KW = dims["T"], dims["DI"], dims["C"], dims["H"], dims["KW"]
    R, E = proj.shape
    rows = lambda w: pl.BlockSpec((T, w), lambda i: (i, 0))
    whole = lambda a: pl.BlockSpec(a.shape, lambda i: (0, 0))
    return pl.pallas_call(
        functools.partial(mix_forward, dims),
        grid=(R // T,),
        in_specs=[rows(E), whole(cpar), whole(hpar), whole(dpar)],
        out_specs=[rows(DI), rows(DI), rows(LANES)],
        out_shape=[
            jax.ShapeDtypeStruct((R, DI), bf16),
            jax.ShapeDtypeStruct((R, DI), f32),
            jax.ShapeDtypeStruct((R, LANES), f32),
        ],
        scratch_shapes=[
            pltpu.VMEM((max(2, UNROLL_F), FRONT + T, LANES), f32),
            pltpu.VMEM((T, DI), f32),
            pltpu.VMEM((H, T, LANES), f32),
            pltpu.VMEM((LANES, T), f32),
            pltpu.VMEM((T, T), f32),
            pltpu.VMEM((T, T), f32),
            pltpu.VMEM((T, LANES), f32),
            pltpu.VMEM((T, LANES), f32),
        ],
        compiler_params=pltpu.CompilerParams(vmem_limit_bytes=48 << 20),
        cost_estimate=pl.CostEstimate(
            flops=4 * R * DI * T, bytes_accessed=R * (2 * E + 6 * DI), transcendentals=R * H * T
        ),
        name="mix_forward",
    )(proj, cpar, hpar, dpar)


def run_backward(dims, proj, dmixed, ssd, rstd, cpar, hpar, dpar):
    T, DI, C, H, KW, ST = (dims[k] for k in ("T", "DI", "C", "H", "KW", "ST"))
    R, E = proj.shape
    rows = lambda w: pl.BlockSpec((T, w), lambda i: (i, 0))
    whole = lambda s: pl.BlockSpec(s, lambda i: (0, 0))
    sums = [(8 * (KW + 1), C), (16, DI), (16, LANES)]
    return pl.pallas_call(
        functools.partial(mix_backward, dims),
        grid=(R // T,),
        in_specs=[rows(E), rows(DI), rows(DI), rows(LANES)]
        + [whole(a.shape) for a in (cpar, hpar, dpar)],
        out_specs=[rows(E)] + [whole(s) for s in sums],
        out_shape=[jax.ShapeDtypeStruct((R, E), bf16)]
        + [jax.ShapeDtypeStruct(s, f32) for s in sums],
        scratch_shapes=[
            pltpu.VMEM((max(2, UNROLL_B), FRONT + T, LANES), f32),
            pltpu.VMEM((max(2, UNROLL_B), FRONT + T, LANES), f32),
            pltpu.VMEM((H, T, LANES), f32),
            pltpu.VMEM((LANES, T), f32),
            pltpu.VMEM((T, T), f32),
            pltpu.VMEM((T, T), f32),
            pltpu.VMEM((T, LANES), f32),
            pltpu.VMEM((T, LANES), f32),
            pltpu.VMEM((T, T), f32),
            pltpu.VMEM((T, LANES), f32),
            pltpu.VMEM((T, LANES), f32),
            pltpu.VMEM((2, T, ST), bf16),
        ],
        compiler_params=pltpu.CompilerParams(vmem_limit_bytes=56 << 20),
        cost_estimate=pl.CostEstimate(
            flops=8 * R * DI * T, bytes_accessed=R * (4 * E + 8 * DI), transcendentals=R * H * T
        ),
        name="mix_backward",
    )(proj, dmixed, ssd, rstd, cpar, hpar, dpar)


def local(axis, n, tokens, in_weight, conv_weight, conv_bias, dt_bias, a_log, skip_d,
          norm_scale, gate_scale, out_weight, grad_out):
    MB, S, T, D = tokens.shape
    R = MB * S * T
    E = in_weight.shape[1]
    H = a_log.shape[0]
    DI = out_weight.shape[0] * n
    C = conv_weight.shape[0] * n
    KW = conv_weight.shape[1]
    HD = DI // H
    ST = (C - DI) // 2
    dims = dict(T=T, DI=DI, C=C, H=H, HD=HD, ST=ST, KW=KW)
    assert LANES % HD == 0 and ST == LANES and DI % (LANES * 2) == 0 and T % 16 == 0

    small = jnp.concatenate(
        [conv_weight.reshape(-1), conv_bias, norm_scale, gate_scale]
    )
    smalls = lax.all_gather(small, axis, axis=0)
    c1, c2, c3 = C // n * KW, C // n * (KW + 1), C // n * (KW + 1) + D // n
    conv_w = smalls[:, :c1].reshape(C, KW).astype(f32)
    conv_b = smalls[:, c1:c2].reshape(C).astype(f32)
    norm_s = smalls[:, c2:c3].reshape(1, D).astype(f32)
    gate_s = smalls[:, c3:].reshape(DI).astype(f32)
    in_full = lax.all_gather(in_weight, axis, axis=0, tiled=True)
    out_full = lax.all_gather(out_weight, axis, axis=0, tiled=True)

    u = tokens.reshape(R, D).astype(f32)
    rstd_in = lax.rsqrt(jnp.mean(u * u, axis=-1, keepdims=True) + epsilon)
    normed = (u * rstd_in * norm_s).astype(bf16)
    proj = jnp.dot(normed, in_full, preferred_element_type=f32).astype(bf16)
    rate = -jnp.exp(a_log)
    cpar = jnp.concatenate([conv_w.T, conv_b[None], jnp.zeros((8 - KW - 1, C), f32)], axis=0)
    hpar = jnp.zeros((8, LANES), f32).at[0, :H].set(dt_bias).at[1, :H].set(rate)
    dpar = jnp.concatenate(
        [gate_s[None], jnp.repeat(skip_d, HD)[None], jnp.zeros((6, DI), f32)], axis=0
    )
    mixed, ssd, rstd = run_forward(dims, proj, cpar, hpar, dpar)
    grad_rows = grad_out.reshape(R, D)
    output = (u + jnp.dot(mixed, out_full, preferred_element_type=f32)).astype(bf16)
    d_out_w = lax.dot_general(
        mixed, grad_rows, (((0,), (0,)), ((), ())), preferred_element_type=f32
    ).astype(bf16)
    d_out_w = lax.psum_scatter(d_out_w, axis, scatter_dimension=0, tiled=True)
    d_mixed = lax.dot_general(
        grad_rows, out_full, (((1,), (1,)), ((), ())), preferred_element_type=f32
    )
    dproj, cacc, dacc, hacc = run_backward(dims, proj, d_mixed, ssd, rstd, cpar, hpar, dpar)
    d_in_w = lax.dot_general(
        normed, dproj, (((0,), (0,)), ((), ())), preferred_element_type=f32
    ).astype(bf16)
    d_in_w = lax.psum_scatter(d_in_w, axis, scatter_dimension=0, tiled=True)
    d_normed = lax.dot_general(
        dproj, in_full, (((1,), (1,)), ((), ())), preferred_element_type=f32
    )
    u_hat = u * rstd_in
    d_norm_scale = jnp.sum(d_normed * u_hat, axis=0)
    d_uhat = d_normed * norm_s
    d_tokens = grad_rows.astype(f32) + rstd_in * (
        d_uhat - u_hat * jnp.mean(d_uhat * u_hat, axis=-1, keepdims=True)
    )
    csums = cacc.reshape(KW + 1, 8, C).sum(axis=1)
    dsums = dacc.reshape(2, 8, DI).sum(axis=1)
    hsums = hacc.reshape(2, 8, LANES).sum(axis=1)
    d_skip = dsums[1].reshape(H, HD).sum(axis=1)
    heads = lax.psum(
        jnp.concatenate([hsums[0, :H], hsums[1, :H] * rate, d_skip]), axis
    )
    grads = jnp.concatenate(
        [
            csums[:KW].T.reshape(n, -1),
            csums[KW].reshape(n, -1),
            d_norm_scale.reshape(n, -1),
            dsums[0].reshape(n, -1),
        ],
        axis=1,
    )
    grads = lax.psum_scatter(grads, axis, scatter_dimension=0, tiled=True)[0]
    return (
        output.reshape(tokens.shape),
        d_tokens.reshape(tokens.shape),
        d_in_w.astype(f32),
        grads[:c1].reshape(C // n, KW),
        grads[c1:c2],
        heads[:H],
        heads[H : 2 * H],
        heads[2 * H :],
        grads[c2:c3],
        grads[c3:],
        d_out_w.astype(f32),
    )


def solution(mesh):
    axis = mesh.axis_names[0]
    n = mesh.shape[axis]
    rows, flat, batch = P(axis, None), P(axis), P(None, axis, None, None)
    return jax.shard_map(
        functools.partial(local, axis, n),
        mesh=mesh,
        in_specs=(batch, rows, rows, flat, P(), P(), P(), flat, flat, rows, batch),
        out_specs=(batch, batch, rows, rows, flat, P(), P(), P(), flat, flat, rows),
        check_vma=False,
    )
```

time: 1380 us -> 925 us (0.67)
  waiting for transfers between devices: 708 us -> 516 us
  matrix products: 280 us -> 135 us
  other arithmetic: 150 us -> 18.9 us
  Pallas kernels: 0 us -> 130 us
  local copies, waits for them, and re-layouts: 132 us -> 18.3 us
    reduce_scatter x2, waiting for transfers between devices: 579 us -> 355 us  [the longest x1 217 us: local(): d_in_w = lax.psum_scatter(d_in_w, axis, scatter_dimension=0, tiled=True)]
    dot_general x24 -> x6, matrix products: 280 us -> 135 us  [the longest x1 30 us: local(): lax.dot_general(dproj, in_full, (((1,), (1,)), ((), ())), preferred_eleme...]
    pallas_call x0 -> x2, Pallas kernels: none -> 130 us  [the longest x1 86.6 us: run_backward(): pl.pallas_call(functools.partial(mix_backward, dims), grid=(R // T,), in_...]
    reshape x10 -> x4, local copies, waits for them, and re-layouts: 64.3 us -> 2.24 us  [the longest x1 1.95 us: local(): csums[:KW].T.reshape(n, -1)]
    reduce_sum x9 -> x5, other arithmetic: 54.5 us -> 3 us  [the longest x1 1.19 us: local(): csums = cacc.reshape(KW + 1, 8, C).sum(axis=1)]
    another operation x8 -> x1, other arithmetic: 49.9 us -> 0.66 us
    all_gather x1 -> x0, blocking collectives: 41.2 us -> none  [gather_weights(): lax.all_gather(conv_weight, 'fsdp', axis=0, tiled=True)]
    psum x0 -> x1, blocking collectives: none -> 38.6 us  [local(): lax.psum(jnp.concatenate([hsums[0, :H], hsums[1, :H] * rate, d_skip]), axis)]
  transfers between devices with their start and end apart: 5 -> 5, of which waited for: 4 -> 5; matrix products, arithmetic and copies ran while one was open for 10% -> 11% of each run, Pallas kernels for 0% -> 0%
where the time goes in v1:
time: 925 us; the launch traced here: 916 us
  waiting for transfers between devices  516 us (56%)
  matrix products  135 us (15%)
  Pallas kernels  130 us (14%)
  blocking collectives  82.4 us (9%)
  other arithmetic  18.9 us (2%)
  local copies, waits for them, and re-layouts  18.3 us (2%)
  between operations  14.4 us (2%)
    reduce_scatter x1, waiting for transfers between devices, local(): d_in_w = lax.psum_scatter(d_in_w, axis, scatter_dimension=0, tiled=True)  217 us
    reduce_scatter x1, waiting for transfers between devices, local(): d_out_w = lax.psum_scatter(d_out_w, axis, scatter_dimension=0, tiled=True)  138 us
    all_gather x1, waiting for transfers between devices, local(): in_full = lax.all_gather(in_weight, axis, axis=0, tiled=True)  115 us
    pallas_call x1, Pallas kernels, run_backward(): pl.pallas_call(functools.partial(mix_backward, dims), grid=(R // T,), in_...  86.6 us
    pallas_call x1, Pallas kernels, run_forward(): pl.pallas_call(functools.partial(mix_forward, dims), grid=(R // T,), in_s...  43.8 us
    unnamed x1, blocking collectives  43.8 us
    psum x1, blocking collectives, local(): lax.psum(jnp.concatenate([hsums[0, :H], hsums[1, :H] * rate, d_skip]), axis)  38.6 us
    all_gather x1, waiting for transfers between devices, local(): out_full = lax.all_gather(out_weight, axis, axis=0, tiled=True)  31.2 us
  transfers between devices with their start and end apart: 5, of which 5 were waited for; matrix products, arithmetic and copies ran while one was open for 11% of the time, Pallas kernels for 0%

profile of v1, /device:TPU:0, one launch (start us, length us, event | category | flops | bytes accessed | tf_op | source)
XLA Modules:
  0.0 915.6 jit_solution(18187793846465952629)
XLA Ops:
  8.7 0.8 copy.33
  9.6 0.8 pad_maximum_fusion.1
  10.7 43.8 %all-reduce.1 = bf16[21248]{0:T(1024)(128)(2,1)S(1)} all-reduce(bf16[21248]{0:T(1024)(128)(2,1)S(1)} %dynamic-update-slice.4), channel_id=2, replica_groups=mesh['fsdp'=32] {'fsdp'}, use_global_device_ids=true, to_apply=%add.1 | all-reduce | flops 21248 | bytes 84992
  54.9 1.7 reshape.195
  56.6 2.0 copy.35
  61.9 2.9 fusion.4
  64.9 31.2 %all-gather.6.cloned.1.call-done = bf16[3072,1536]{1,0:T(8,128)(2,1)} async-done(((bf16[96,1536]{1,0:T(8,128)(2,1)}), bf16[3072,1536]{1,0:T(8,128)(2,1)}) %all-gather.6.cloned.1.call-update) | async-done | bytes 9437200 | tf_op jit(solution)/shard_map/all_gather | solution.py:363
  96.1 16.1 %fusion.14.dmixed = f32[1024,3072]{1,0:T(8,128)} fusion(bf16[1024,1536]{1,0:T(8,128)(2,1)} %bitcast.65, bf16[3072,1536]{1,0:T(8,128)(2,1)} %all-gather.6.cloned.1.call-done), kind=kOutput, calls=%fused_computation.45 | convolution fusion | flops 9663676416 | bytes 25165824 | tf_op jit(solution)/shard_map/dot_general | solution.py:382
  112.3 114.8 %all-gather.4.cloned.1.call-done = bf16[1536,6448]{1,0:T(8,128)(2,1)} async-done(((bf16[48,6448]{1,0:T(8,128)(2,1)}), bf16[1536,6448]{1,0:T(8,128)(2,1)}) %all-gather.4.cloned.1.call-update) | async-done | bytes 19808272 | tf_op jit(solution)/shard_map/all_gather | solution.py:362
  227.0 28.4 %convolution_convert_fusion.1.proj = bf16[1024,6448]{1,0:T(8,128)(2,1)} fusion(bf16[1024,1536]{1,0:T(8,128)(2,1)} %fusion.4, bf16[1536,6448]{1,0:T(8,128)(2,1)} %all-gather.4.cloned.1.call-done), kind=kOutput, calls=%fused_computation.1 | convolution fusion | flops 20290256896 | bytes 36159488 | tf_op jit(solution)/shard_map/dot_general | solution.py:368
  255.4 43.8 %mix_forward.1 = (bf16[1024,3072]{1,0:T(8,128)(2,1)}, f32[1024,3072]{1,0:T(8,128)}, f32[1024,128]{1,0:T(8,128)S(1)}) custom-call(bf16[1024,6448]{1,0:T(8,128)(2,1)} %convolution_convert_fusion.1.proj, f32[8,3328]{1,0:T(8,128)S(1)} %maximum_maximum_fusion.cpar, f32[8,128]{1,0:T(8,128)S(1)} %scatter.9.hpar, f32[8,3072]{1,0:T(8,128)S(1)} %maximum_maximum_fusion.1.dpar), custom_call_target="tpu_custom_call" | custom-call | flops 1610612736 | bytes 32079872 | tf_op jit(solution)/shard_map/mix_forward/pallas_call | solution.py:275
  299.2 0.8 copy-done.2
  300.0 86.6 %mix_backward.1 = (bf16[1024,6448]{1,0:T(8,128)(2,1)}, f32[40,3328]{1,0:T(8,128)}, f32[16,3072]{1,0:T(8,128)}, f32[16,128]{1,0:T(8,128)}) custom-call(bf16[1024,6448]{1,0:T(8,128)(2,1)} %convolution_convert_fusion.1.proj, f32[1024,3072]{1,0:T(8,128)} %fusion.14.dmixed, f32[1024,3072]{1,0:T(8,128)} %get-tuple-element.43.ssd, f32[1024,128]{1,0:T(8,128)} %copy-done.2, ...), custom_call_target="tpu_custom_call" | custom-call | flops 3221225472 | bytes 51576832 | tf_op jit(solution)/shard_map/mix_backward/pallas_call | solution.py:309
  386.6 1.2 bitcast_reduce_fusion
  387.8 1.0 bitcast_reduce_fusion.1
  389.0 30.0 %fusion.9 = (f32[1536]{0:T(1024)S(1)}, f32[1024]{0:T(1024)S(1)}, f32[1024,1536]{1,0:T(8,128)}) fusion(bf16[2,4,128,1536]{3,2,1,0:T(8,128)(2,1)S(1)} %copy-done.4, f32[1024]{0:T(1024)S(1)} %bitcast.69, f32[1536]{0:T(1024)S(1)} %reshape.192, bf16[1024,6448]{1,0:T(8,128)(2,1)} %get-tuple-element.45, bf16[1536,6448]{1,0:T(8,128)(2,1)} %all-gather.4.cloned.1.call-done), kind=kOutput, calls=%fused_computation.15 | convolution fusion | flops 20294660096 | bytes 42471424 | tf_op jit(solution)/shard_map/dot_general | solution.py:390
  419.1 1.7 copy.36
  420.8 1.9 reshape.186
  422.8 0.7 pad_maximum_fusion
  423.6 15.5 %convolution_convert_fusion.2 = bf16[3072,1536]{1,0:T(8,128)(2,1)} fusion(bf16[1024,3072]{1,0:T(8,128)(2,1)} %get-tuple-element.42, bf16[1024,1536]{1,0:T(8,128)(2,1)} %bitcast.66), kind=kOutput, calls=%fused_computation.2 | convolution fusion | flops 9668395008 | bytes 18874368 | tf_op jit(solution)/shard_map/dot_general | solution.py:378
  439.1 29.8 %convolution_convert_fusion = bf16[1536,6448]{1,0:T(8,128)(2,1)} fusion(bf16[1024,1536]{1,0:T(8,128)(2,1)} %fusion.4, bf16[1024,6448]{1,0:T(8,128)(2,1)} %get-tuple-element.45), kind=kOutput, calls=%fused_computation | convolution fusion | flops 20293558272 | bytes 36159488 | tf_op jit(solution)/shard_map/dot_general | solution.py:386
  469.8 38.6 %psum.7 = f32[144]{0:T(256)S(1)} all-reduce(f32[144]{0:T(256)S(1)} %pad_maximum_fusion.2), channel_id=1, replica_groups=mesh['fsdp'=32] {'fsdp'}, use_global_device_ids=true, to_apply=%region_9.0 | all-reduce | flops 144 | bytes 1152 | tf_op jit(solution)/shard_map/psum | solution.py:403
  509.0 6.3 fusion.8
  515.3 15.5 %fusion.11 = bf16[1024,1536]{1,0:T(8,128)(2,1)} fusion(bf16[2,4,128,1536]{3,2,1,0:T(8,128)(2,1)S(1)} %copy-done.4, bf16[1024,3072]{1,0:T(8,128)(2,1)} %get-tuple-element.42, bf16[3072,1536]{1,0:T(8,128)(2,1)} %all-gather.6.cloned.1.call-done), kind=kOutput, calls=%fused_computation.17 | convolution fusion | flops 9668395008 | bytes 22020096 | tf_op jit(solution)/shard_map/dot_general | solution.py:377
  530.8 13.8 %all-reduce.5.cloned.1.call-done = f32[32,664]{1,0:T(8,128)} async-done(((f32[32,664]{1,0:T(8,128)}), f32[32,664]{1,0:T(8,128)}) %all-reduce.5.cloned.1.call-update) | async-done | bytes 85008
  546.1 1.3 dynamic-slice_bitcast_fusion.2
  547.4 1.3 dynamic-slice_bitcast_fusion.1
  548.6 1.3 dynamic-slice_bitcast_fusion
  549.9 137.5 %reduce-scatter.5.cloned.1.call-done = bf16[96,1536]{1,0:T(8,128)(2,1)} async-done(((bf16[3072,1536]{1,0:T(8,128)(2,1)}), bf16[96,1536]{1,0:T(8,128)(2,1)}) %reduce-scatter.5.cloned.1.call-update) | async-done | bytes 294928 | tf_op jit(solution)/shard_map/reduce_scatter | solution.py:381
  687.5 1.8 convert_element_type.91
  689.3 217.1 %reduce-scatter.3.cloned.1.call-done = bf16[48,6448]{1,0:T(8,128)(2,1)} async-done(((bf16[1536,6448]{1,0:T(8,128)(2,1)}), bf16[48,6448]{1,0:T(8,128)(2,1)}) %reduce-scatter.3.cloned.1.call-update) | async-done | bytes 619024 | tf_op jit(solution)/shard_map/reduce_scatter | solution.py:389
  906.4 2.2 convert_element_type.89
  (64 shorter events, 9.1 us)
Async XLA Ops:
  7.2 54.0 %copy-start.4 = (bf16[2,4,128,1536]{3,2,1,0:T(8,128)(2,1)S(1)}, bf16[2,4,128,1536]{3,2,1,0:T(8,128)(2,1)}, u32[]{:S(2)}) copy-start(bf16[2,4,128,1536]{3,2,1,0:T(8,128)(2,1)} %param.15) | copy-start | bytes 9437188
  7.2 88.9 %all-gather.6.cloned.1.call-start = ((), (), s32[]{:S(2)}) async-start(), calls=%async_computation.3 | async-start | bytes 9732096 | tf_op jit(solution)/shard_map/all_gather | solution.py:363
  7.9 219.1 %all-gather.4.cloned.1.call-start = ((), (), s32[]{:S(2)}) async-start(), calls=%async_computation.2 | async-start | bytes 20680704 | tf_op jit(solution)/shard_map/all_gather | solution.py:362
  8.7 535.9 %all-reduce.5.cloned.1.call-start = ((), (), s32[]{:S(2)}) async-start(), calls=%async_computation.6 | async-start | bytes 196608
  61.2 194.2 %copy-start.3 = (f32[8,128]{1,0:T(8,128)}, f32[8,128]{1,0:T(8,128)S(1)}, u32[]{:S(2)}) copy-start(f32[8,128]{1,0:T(8,128)S(1)} %scatter.9.hpar) | copy-start | bytes 12292
  64.8 190.6 %copy-start.1 = (f32[8,3072]{1,0:T(8,128)}, f32[8,3072]{1,0:T(8,128)S(1)}, u32[]{:S(2)}) copy-start(f32[8,3072]{1,0:T(8,128)S(1)} %maximum_maximum_fusion.1.dpar) | copy-start | bytes 294916
  64.9 190.5 %copy-start = (f32[8,3328]{1,0:T(8,128)}, f32[8,3328]{1,0:T(8,128)S(1)}, u32[]{:S(2)}) copy-start(f32[8,3328]{1,0:T(8,128)S(1)} %maximum_maximum_fusion.cpar) | copy-start | bytes 319492
  299.2 0.8 copy-start.2
  423.6 263.9 %reduce-scatter.5.cloned.1.call-start = ((), (), s32[]{:S(2)}) async-start(), calls=%async_computation.5 | async-start | bytes 9732096 | tf_op jit(solution)/shard_map/reduce_scatter | solution.py:381
  439.1 467.3 %reduce-scatter.3.cloned.1.call-start = ((), (), s32[]{:S(2)}) async-start(), calls=%async_computation.4 | async-start | bytes 20680704 | tf_op jit(solution)/shard_map/reduce_scatter | solution.py:389
  469.0 0.7 copy-start.5
  469.0 0.7 copy-start.6
Sparse Core Ops, SparseCore 0:
  10.9 85.1 all-gather.5
  99.0 127.9 all-gather.3
  423.7 120.8 all-reduce.4
  550.3 137.0 reduce-scatter.4
  693.7 212.6 reduce-scatter.2

commit v2 on v1

--- a/solution.py
+++ b/solution.py
@@ -1,4 +1,5 @@
 import functools
+import math
 
 import jax
 import jax.numpy as jnp
@@ -104,7 +105,7 @@
         core = jnp.dot(
             jnp.concatenate(mix, axis=1), stack_heads(dims, x), preferred_element_type=f32
         )
-        out = core + dpar[1:2, lanes] * x.astype(f32)
+        out = core + dpar[0:1, lanes] * x.astype(f32)
         ssd[:, lanes] = out
         gate = proj[:, lanes].astype(f32)
         g = out * (gate * sigmoid(gate))
@@ -125,14 +126,14 @@
 
     def finish(j, _):
         lanes = pl.ds(pl.multiple_of(j * LANES, LANES), LANES)
-        mixed[:, lanes] = (gated[:, lanes] * rb * dpar[0:1, lanes]).astype(bf16)
+        mixed[:, lanes] = (gated[:, lanes] * rb * dpar[1:2, lanes]).astype(bf16)
         return 0
 
     lax.fori_loop(0, tiles, finish, 0)
 
 
-def mix_backward(dims, proj, dmixed, ssd, rstd, cpar, hpar, dpar, dproj, cacc, dacc, hacc,
-                 pad, dpad, colb, rowb, mask, scores, acc, dtp, dscores, dlog, csum, bcs):
+def mix_backward(dims, steps, proj, dmixed, ssd, rstd, cpar, hpar, dpar, dproj, small,
+                 cacc, dacc, hacc, pad, dpad, colb, rowb, mask, scores, acc, dtp, dscores, dlog, csum, bcs):
     T, DI, C, H, HD, ST, KW = (dims[k] for k in ("T", "DI", "C", "H", "HD", "ST", "KW"))
     HP = LANES // HD
     tiles = DI // LANES
@@ -167,8 +168,8 @@
         lanes = pl.ds(pl.multiple_of(j * LANES, LANES), LANES)
         gate = proj[:, lanes].astype(f32)
         p = dmixed[:, lanes] * (ssd[:, lanes] * (gate * sigmoid(gate)))
-        acc[...] += p * dpar[0:1, lanes]
-        dacc[0:8, lanes] += sum8(p * rb)
+        acc[...] += p * dpar[1:2, lanes]
+        dacc[8:16, lanes] += sum8(p * rb)
         return 0
 
     lax.fori_loop(0, tiles, first, 0)
@@ -201,11 +202,11 @@
         act = gate * gs
         out = ssd[:, lanes]
         r = rstd[...]
-        dgated = r * (dmixed[:, lanes] * dpar[0:1, lanes]) - (out * act) * acc[...]
+        dgated = r * (dmixed[:, lanes] * dpar[1:2, lanes]) - (out * act) * acc[...]
         dssd = dgated * act
         dproj[:, lanes] = (dgated * out * (gs * (1.0 + gate * (1.0 - gs)))).astype(bf16)
         low = dssd.astype(bf16)
-        dacc[8:16, lanes] += sum8(dssd * xf)
+        dacc[0:8, lanes] += sum8(dssd * xf)
         lows = stack_heads(dims, low)
         dmix = lax.dot_general(
             x, lows, (((1,), (1,)), ((), ())), preferred_element_type=f32
@@ -219,7 +220,7 @@
             term = dmix[:, a * T : (a + 1) * T] * decay
             part = term if part is None else part + term
         core = jnp.dot(jnp.concatenate(mix, axis=1), lows, preferred_element_type=f32)
-        skip = dpar[1:2, lanes]
+        skip = dpar[0:1, lanes]
         from_cols = xf * core
         diff = low.astype(f32) * (out - skip * xf) - from_cols
         prow, pcol = iotas(LANES, LANES)
@@ -262,9 +263,28 @@
     sg = jnp.where(v >= 0.0, 1.0, e) / (1.0 + e)
     ratio = jnp.where(step > 1e-30, sg / jnp.maximum(step, 1e-30), 1.0)
     ddt = csum[...] * ratio + dsteps * hpar[1:2, :] * sg
-    dproj[:, DI + C : DI + C + H] = ddt[:, 0:H].astype(bf16)
+    tail = dproj.shape[1] - DI - C
+    if tail > H:
+        dproj[:, DI + C :] = jnp.concatenate(
+            [ddt[:, 0:H].astype(bf16), jnp.zeros((T, tail - H), bf16)], axis=1
+        )
+    else:
+        dproj[:, DI + C :] = ddt[:, 0:H].astype(bf16)
     hacc[0:8, :] += sum8(ddt)
     hacc[8:16, :] += sum8(dsteps * step)
+
+    @pl.when(pl.program_id(0) == steps - 1)
+    def _():
+        small[...] = jnp.zeros_like(small)
+        for k in range(KW + 1):
+            small[k : k + 1, :] = jnp.sum(cacc[8 * k : 8 * k + 8, :], axis=0, keepdims=True)
+        for k in range(2):
+            small[KW + 1 + k : KW + 2 + k, 0:DI] = jnp.sum(
+                dacc[8 * k : 8 * k + 8, :], axis=0, keepdims=True
+            )
+            small[KW + 3 : KW + 4, k * LANES : (k + 1) * LANES] = jnp.sum(
+                hacc[8 * k : 8 * k + 8, :], axis=0, keepdims=True
+            )
 
 
 def run_forward(dims, proj, cpar, hpar, dpar):
@@ -300,21 +320,25 @@
     )(proj, cpar, hpar, dpar)
 
 
-def run_backward(dims, proj, dmixed, ssd, rstd, cpar, hpar, dpar):
+def run_backward(dims, EP, proj, dmixed, ssd, rstd, cpar, hpar, dpar):
     T, DI, C, H, KW, ST = (dims[k] for k in ("T", "DI", "C", "H", "KW", "ST"))
     R, E = proj.shape
     rows = lambda w: pl.BlockSpec((T, w), lambda i: (i, 0))
     whole = lambda s: pl.BlockSpec(s, lambda i: (0, 0))
+    assert KW + 4 <= 8
     sums = [(8 * (KW + 1), C), (16, DI), (16, LANES)]
     return pl.pallas_call(
-        functools.partial(mix_backward, dims),
+        functools.partial(mix_backward, dims, R // T),
         grid=(R // T,),
         in_specs=[rows(E), rows(DI), rows(DI), rows(LANES)]
         + [whole(a.shape) for a in (cpar, hpar, dpar)],
-        out_specs=[rows(E)] + [whole(s) for s in sums],
-        out_shape=[jax.ShapeDtypeStruct((R, E), bf16)]
-        + [jax.ShapeDtypeStruct(s, f32) for s in sums],
-        scratch_shapes=[
+        out_specs=[rows(EP), whole((8, C))],
+        out_shape=[
+            jax.ShapeDtypeStruct((R, EP), bf16),
+            jax.ShapeDtypeStruct((8, C), f32),
+        ],
+        scratch_shapes=[pltpu.VMEM(s, f32) for s in sums]
+        + [
             pltpu.VMEM((max(2, UNROLL_B), FRONT + T, LANES), f32),
             pltpu.VMEM((max(2, UNROLL_B), FRONT + T, LANES), f32),
             pltpu.VMEM((H, T, LANES), f32),
@@ -336,95 +360,688 @@
     )(proj, dmixed, ssd, rstd, cpar, hpar, dpar)
 
 
+MESH = pl.DeviceIdType.MESH
+CHUNK = 512
+VMEM = 67043328
+
+
+def geometry(n):
+    chips = n // 2
+    A0 = 4 if chips % 4 == 0 else 1
+    A = math.isqrt(chips // A0)
+    return (A0, A) if n % 2 == 0 and A > 1 and A0 * A * A == chips else None
+
+
+class Place:
+    def __init__(self, axis, A0, A):
+        me = lax.axis_index(axis)
+        self.A0, self.A = A0, A
+        self.c = lax.rem(me, 2)
+        chip = lax.div(me, 2)
+        self.a2 = lax.rem(chip, A)
+        self.a1 = lax.rem(lax.div(chip, A), A)
+        self.a0 = lax.div(chip, A * A)
+        c = self.c
+        self.f = self.a1 + c * (self.a2 - self.a1)
+        self.s = self.a2 + c * (self.a1 - self.a2)
+        self.sf = A + c * (1 - A)
+        self.ss = 1 + c * (A - 1)
+
+    def pos(self, f, s):
+        return f * self.sf + s * self.ss
+
+    def device(self, a0, f, s, c):
+        return ((a0 * self.A * self.A + self.pos(f, s)) * 2 + c,)
+
+    def line(self, q):
+        return lax.rem(self.a0 + q + self.A0, self.A0)
+
+    def first(self, q):
+        return lax.rem(self.f + q + self.A, self.A)
+
+    def second(self, q):
+        return lax.rem(self.s + q + self.A, self.A)
+
+    def partner(self):
+        return self.device(self.a0, self.f, self.s, 1 - self.c)
+
+    def peers(self):
+        out = [self.partner()]
+        out += [self.device(self.line(q), self.f, self.s, self.c) for q in range(1, self.A0)]
+        out += [self.device(self.a0, self.first(q), self.s, self.c) for q in range(1, self.A)]
+        out += [self.device(self.a0, self.f, self.second(q), self.c) for q in range(1, self.A)]
+        return out
+
+    def barrier(self):
+        sem = pltpu.get_barrier_semaphore()
+        peers = self.peers()
+        for peer in peers:
+            pl.semaphore_signal(sem, inc=1, device_id=peer, device_id_type=MESH)
+        pl.semaphore_wait(sem, len(peers))
+
+
+def send(src, dst, ssem, rsem, device):
+    return pltpu.make_async_remote_copy(
+        src_ref=src, dst_ref=dst, send_sem=ssem, recv_sem=rsem,
+        device_id=device, device_id_type=MESH,
+    )
+
+
+class Gather:
+    def __init__(self, at, K, wl, buf, ssem, rsem, lsem):
+        self.at, self.K, self.wl, self.buf = at, K, wl, buf
+        self.ssem, self.rsem, self.lsem = ssem, rsem, lsem
+
+    @staticmethod
+    def sems(A0, A):
+        return (A0 - 1) + (A - 1) + (A - 1) * A + 1
+
+    def local(self, j):
+        at = self.at
+        return pltpu.make_async_copy(
+            self.wl.at[j], self.buf.at[j, at.a0, at.pos(at.f, at.s), at.c],
+            self.lsem.at[lax.rem(j, 2)],
+        )
+
+    def copies(self, stage, j, sending):
+        at, buf = self.at, self.buf
+        A0, A = at.A0, at.A
+        par = lax.rem(j, 2)
+        out = []
+
+        def add(k, src, dst, device):
+            out.append(send(src, dst, self.ssem.at[par, k], self.rsem.at[j, k], device))
+
+        if stage == 0:
+            for q in range(1, A0):
+                a = at.a0 if sending else at.line(-q)
+                add(q - 1, self.wl.at[j], buf.at[j, a, at.pos(at.f, at.s), at.c],
+                    at.device(at.line(q), at.f, at.s, at.c))
+        elif stage == 1:
+            for q in range(1, A):
+                f = at.f if sending else at.first(-q)
+                ref = buf.at[j, :, at.pos(f, at.s), at.c]
+                add(A0 - 1 + q - 1, ref, ref, at.device(at.a0, at.first(q), at.s, at.c))
+        elif stage == 2:
+            for q in range(1, A):
+                s = at.s if sending else at.second(-q)
+                for o in range(A):
+                    ref = buf.at[j, :, at.pos(o, s), at.c]
+                    add(A0 - 1 + A - 1 + (q - 1) * A + o, ref, ref,
+                        at.device(at.a0, at.f, at.second(q), at.c))
+        else:
+            ref = buf.at[j, :, :, at.c if sending else 1 - at.c]
+            add(A0 - 1 + (A - 1) * (A + 1), ref, ref, at.partner())
+        return out
+
+    def step(self, i):
+        for stage in range(5):
+            j = i - stage
+
+            @pl.when((j >= 0) & (j < self.K))
+            def _(stage=stage, j=j):
+                if stage > 0:
+                    for cp in self.copies(stage - 1, j, False):
+                        cp.wait_recv()
+                if stage < 4:
+
+                    @pl.when(j >= 2)
+                    def _():
+                        for cp in self.copies(stage, j - 2, True):
+                            cp.wait_send()
+
+                    if stage == 1:
+                        self.local(j).wait()
+                    for cp in self.copies(stage, j, True):
+                        cp.start()
+                    if stage == 0:
+                        self.local(j).start()
+
+    def drain(self):
+        for j in range(max(0, self.K - 2), self.K):
+            for stage in range(4):
+                for cp in self.copies(stage, jnp.int32(j), True):
+                    cp.wait_send()
+
+
+class Reduce:
+    def __init__(self, at, K, refs):
+        self.at, self.K = at, K
+        (self.own0, self.own1, self.own2, self.own3, self.s0, self.s1, self.s2, self.s3,
+         self.r0, self.r1, self.r2, self.r3, self.ssem, self.rsem) = refs
+
+    @staticmethod
+    def sems(A0, A):
+        return 1 + (A - 1) + (A - 1) + (A0 - 1)
+
+    @staticmethod
+    def scratch(K, A0, A, r, w):
+        N = A0 * A * A
+        NS = Reduce.sems(A0, A)
+        return [
+            pltpu.VMEM((2, N, r, w), f32),
+            pltpu.VMEM((2, A0 * A, r, w), f32),
+            pltpu.VMEM((2, A0, r, w), f32),
+            pltpu.VMEM((2, r, w), f32),
+            pltpu.VMEM((2, N, r, w), bf16),
+            pltpu.VMEM((2, A - 1, A0 * A, r, w), bf16),
+            pltpu.VMEM((2, A - 1, A0, r, w), bf16),
+            pltpu.VMEM((2, A0 - 1, r, w), bf16),
+            pltpu.VMEM((K, N, r, w), bf16),
+            pltpu.VMEM((K, A - 1, A0 * A, r, w), bf16),
+            pltpu.VMEM((K, A - 1, A0, r, w), bf16),
+            pltpu.VMEM((K, A0 - 1, r, w), bf16),
+            pltpu.SemaphoreType.DMA((2, NS)),
+            pltpu.SemaphoreType.DMA((K, NS)),
+        ]
+
+    def copies(self, stage, j):
+        at = self.at
+        A0, A = at.A0, at.A
+        par = lax.rem(j, 2)
+
+        def make(k, src, dst, device):
+            return send(src, dst, self.ssem.at[par, k], self.rsem.at[j, k], device)
+
+        if stage == 0:
+            return [make(0, self.s0.at[par], self.r0.at[j], at.partner())]
+        if stage == 1:
+            return [
+                make(q, self.s1.at[par, q - 1], self.r1.at[j, q - 1],
+                     at.device(at.a0, at.f, at.second(q), at.c))
+                for q in range(1, A)
+            ]
+        if stage == 2:
+            return [
+                make(A - 1 + q, self.s2.at[par, q - 1], self.r2.at[j, q - 1],
+                     at.device(at.a0, at.first(q), at.s, at.c))
+                for q in range(1, A)
+            ]
+        return [
+            make(2 * (A - 1) + q, self.s3.at[par, q - 1], self.r3.at[j, q - 1],
+                 at.device(at.line(q), at.f, at.s, at.c))
+            for q in range(1, A0)
+        ]
+
+    def free(self, stage, j):
+        @pl.when(j >= 2)
+        def _():
+            for cp in self.copies(stage, j - 2):
+                cp.wait_send()
+
+    def start(self, stage, j):
+        for cp in self.copies(stage, j):
+            cp.start()
+
+    def arrive(self, stage, j):
+        for cp in self.copies(stage, j):
+            cp.wait_recv()
+
+    def step(self, i, finish):
+        at = self.at
+        A0, A = at.A0, at.A
+
+        def stage1(j):
+            par = lax.rem(j, 2)
+            self.arrive(0, j)
+            self.free(1, j)
+
+            def line(a, _):
+                for o in range(A):
+                    for q in range(A):
+                        b = a * A * A + at.pos(o, at.second(q))
+                        v = self.own0[par, b] + self.r0[j, b].astype(f32)
+                        if q == 0:
+                            self.own1[par, a * A + o] = v
+                        else:
+                            self.s1[par, q - 1, a * A + o] = v.astype(bf16)
+                return 0
+
+            lax.fori_loop(0, A0, line, 0)
+            self.start(1, j)
+
+        def stage2(j):
+            par = lax.rem(j, 2)
+            self.arrive(1, j)
+            self.free(2, j)
+
+            def line(a, _):
+                for q in range(A):
+                    b = a * A + at.first(q)
+                    v = self.own1[par, b]
+                    for p in range(A - 1):
+                        v = v + self.r1[j, p, b].astype(f32)
+                    if q == 0:
+                        self.own2[par, a] = v
+                    else:
+                        self.s2[par, q - 1, a] = v.astype(bf16)
+                return 0
+
+            lax.fori_loop(0, A0, line, 0)
+            self.start(2, j)
+
+        def stage3(j):
+            par = lax.rem(j, 2)
+            self.arrive(2, j)
+            self.free(3, j)
+            for q in range(A0):
+                a = at.line(q)
+                v = self.own2[par, a]
+                for p in range(A - 1):
+                    v = v + self.r2[j, p, a].astype(f32)
+                if q == 0:
+                    self.own3[par] = v
+                else:
+                    self.s3[par, q - 1] = v.astype(bf16)
+            self.start(3, j)
+
+        def stage4(j):
+            self.arrive(3, j)
+            v = self.own3[lax.rem(j, 2)]
+            for p in range(A0 - 1):
+                v = v + self.r3[j, p].astype(f32)
+            finish(j, v)
+
+        for k, stage in ((1, stage1), (2, stage2), (3, stage3), (4, stage4)):
+            j = i - k
+
+            @pl.when((j >= 0) & (j < self.K))
+            def _(j=j, stage=stage):
+                stage(j)
+
+    def drain(self):
+        for j in range(max(0, self.K - 2), self.K):
+            for stage in range(4):
+                for cp in self.copies(stage, jnp.int32(j)):
+                    cp.wait_send()
+
+
+class SumAll:
+    def __init__(self, at, refs):
+        self.at = at
+        self.hold, self.land, self.ssem, self.rsem = refs
+
+    @staticmethod
+    def scratch(A0, A, shape):
+        slots = 2 + A + A + A0
+        return [
+            pltpu.VMEM((4,) + shape, f32),
+            pltpu.VMEM((slots,) + shape, f32),
+            pltpu.SemaphoreType.DMA((slots,)),
+            pltpu.SemaphoreType.DMA((slots,)),
+        ]
+
+    def group(self, stage):
+        at = self.at
+        A0, A = at.A0, at.A
+        chip = at.a0 * A * A + at.a1 * A + at.a2
+        if stage == 0:
+            return 0, 2, at.c, 1, chip * 2
+        if stage == 1:
+            return 2, A, at.a2, 2, (chip - at.a2) * 2 + at.c
+        if stage == 2:
+            return 2 + A, A, at.a1, 2 * A, (chip - at.a1 * A) * 2 + at.c
+        return 2 + 2 * A, A0, at.a0, 2 * A * A, (chip - at.a0 * A * A) * 2 + at.c
+
+    def copies(self, stage, sending):
+        base, size, mine, stride, origin = self.group(stage)
+        out = []
+        for q in range(1, size):
+            to = lax.rem(mine + q, size)
+            slot = mine if sending else lax.rem(mine - q + size, size)
+            out.append(
+                send(self.hold.at[stage], self.land.at[base + slot], self.ssem.at[base + q],
+                     self.rsem.at[base + q], (origin + to * stride,))
+            )
+        return out
+
+    def start(self, stage, value):
+        base, _, mine, _, _ = self.group(stage)
+        self.hold[stage] = value
+        self.land[base + mine] = value
+        for cp in self.copies(stage, True):
+            cp.start()
+
+    def finish(self, stage):
+        base, size, _, _, _ = self.group(stage)
+        for cp in self.copies(stage, False):
+            cp.wait_recv()
+        for cp in self.copies(stage, True):
+            cp.wait_send()
+        total = self.land[base]
+        for k in range(1, size):
+            total = total + self.land[base + k]
+        return total
+
+
+def gather_project(axis, geom, K, tok, wl, proj, wfull, uT, scale, buf, uh, ssem, rsem, lsem):
+    A0, A = geom
+    at = Place(axis, A0, A)
+    i = pl.program_id(0)
+    R, D = tok.shape
+    w = wl.shape[2]
+
+    @pl.when(i == 0)
+    def _():
+        at.barrier()
+
+    net = Gather(at, K, wl, buf, ssem, rsem, lsem)
+    net.step(i)
+
+    @pl.when(i == 4)
+    def _():
+        last = buf[0].reshape(D, w)[:, w - LANES :].astype(f32).T
+        scale[...] = jnp.broadcast_to(last[LANES - 1 :, :], scale.shape)
+
+        def norm(k, _):
+            rows = pl.ds(pl.multiple_of(k * LANES, LANES), LANES)
+            u = tok[rows, :].astype(f32)
+            r = lax.rsqrt(jnp.mean(u * u, axis=-1, keepdims=True) + epsilon)
+            v = u * r * scale[0:1, :]
+            uh[rows, :] = v.astype(bf16)
+            uT[:, rows] = v.T.astype(bf16)
+            return 0
+
+        lax.fori_loop(0, R // LANES, norm, 0)
+
+    @pl.when(i >= 4)
+    def _():
+        wfull[...] = buf[i - 4].reshape(D, w)
+        M = 256
+
+        def rows(k, _):
+            at_ = pl.ds(pl.multiple_of(k * M, M), M)
+            proj[at_, :] = jnp.dot(
+                uh[at_, :], wfull[...], preferred_element_type=f32
+            ).astype(bf16)
+            return 0
+
+        lax.fori_loop(0, R // M, rows, 0)
+
+    @pl.when(i == K + 3)
+    def _():
+        net.drain()
+
+
+def run_gather(axis, geom, tok, wl, E):
+    A0, A = geom
+    R, D = tok.shape
+    K, r, w = wl.shape
+    NS = Gather.sems(A0, A)
+    late = lambda i: (0, lax.rem(jnp.maximum(i - 4, 0) + K - 1, K))
+    once = dict(pipeline_mode=pl.Buffered(1))
+    return pl.pallas_call(
+        functools.partial(gather_project, axis, geom, K),
+        grid=(K + 4,),
+        in_specs=[
+            pl.BlockSpec((R, D), lambda i: (0, 0), **once),
+            pl.BlockSpec((K, r, w), lambda i: (0, 0, 0), **once),
+        ],
+        out_specs=[
+            pl.BlockSpec((R, w), late),
+            pl.BlockSpec((D, w), late),
+            pl.BlockSpec((D, R), lambda i: (0, 0), **once),
+            pl.BlockSpec((8, D), lambda i: (0, 0), **once),
+        ],
+        out_shape=[
+            jax.ShapeDtypeStruct((R, E), bf16),
+            jax.ShapeDtypeStruct((D, K * w), bf16),
+            jax.ShapeDtypeStruct((D, R), bf16),
+            jax.ShapeDtypeStruct((8, D), f32),
+        ],
+        scratch_shapes=[
+            pltpu.VMEM((K, A0, A * A, 2, r, w), bf16),
+            pltpu.VMEM((R, D), bf16),
+            pltpu.SemaphoreType.DMA((2, NS)),
+            pltpu.SemaphoreType.DMA((K, NS)),
+            pltpu.SemaphoreType.DMA((2,)),
+        ],
+        compiler_params=pltpu.CompilerParams(
+            collective_id=1, has_side_effects=True, vmem_limit_bytes=VMEM
+        ),
+        cost_estimate=pl.CostEstimate(
+            flops=2 * R * D * E, bytes_accessed=2 * D * E * 40, transcendentals=0
+        ),
+        name="gather_project",
+    )(tok, wl)
+
+
+def reduce_in(axis, geom, K, E, uT, dproj, wfull, wl, scale, tok, go, small,
+              dw, dns, dtok, sums, own, *refs):
+    A0, A = geom
+    at = Place(axis, A0, A)
+    i = pl.program_id(0)
+    R, D = tok.shape
+    N, _, r, _ = uT.shape
+    w = dproj.shape[1]
+    net = Reduce(at, K, refs[:14])
+    total = SumAll(at, refs[14:18])
+
+    @pl.when(i == 0)
+    def _():
+        at.barrier()
+        total.start(0, small[...])
+        own[0] = uT[:, at.c].reshape(N * r, R)
+        own[1] = uT[:, 1 - at.c].reshape(N * r, R)
+        dns[...] = jnp.zeros_like(dns)
+
+    for stage in range(1, 4):
+
+        @pl.when(i == stage)
+        def _(stage=stage):
+            total.start(stage, total.finish(stage - 1))
+
+    @pl.when(i == 4)
+    def _():
+        sums[...] = total.finish(3)
+
+    @pl.when(i < K)
+    def _():
+        par = lax.rem(i, 2)
+        net.free(0, i)
+        d = dproj[...]
+        net.s0[par] = (
+            jnp.dot(own[1], d, preferred_element_type=f32).astype(bf16).reshape(N, r, w)
+        )
+        net.start(0, i)
+        net.own0[par] = jnp.dot(own[0], d, preferred_element_type=f32).reshape(N, r, w)
+        M = 256
+
+        def rows(k, _):
+            at_ = pl.ds(pl.multiple_of(k * M, M), M)
+            part = lax.dot_general(
+                dproj[at_, :], wfull[...], (((1,), (1,)), ((), ())), preferred_element_type=f32
+            )
+
+            @pl.when(i == 0)
+            def _():
+                dtok[at_, :] = part
+
+            @pl.when(i > 0)
+            def _():
+                dtok[at_, :] += part
+
+            return 0
+
+        lax.fori_loop(0, R // M, rows, 0)
+
+    def finish(j, v):
+        dw[...] = v
+        _, col = iotas(r, w)
+        p = jnp.where(col < E - j * w, v * wl[:, pl.ds(0, w)].astype(f32), 0.0)
+        part = p[:, 0:LANES]
+        for k in range(1, w // LANES):
+            part = part + p[:, k * LANES : (k + 1) * LANES]
+        dns[...] += part
+
+    net.step(i, finish)
+
+    @pl.when((i >= K) & (i < K + 4))
+    def _():
+        M = R // 4
+
+        def tail(k, _):
+            at_ = pl.ds(pl.multiple_of((i - K) * M + k * 64, 64), 64)
+            u = tok[at_, :].astype(f32)
+            rs = lax.rsqrt(jnp.mean(u * u, axis=-1, keepdims=True) + epsilon)
+            u = u * rs
+            d = dtok[at_, :] * scale[0:1, :]
+            m = jnp.mean(d * u, axis=-1, keepdims=True)
+            dtok[at_, :] = go[at_, :].astype(f32) + rs * (d - u * m)
+            return 0
+
+        lax.fori_loop(0, M // 64, tail, 0)
+
+    @pl.when(i == K + 3)
+    def _():
+        net.drain()
+
+
+def run_reduce_in(axis, geom, uT, dproj, wfull, wl, scale, tok, go, small):
+    A0, A = geom
+    R, D = tok.shape
+    r, E = wl.shape
+    w = CHUNK
+    K = dproj.shape[1] // w
+    N = A0 * A * A
+    once = dict(pipeline_mode=pl.Buffered(1))
+    late = lambda i: (0, jnp.clip(i - 4, 0, K - 1))
+    early = lambda i: (0, jnp.minimum(i, K - 1))
+    whole = lambda i: (0, 0)
+    return pl.pallas_call(
+        functools.partial(reduce_in, axis, geom, K, E),
+        grid=(K + 4,),
+        in_specs=[
+            pl.BlockSpec((N, 2, r, R), lambda i: (0, 0, 0, 0), **once),
+            pl.BlockSpec((R, w), early),
+            pl.BlockSpec((D, w), early),
+            pl.BlockSpec((r, w), late),
+            pl.BlockSpec((8, D), whole, **once),
+            pl.BlockSpec((R, D), whole, **once),
+            pl.BlockSpec((R, D), whole, **once),
+            pl.BlockSpec(small.shape, whole, **once),
+        ],
+        out_specs=[
+            pl.BlockSpec((r, w), late),
+            pl.BlockSpec((r, LANES), whole, **once),
+            pl.BlockSpec((R, D), whole, **once),
+            pl.BlockSpec(small.shape, whole, **once),
+        ],
+        out_shape=[
+            jax.ShapeDtypeStruct((r, E), f32),
+            jax.ShapeDtypeStruct((r, LANES), f32),
+            jax.ShapeDtypeStruct((R, D), f32),
+            jax.ShapeDtypeStruct(small.shape, f32),
+        ],
+        scratch_shapes=[pltpu.VMEM((2, N * r, R), bf16)]
+        + Reduce.scratch(K, A0, A, r, w)
+        + SumAll.scratch(A0, A, small.shape),
+        compiler_params=pltpu.CompilerParams(
+            collective_id=2, has_side_effects=True, vmem_limit_bytes=VMEM
+        ),
+        cost_estimate=pl.CostEstimate(
+            flops=4 * R * D * E, bytes_accessed=2 * D * E * 40, transcendentals=0
+        ),
+        name="reduce_in",
+    )(uT.reshape(N, 2, r, R), dproj, wfull, wl, scale, tok, go, small)
+
+
 def local(axis, n, tokens, in_weight, conv_weight, conv_bias, dt_bias, a_log, skip_d,
           norm_scale, gate_scale, out_weight, grad_out):
     MB, S, T, D = tokens.shape
     R = MB * S * T
-    E = in_weight.shape[1]
+    r, E = in_weight.shape
     H = a_log.shape[0]
     DI = out_weight.shape[0] * n
-    C = conv_weight.shape[0] * n
-    KW = conv_weight.shape[1]
+    Cn, KW = conv_weight.shape
+    C = Cn * n
     HD = DI // H
     ST = (C - DI) // 2
     dims = dict(T=T, DI=DI, C=C, H=H, HD=HD, ST=ST, KW=KW)
     assert LANES % HD == 0 and ST == LANES and DI % (LANES * 2) == 0 and T % 16 == 0
-
-    small = jnp.concatenate(
-        [conv_weight.reshape(-1), conv_bias, norm_scale, gate_scale]
-    )
-    smalls = lax.all_gather(small, axis, axis=0)
-    c1, c2, c3 = C // n * KW, C // n * (KW + 1), C // n * (KW + 1) + D // n
-    conv_w = smalls[:, :c1].reshape(C, KW).astype(f32)
-    conv_b = smalls[:, c1:c2].reshape(C).astype(f32)
-    norm_s = smalls[:, c2:c3].reshape(1, D).astype(f32)
-    gate_s = smalls[:, c3:].reshape(DI).astype(f32)
-    in_full = lax.all_gather(in_weight, axis, axis=0, tiled=True)
+    geom = geometry(n)
+    w = CHUNK
+    K = -(-E // w)
+    EP = K * w
+    Gn = DI // n
+    own = (
+        geom is not None and r % 16 == 0 and EP - LANES >= E and max(Cn, Gn) < LANES
+        and KW + 2 <= r
+    )
+    me = lax.axis_index(axis)
+
+    ns = norm_scale.astype(f32)
+    tok = tokens.reshape(R, D)
+    go = grad_out.reshape(R, D)
     out_full = lax.all_gather(out_weight, axis, axis=0, tiled=True)
-
-    u = tokens.reshape(R, D).astype(f32)
-    rstd_in = lax.rsqrt(jnp.mean(u * u, axis=-1, keepdims=True) + epsilon)
-    normed = (u * rstd_in * norm_s).astype(bf16)
-    proj = jnp.dot(normed, in_full, preferred_element_type=f32).astype(bf16)
+    if own:
+        rows = [conv_weight.T, conv_bias[None], gate_scale[None]]
+        pads = jnp.concatenate(
+            [jnp.pad(v, ((0, 0), (0, LANES - 1 - v.shape[1]))) for v in rows]
+            + [jnp.zeros((r - KW - 2, LANES - 1), bf16)],
+            axis=0,
+        )
+        wl = jnp.concatenate(
+            [in_weight, jnp.zeros((r, EP - LANES - E), bf16), pads, norm_scale[:, None]], axis=1
+        )
+        wl = jnp.roll(wl.reshape(r, K, w).transpose(1, 0, 2), 1, axis=0)
+        proj, wfull, uT, scale = run_gather(axis, geom, tok, wl, E)
+        got = wfull.reshape(n, r, EP)[:, : KW + 2, EP - LANES :]
+        conv, gate = got[:, : KW + 1, :Cn], got[:, KW + 1, :Gn]
+    else:
+        EP = E
+        wfull = lax.all_gather(in_weight, axis, axis=0, tiled=True)
+        conv = lax.all_gather(jnp.concatenate([conv_weight.T, conv_bias[None]]), axis, axis=0)
+        gate = lax.all_gather(gate_scale, axis, axis=0)
+        scale = lax.all_gather(norm_scale, axis, axis=0).reshape(1, D).astype(f32)
+        u = tok.astype(f32)
+        rs = lax.rsqrt(jnp.mean(u * u, axis=-1, keepdims=True) + epsilon)
+        uh = (u * rs * scale).astype(bf16)
+        proj = jnp.dot(uh, wfull, preferred_element_type=f32).astype(bf16)
+    conv = conv.transpose(1, 0, 2).reshape(KW + 1, C).astype(f32)
+
     rate = -jnp.exp(a_log)
-    cpar = jnp.concatenate([conv_w.T, conv_b[None], jnp.zeros((8 - KW - 1, C), f32)], axis=0)
+    cpar = jnp.concatenate([conv, jnp.zeros((8 - KW - 1, C), f32)], axis=0)
     hpar = jnp.zeros((8, LANES), f32).at[0, :H].set(dt_bias).at[1, :H].set(rate)
     dpar = jnp.concatenate(
-        [gate_s[None], jnp.repeat(skip_d, HD)[None], jnp.zeros((6, DI), f32)], axis=0
+        [jnp.repeat(skip_d, HD)[None], gate.reshape(1, DI).astype(f32), jnp.zeros((6, DI), f32)]
     )
     mixed, ssd, rstd = run_forward(dims, proj, cpar, hpar, dpar)
-    grad_rows = grad_out.reshape(R, D)
-    output = (u + jnp.dot(mixed, out_full, preferred_element_type=f32)).astype(bf16)
-    d_out_w = lax.dot_general(
-        mixed, grad_rows, (((0,), (0,)), ((), ())), preferred_element_type=f32
+    output = (tok.astype(f32) + jnp.dot(mixed, out_full, preferred_element_type=f32)).astype(bf16)
+    g_out = lax.dot_general(
+        mixed, go, (((0,), (0,)), ((), ())), preferred_element_type=f32
     ).astype(bf16)
-    d_out_w = lax.psum_scatter(d_out_w, axis, scatter_dimension=0, tiled=True)
-    d_mixed = lax.dot_general(
-        grad_rows, out_full, (((1,), (1,)), ((), ())), preferred_element_type=f32
-    )
-    dproj, cacc, dacc, hacc = run_backward(dims, proj, d_mixed, ssd, rstd, cpar, hpar, dpar)
-    d_in_w = lax.dot_general(
-        normed, dproj, (((0,), (0,)), ((), ())), preferred_element_type=f32
-    ).astype(bf16)
-    d_in_w = lax.psum_scatter(d_in_w, axis, scatter_dimension=0, tiled=True)
-    d_normed = lax.dot_general(
-        dproj, in_full, (((1,), (1,)), ((), ())), preferred_element_type=f32
-    )
-    u_hat = u * rstd_in
-    d_norm_scale = jnp.sum(d_normed * u_hat, axis=0)
-    d_uhat = d_normed * norm_s
-    d_tokens = grad_rows.astype(f32) + rstd_in * (
-        d_uhat - u_hat * jnp.mean(d_uhat * u_hat, axis=-1, keepdims=True)
-    )
-    csums = cacc.reshape(KW + 1, 8, C).sum(axis=1)
-    dsums = dacc.reshape(2, 8, DI).sum(axis=1)
-    hsums = hacc.reshape(2, 8, LANES).sum(axis=1)
-    d_skip = dsums[1].reshape(H, HD).sum(axis=1)
-    heads = lax.psum(
-        jnp.concatenate([hsums[0, :H], hsums[1, :H] * rate, d_skip]), axis
-    )
-    grads = jnp.concatenate(
-        [
-            csums[:KW].T.reshape(n, -1),
-            csums[KW].reshape(n, -1),
-            d_norm_scale.reshape(n, -1),
-            dsums[0].reshape(n, -1),
-        ],
-        axis=1,
-    )
-    grads = lax.psum_scatter(grads, axis, scatter_dimension=0, tiled=True)[0]
+    g_out = lax.psum_scatter(g_out, axis, scatter_dimension=0, tiled=True)
+    d_mixed = lax.dot_general(go, out_full, (((1,), (1,)), ((), ())), preferred_element_type=f32)
+    dproj, small = run_backward(dims, EP, proj, d_mixed, ssd, rstd, cpar, hpar, dpar)
+    if own:
+        dw, dns, dtok, sums = run_reduce_in(
+            axis, geom, uT, dproj, wfull, in_weight, scale, tok, go, small
+        )
+    else:
+        g_in = lax.dot_general(
+            uh, dproj, (((0,), (0,)), ((), ())), preferred_element_type=f32
+        ).astype(bf16)
+        dw = lax.psum_scatter(g_in, axis, scatter_dimension=0, tiled=True).astype(f32)
+        dns = dw * in_weight.astype(f32)
+        d = lax.dot_general(dproj, wfull, (((1,), (1,)), ((), ())), preferred_element_type=f32)
+        u, d = u * rs, d * scale
+        dtok = go.astype(f32) + rs * (d - u * jnp.mean(d * u, axis=-1, keepdims=True))
+        sums = lax.psum(small, axis)
+    dconv = lax.dynamic_slice(sums, (0, me * Cn), (KW + 1, Cn))
+    heads = sums[KW + 3]
     return (
         output.reshape(tokens.shape),
-        d_tokens.reshape(tokens.shape),
-        d_in_w.astype(f32),
-        grads[:c1].reshape(C // n, KW),
-        grads[c1:c2],
+        dtok.reshape(tokens.shape),
+        dw,
+        dconv[:KW].T,
+        dconv[KW],
         heads[:H],
-        heads[H : 2 * H],
-        heads[2 * H :],
-        grads[c2:c3],
-        grads[c3:],
-        d_out_w.astype(f32),
+        heads[LANES : LANES + H] * rate,
+        sums[KW + 1, :DI].reshape(H, HD).sum(axis=1),
+        dns.sum(axis=1) / ns,
+        lax.dynamic_slice(sums[KW + 2], (me * Gn,), (Gn,)),
+        g_out.astype(f32),
     )
 
 

time: 925 us -> 673 us (0.73)
  waiting for transfers between devices: 516 us -> 218 us
  Pallas kernels: 130 us -> 370 us
  matrix products: 135 us -> 46.1 us
  blocking collectives: 82.4 us -> 0 us
  other arithmetic: 18.9 us -> 6.99 us
    pallas_call x1 -> x3, Pallas kernels: 86.6 us -> 327 us  [the longest x1 127 us: run_reduce_in(): pl.pallas_call(functools.partial(reduce_in, axis, geom, K, E), grid=(K +...]
    reduce_scatter x2 -> x1, waiting for transfers between devices: 355 us -> 136 us  [local(): g_out = lax.psum_scatter(g_out, axis, scatter_dimension=0, tiled=True)]
    all_gather x1 -> x0, waiting for transfers between devices: 115 us -> none  [local(): in_full = lax.all_gather(in_weight, axis, axis=0, tiled=True)]
    dot_general x5 -> x2, matrix products: 120 us -> 30.1 us  [the longest x1 15.1 us: local(): lax.dot_general(go, out_full, (((1,), (1,)), ((), ())), preferred_element...]
    all_gather x1, waiting for transfers between devices: 31.2 us -> 81.6 us  [local(): out_full = lax.all_gather(out_weight, axis, axis=0, tiled=True)]
    unnamed x1 -> x0, blocking collectives: 43.8 us -> none
    psum x1 -> x0, blocking collectives: 38.6 us -> none  [local(): lax.psum(jnp.concatenate([hsums[0, :H], hsums[1, :H] * rate, d_skip]), axis)]
    unnamed x6 -> x2, waiting for transfers between devices: 15.2 us -> 0.71 us
  transfers between devices with their start and end apart: 5 -> 2, of which waited for: 5 -> 2; matrix products, arithmetic and copies ran while one was open for 11% -> 0% of each run, Pallas kernels for 0% -> 0%
where the time goes in v2:
time: 673 us; the launch traced here: 672 us
  Pallas kernels  370 us (55%)
  waiting for transfers between devices  218 us (32%)
  matrix products  46.1 us (7%)
  local copies, waits for them, and re-layouts  15.9 us (2%)
  between operations  14.2 us (2%)
  other arithmetic  6.99 us (1%)
    reduce_scatter x1, waiting for transfers between devices, local(): g_out = lax.psum_scatter(g_out, axis, scatter_dimension=0, tiled=True)  136 us
    pallas_call x1, Pallas kernels, run_reduce_in(): pl.pallas_call(functools.partial(reduce_in, axis, geom, K, E), grid=(K +...  127 us
    pallas_call x1, Pallas kernels, run_gather(): pl.pallas_call(functools.partial(gather_project, axis, geom, K), grid=(K...  112 us
    pallas_call x1, Pallas kernels, run_backward(): pl.pallas_call(functools.partial(mix_backward, dims, R // T), grid=(R //...  86.8 us
    all_gather x1, waiting for transfers between devices, local(): out_full = lax.all_gather(out_weight, axis, axis=0, tiled=True)  81.6 us
    pallas_call x1, Pallas kernels, run_forward(): pl.pallas_call(functools.partial(mix_forward, dims), grid=(R // T,), in_s...  43.7 us
    dot_general x1, matrix products, local(): jnp.dot(mixed, out_full, preferred_element_type=f32)  16 us
    dot_general x1, matrix products, local(): lax.dot_general(go, out_full, (((1,), (1,)), ((), ())), preferred_element...  15.1 us
  transfers between devices with their start and end apart: 2, of which 2 were waited for; matrix products, arithmetic and copies ran while one was open for 0% of the time, Pallas kernels for 0%

profile of v2, /device:TPU:0, one launch (start us, length us, event | category | flops | bytes accessed | tf_op | source)
XLA Modules:
  0.0 672.0 jit_solution(11796521411550575508)
XLA Ops:
  7.2 0.8 copy.25
  8.1 0.8 fusion.6
  8.9 1.2 concatenate.23
  10.1 0.9 pad_maximum_fusion.wl
  11.0 112.3 %gather_project.1 = (bf16[1024,6448]{1,0:T(8,128)(2,1)}, bf16[1536,6656]{1,0:T(8,128)(2,1)}, bf16[1536,1024]{1,0:T(8,128)(2,1)}, f32[8,1536]{1,0:T(8,128)}) custom-call(bf16[1024,1536]{1,0:T(8,128)(2,1)} %bitcast.56, bf16[13,48,512]{2,1,0:T(8,128)(2,1)} %pad_maximum_fusion.wl), custom_call_target="tpu_custom_call" | custom-call | flops 20283654144 | bytes 792330240 | tf_op jit(solution)/shard_map/gather_project/pallas_call | solution.py:773
  123.3 0.8 slice.93
  124.2 0.9 slice.94
  125.2 0.7 fusion.8
  126.0 0.7 broadcast_in_dim.28
  126.8 0.7 scatter.6
  127.9 43.7 %mix_forward.1 = (bf16[1024,3072]{1,0:T(8,128)(2,1)}, f32[1024,3072]{1,0:T(8,128)}, f32[1024,128]{1,0:T(8,128)S(1)}) custom-call(bf16[1024,6448]{1,0:T(8,128)(2,1)} %get-tuple-element.48.proj, f32[8,3328]{1,0:T(8,128)S(1)} %pad_convert_fusion.cpar, f32[8,128]{1,0:T(8,128)S(1)} %scatter.9.hpar, f32[8,3072]{1,0:T(8,128)S(1)} %maximum_maximum_fusion.dpar), custom_call_target="tpu_custom_call" | custom-call | flops 1610612736 | bytes 32079872 | tf_op jit(solution)/shard_map/mix_forward/pallas_call | solution.py:295
  171.6 0.8 copy-done.2
  172.4 15.0 %convolution_convert_fusion = bf16[3072,1536]{1,0:T(8,128)(2,1)} fusion(bf16[1024,3072]{1,0:T(8,128)(2,1)} %get-tuple-element.50, bf16[1024,1536]{1,0:T(8,128)(2,1)S(1)} %bitcast.54), kind=kOutput, calls=%fused_computation | convolution fusion | flops 9668395008 | bytes 18874368 | tf_op jit(solution)/shard_map/dot_general | solution.py:1011
  187.4 0.7 all-gather.2.cloned.1.call-update
  188.1 136.2 %reduce-scatter.2.cloned.1.call-done = bf16[96,1536]{1,0:T(8,128)(2,1)} async-done(((bf16[3072,1536]{1,0:T(8,128)(2,1)}), bf16[96,1536]{1,0:T(8,128)(2,1)}) %reduce-scatter.2.cloned.1.call-update) | async-done | bytes 294928 | tf_op jit(solution)/shard_map/reduce_scatter | solution.py:1014
  324.3 1.8 convert_element_type.50
  326.1 81.6 %all-gather.2.cloned.1.call-done = bf16[3072,1536]{1,0:T(8,128)(2,1)} async-done(((bf16[96,1536]{1,0:T(8,128)(2,1)}), bf16[3072,1536]{1,0:T(8,128)(2,1)}) %all-gather.2.cloned.1.call-update) | async-done | bytes 9437200 | tf_op jit(solution)/shard_map/all_gather | solution.py:976
  407.7 15.1 %fusion.9.dmixed = f32[1024,3072]{1,0:T(8,128)} fusion(bf16[1024,1536]{1,0:T(8,128)(2,1)S(1)} %bitcast.55, bf16[3072,1536]{1,0:T(8,128)(2,1)} %all-gather.2.cloned.1.call-done), kind=kOutput, calls=%fused_computation.31 | convolution fusion | flops 9663676416 | bytes 25165824 | tf_op jit(solution)/shard_map/dot_general | solution.py:1015
  422.8 86.8 %mix_backward.1 = (bf16[1024,6656]{1,0:T(8,128)(2,1)}, f32[8,3328]{1,0:T(8,128)}) custom-call(bf16[1024,6448]{1,0:T(8,128)(2,1)} %get-tuple-element.48.proj, f32[1024,3072]{1,0:T(8,128)} %fusion.9.dmixed, f32[1024,3072]{1,0:T(8,128)} %get-tuple-element.52.ssd, f32[1024,128]{1,0:T(8,128)} %copy-done.2, f32[8,3328]{1,0:T(8,128)} %copy-done, ...), custom_call_target="tpu_custom_call" | custom-call | flops 3221225472 | bytes 51576832 | tf_op jit(solution)/shard_map/mix_backward/pallas_call | solution.py:330
  509.6 127.4 %reduce_in.1 = (f32[48,6448]{1,0:T(8,128)}, f32[48,128]{1,0:T(8,128)}, f32[1024,1536]{1,0:T(8,128)}, f32[8,3328]{1,0:T(8,128)}) custom-call(bf16[16,2,48,1024]{3,2,1,0:T(8,128)(2,1)} %bitcast.59, bf16[1024,6656]{1,0:T(8,128)(2,1)} %get-tuple-element.54.dproj, bf16[1536,6656]{1,0:T(8,128)(2,1)} %get-tuple-element.49.wfull, bf16[48,6448]{1,0:T(8,128)(2,1)} %wl.1, ...), custom_call_target="tpu_custom_call" | custom-call | flops 40567308288 | bytes 792330240 | tf_op jit(solution)/shard_map/reduce_in/pallas_call | solution.py:911
  637.1 0.8 constant_dynamic-slice_fusion
  637.9 0.6 slice_bitcast_fusion
  638.9 1.2 slice_bitcast_fusion.1
  640.1 0.9 slice_reduce_fusion
  641.1 0.9 slice.90
  642.0 0.8 reduce_sum.19
  642.8 1.2 bitcast_multiply_fusion
  644.1 0.6 reduce_sum.18
  644.8 0.6 dynamic-slice_bitcast_fusion
  645.3 16.0 %add_convert_fusion = bf16[1024,1536]{1,0:T(8,128)(2,1)} fusion(bf16[1024,1536]{1,0:T(8,128)(2,1)} %bitcast.58, bf16[1024,3072]{1,0:T(8,128)(2,1)} %get-tuple-element.50, bf16[3072,1536]{1,0:T(8,128)(2,1)} %all-gather.2.cloned.1.call-done), kind=kOutput, calls=%fused_computation.1 | convolution fusion | flops 9668395008 | bytes 22020096 | tf_op jit(solution)/shard_map/dot_general | solution.py:1010
  661.4 2.7 copy.40
  664.1 1.0 copy.41
  (34 shorter events, 1.6 us)
Async XLA Ops:
  7.2 317.1 %reduce-scatter.2.cloned.1.call-start = ((), (), s32[]{:S(2)}) async-start(), calls=%async_computation.2 | async-start | bytes 9732096 | tf_op jit(solution)/shard_map/reduce_scatter | solution.py:1014
  125.2 46.3 %copy-start = (f32[8,3328]{1,0:T(8,128)}, f32[8,3328]{1,0:T(8,128)S(1)}, u32[]{:S(2)}) copy-start(f32[8,3328]{1,0:T(8,128)S(1)} %pad_convert_fusion.cpar) | copy-start | bytes 319492
  127.7 43.9 %copy-start.1 = (f32[8,3072]{1,0:T(8,128)}, f32[8,3072]{1,0:T(8,128)S(1)}, u32[]{:S(2)}) copy-start(f32[8,3072]{1,0:T(8,128)S(1)} %maximum_maximum_fusion.dpar) | copy-start | bytes 294916
  127.9 43.7 %copy-start.3 = (f32[8,128]{1,0:T(8,128)}, f32[8,128]{1,0:T(8,128)S(1)}, u32[]{:S(2)}) copy-start(f32[8,128]{1,0:T(8,128)S(1)} %scatter.9.hpar) | copy-start | bytes 12292
  127.9 44.5 %copy-start.6 = (bf16[2,4,128,1536]{3,2,1,0:T(8,128)(2,1)S(1)}, bf16[2,4,128,1536]{3,2,1,0:T(8,128)(2,1)}, u32[]{:S(2)}) copy-start(bf16[2,4,128,1536]{3,2,1,0:T(8,128)(2,1)} %param.25) | copy-start | bytes 9437188
  171.6 0.8 copy-start.2
  187.4 220.3 %all-gather.2.cloned.1.call-start = ((), (), s32[]{:S(2)}) async-start(), calls=%async_computation.1 | async-start | bytes 9732096 | tf_op jit(solution)/shard_map/all_gather | solution.py:976
  645.3 16.0 %copy-start.4 = (f32[1024,1536]{1,0:T(8,128)S(1)}, f32[1024,1536]{1,0:T(8,128)}, u32[]{:S(2)}) copy-start(f32[1024,1536]{1,0:T(8,128)} %get-tuple-element.57) | copy-start | bytes 18874372
  661.4 2.7 copy-start.5
Sparse Core Ops, SparseCore 0:
  187.5 136.7 reduce-scatter.1
  327.2 80.4 all-gather.1

commit v3 on v2

--- a/solution.py
+++ b/solution.py
@@ -71,8 +71,396 @@
     )
 
 
-def mix_forward(dims, proj, cpar, hpar, dpar, mixed, ssd, rstd,
-                pad, gated, colb, rowb, mask, scores, acc, dtp):
+MESH = pl.DeviceIdType.MESH
+CHUNK = 512
+VMEM = 67043328
+
+
+def geometry(n):
+    chips = n // 2
+    A0 = 4 if chips % 4 == 0 else 1
+    A = math.isqrt(chips // A0)
+    return (A0, A) if n % 2 == 0 and A > 1 and A0 * A * A == chips else None
+
+
+class Place:
+    def __init__(self, axis, A0, A):
+        me = lax.axis_index(axis)
+        self.A0, self.A = A0, A
+        self.c = lax.rem(me, 2)
+        chip = lax.div(me, 2)
+        self.a2 = lax.rem(chip, A)
+        self.a1 = lax.rem(lax.div(chip, A), A)
+        self.a0 = lax.div(chip, A * A)
+        c = self.c
+        self.f = self.a1 + c * (self.a2 - self.a1)
+        self.s = self.a2 + c * (self.a1 - self.a2)
+        self.sf = A + c * (1 - A)
+        self.ss = 1 + c * (A - 1)
+
+    def pos(self, f, s):
+        return f * self.sf + s * self.ss
+
+    def device(self, a0, f, s, c):
+        return ((a0 * self.A * self.A + self.pos(f, s)) * 2 + c,)
+
+    def line(self, q):
+        return lax.rem(self.a0 + q + self.A0, self.A0)
+
+    def first(self, q):
+        return lax.rem(self.f + q + self.A, self.A)
+
+    def second(self, q):
+        return lax.rem(self.s + q + self.A, self.A)
+
+    def partner(self):
+        return self.device(self.a0, self.f, self.s, 1 - self.c)
+
+    def peers(self):
+        out = [self.partner()]
+        out += [self.device(self.line(q), self.f, self.s, self.c) for q in range(1, self.A0)]
+        out += [self.device(self.a0, self.first(q), self.s, self.c) for q in range(1, self.A)]
+        out += [self.device(self.a0, self.f, self.second(q), self.c) for q in range(1, self.A)]
+        return out
+
+    def barrier(self):
+        sem = pltpu.get_barrier_semaphore()
+        peers = self.peers()
+        for peer in peers:
+            pl.semaphore_signal(sem, inc=1, device_id=peer, device_id_type=MESH)
+        pl.semaphore_wait(sem, len(peers))
+
+
+def columns(j, w):
+    return pl.ds(pl.multiple_of(j * w, w), w)
+
+
+def send(src, dst, ssem, rsem, device):
+    return pltpu.make_async_remote_copy(
+        src_ref=src, dst_ref=dst, send_sem=ssem, recv_sem=rsem,
+        device_id=device, device_id_type=MESH,
+    )
+
+
+class Gather:
+    def __init__(self, at, K, mine, whole, ssem, rsem, lsem):
+        self.at, self.K, self.mine, self.whole = at, K, mine, whole
+        self.ssem, self.rsem, self.lsem = ssem, rsem, lsem
+
+    @staticmethod
+    def scratch(K, A0, A):
+        NS = (A0 - 1) + (A - 1) + (A - 1) * A + 1
+        return [
+            pltpu.SemaphoreType.DMA((2, NS)),
+            pltpu.SemaphoreType.DMA((K, NS)),
+            pltpu.SemaphoreType.DMA((2,)),
+        ]
+
+    def local(self, j):
+        at = self.at
+        return pltpu.make_async_copy(
+            self.mine(j), self.whole(j, at.a0, at.pos(at.f, at.s), at.c),
+            self.lsem.at[lax.rem(j, 2)],
+        )
+
+    def copies(self, stage, j, sending):
+        at, whole = self.at, self.whole
+        A0, A = at.A0, at.A
+        par = lax.rem(j, 2)
+        every = slice(None)
+        out = []
+
+        def add(k, src, dst, device):
+            out.append(send(src, dst, self.ssem.at[par, k], self.rsem.at[j, k], device))
+
+        if stage == 0:
+            for q in range(1, A0):
+                a = at.a0 if sending else at.line(-q)
+                add(q - 1, self.mine(j), whole(j, a, at.pos(at.f, at.s), at.c),
+                    at.device(at.line(q), at.f, at.s, at.c))
+        elif stage == 1:
+            for q in range(1, A):
+                f = at.f if sending else at.first(-q)
+                ref = whole(j, every, at.pos(f, at.s), at.c)
+                add(A0 - 1 + q - 1, ref, ref, at.device(at.a0, at.first(q), at.s, at.c))
+        elif stage == 2:
+            for q in range(1, A):
+                s = at.s if sending else at.second(-q)
+                for o in range(A):
+                    ref = whole(j, every, at.pos(o, s), at.c)
+                    add(A0 - 1 + A - 1 + (q - 1) * A + o, ref, ref,
+                        at.device(at.a0, at.f, at.second(q), at.c))
+        else:
+            ref = whole(j, every, every, at.c if sending else 1 - at.c)
+            add(A0 - 1 + (A - 1) * (A + 1), ref, ref, at.partner())
+        return out
+
+    def step(self, i):
+        for stage in range(5):
+            j = i - stage
+
+            @pl.when((j >= 0) & (j < self.K))
+            def _(stage=stage, j=j):
+                if stage > 0:
+                    for cp in self.copies(stage - 1, j, False):
+                        cp.wait_recv()
+                if stage < 4:
+
+                    @pl.when(j >= 2)
+                    def _():
+                        for cp in self.copies(stage, j - 2, True):
+                            cp.wait_send()
+
+                    if stage == 1:
+                        self.local(j).wait()
+                    for cp in self.copies(stage, j, True):
+                        cp.start()
+                    if stage == 0:
+                        self.local(j).start()
+
+    def drain(self):
+        for j in range(max(0, self.K - 2), self.K):
+            for stage in range(4):
+                for cp in self.copies(stage, jnp.int32(j), True):
+                    cp.wait_send()
+
+
+class Reduce:
+    def __init__(self, at, K, refs):
+        self.at, self.K = at, K
+        (self.own0, self.own1, self.own2, self.own3, self.s0, self.s1, self.s2, self.s3,
+         self.r0, self.r1, self.r2, self.r3, self.ssem, self.rsem) = refs
+
+    @staticmethod
+    def sems(A0, A):
+        return 1 + (A - 1) + (A - 1) + (A0 - 1)
+
+    @staticmethod
+    def scratch(K, A0, A, r, w):
+        N = A0 * A * A
+        NS = Reduce.sems(A0, A)
+        return [
+            pltpu.VMEM((2, N, r, w), f32),
+            pltpu.VMEM((2, A0 * A, r, w), f32),
+            pltpu.VMEM((2, A0, r, w), f32),
+            pltpu.VMEM((2, r, w), f32),
+            pltpu.VMEM((2, N, r, w), bf16),
+            pltpu.VMEM((2, A - 1, A0 * A, r, w), bf16),
+            pltpu.VMEM((2, A - 1, A0, r, w), bf16),
+            pltpu.VMEM((2, A0 - 1, r, w), bf16),
+            pltpu.VMEM((K, N, r, w), bf16),
+            pltpu.VMEM((K, A - 1, A0 * A, r, w), bf16),
+            pltpu.VMEM((K, A - 1, A0, r, w), bf16),
+            pltpu.VMEM((K, A0 - 1, r, w), bf16),
+            pltpu.SemaphoreType.DMA((2, NS)),
+            pltpu.SemaphoreType.DMA((K, NS)),
+        ]
+
+    def copies(self, stage, j):
+        at = self.at
+        A0, A = at.A0, at.A
+        par = lax.rem(j, 2)
+
+        def make(k, src, dst, device):
+            return send(src, dst, self.ssem.at[par, k], self.rsem.at[j, k], device)
+
+        if stage == 0:
+            return [make(0, self.s0.at[par], self.r0.at[j], at.partner())]
+        if stage == 1:
+            return [
+                make(q, self.s1.at[par, q - 1], self.r1.at[j, q - 1],
+                     at.device(at.a0, at.f, at.second(q), at.c))
+                for q in range(1, A)
+            ]
+        if stage == 2:
+            return [
+                make(A - 1 + q, self.s2.at[par, q - 1], self.r2.at[j, q - 1],
+                     at.device(at.a0, at.first(q), at.s, at.c))
+                for q in range(1, A)
+            ]
+        return [
+            make(2 * (A - 1) + q, self.s3.at[par, q - 1], self.r3.at[j, q - 1],
+                 at.device(at.line(q), at.f, at.s, at.c))
+            for q in range(1, A0)
+        ]
+
+    def free(self, stage, j):
+        @pl.when(j >= 2)
+        def _():
+            for cp in self.copies(stage, j - 2):
+                cp.wait_send()
+
+    def start(self, stage, j):
+        for cp in self.copies(stage, j):
+            cp.start()
+
+    def arrive(self, stage, j):
+        for cp in self.copies(stage, j):
+            cp.wait_recv()
+
+    def begin(self, j, own, right):
+        N, r, w = self.own0.shape[1:]
+        par = lax.rem(j, 2)
+        self.free(0, j)
+        self.s0[par] = (
+            jnp.dot(own[1], right, preferred_element_type=f32).astype(bf16).reshape(N, r, w)
+        )
+        self.start(0, j)
+        self.own0[par] = jnp.dot(own[0], right, preferred_element_type=f32).reshape(N, r, w)
+
+    def step(self, i, finish):
+        at = self.at
+        A0, A = at.A0, at.A
+
+        def stage1(j):
+            par = lax.rem(j, 2)
+            self.arrive(0, j)
+            self.free(1, j)
+
+            def line(a, _):
+                for o in range(A):
+                    for q in range(A):
+                        b = a * A * A + at.pos(o, at.second(q))
+                        v = self.own0[par, b] + self.r0[j, b].astype(f32)
+                        if q == 0:
+                            self.own1[par, a * A + o] = v
+                        else:
+                            self.s1[par, q - 1, a * A + o] = v.astype(bf16)
+                return 0
+
+            lax.fori_loop(0, A0, line, 0)
+            self.start(1, j)
+
+        def stage2(j):
+            par = lax.rem(j, 2)
+            self.arrive(1, j)
+            self.free(2, j)
+
+            def line(a, _):
+                for q in range(A):
+                    b = a * A + at.first(q)
+                    v = self.own1[par, b]
+                    for p in range(A - 1):
+                        v = v + self.r1[j, p, b].astype(f32)
+                    if q == 0:
+                        self.own2[par, a] = v
+                    else:
+                        self.s2[par, q - 1, a] = v.astype(bf16)
+                return 0
+
+            lax.fori_loop(0, A0, line, 0)
+            self.start(2, j)
+
+        def stage3(j):
+            par = lax.rem(j, 2)
+            self.arrive(2, j)
+            self.free(3, j)
+            for q in range(A0):
+                a = at.line(q)
+                v = self.own2[par, a]
+                for p in range(A - 1):
+                    v = v + self.r2[j, p, a].astype(f32)
+                if q == 0:
+                    self.own3[par] = v
+                else:
+                    self.s3[par, q - 1] = v.astype(bf16)
+            self.start(3, j)
+
+        def stage4(j):
+            self.arrive(3, j)
+            v = self.own3[lax.rem(j, 2)]
+            for p in range(A0 - 1):
+                v = v + self.r3[j, p].astype(f32)
+            finish(j, v)
+
+        for k, stage in ((1, stage1), (2, stage2), (3, stage3), (4, stage4)):
+            j = i - k
+
+            @pl.when((j >= 0) & (j < self.K))
+            def _(j=j, stage=stage):
+                stage(j)
+
+    def drain(self):
+        for j in range(max(0, self.K - 2), self.K):
+            for stage in range(4):
+                for cp in self.copies(stage, jnp.int32(j)):
+                    cp.wait_send()
+
+
+class SumAll:
+    def __init__(self, at, refs):
+        self.at = at
+        self.hold, self.land, self.ssem, self.rsem = refs
+
+    @staticmethod
+    def scratch(A0, A, shape):
+        slots = 2 + A + A + A0
+        return [
+            pltpu.VMEM((4,) + shape, f32),
+            pltpu.VMEM((slots,) + shape, f32),
+            pltpu.SemaphoreType.DMA((slots,)),
+            pltpu.SemaphoreType.DMA((slots,)),
+        ]
+
+    def group(self, stage):
+        at = self.at
+        A0, A = at.A0, at.A
+        chip = at.a0 * A * A + at.a1 * A + at.a2
+        if stage == 0:
+            return 0, 2, at.c, 1, chip * 2
+        if stage == 1:
+            return 2, A, at.a2, 2, (chip - at.a2) * 2 + at.c
+        if stage == 2:
+            return 2 + A, A, at.a1, 2 * A, (chip - at.a1 * A) * 2 + at.c
+        return 2 + 2 * A, A0, at.a0, 2 * A * A, (chip - at.a0 * A * A) * 2 + at.c
+
+    def copies(self, stage, sending):
+        base, size, mine, stride, origin = self.group(stage)
+        out = []
+        for q in range(1, size):
+            to = lax.rem(mine + q, size)
+            slot = mine if sending else lax.rem(mine - q + size, size)
+            out.append(
+                send(self.hold.at[stage], self.land.at[base + slot], self.ssem.at[base + q],
+                     self.rsem.at[base + q], (origin + to * stride,))
+            )
+        return out
+
+    def start(self, stage, value):
+        base, _, mine, _, _ = self.group(stage)
+        self.hold[stage] = value
+        self.land[base + mine] = value
+        for cp in self.copies(stage, True):
+            cp.start()
+
+    def finish(self, stage):
+        base, size, _, _, _ = self.group(stage)
+        for cp in self.copies(stage, False):
+            cp.wait_recv()
+        for cp in self.copies(stage, True):
+            cp.wait_send()
+        total = self.land[base]
+        for k in range(1, size):
+            total = total + self.land[base + k]
+        return total
+
+
+def mix_forward(dims, net_of, proj, cpar, hpar, dpar, *refs):
+    if net_of is None:
+        mixed, ssd, rstd, *refs = refs
+        between = lambda half: None
+    else:
+        wl, mixed, ssd, rstd, wfull, *refs = refs
+        net = net_of(wl, wfull, refs[8:])
+        i = pl.program_id(0)
+
+        @pl.when(i == 0)
+        def _():
+            net.at.barrier()
+
+        between = lambda half: net.step(2 * i + half)
+    pad, gated, colb, rowb, mask, scores, acc, dtp = refs[:8]
+    between(0)
     T, DI, H, HD, ST = dims["T"], dims["DI"], dims["H"], dims["HD"], dims["ST"]
     HP = LANES // HD
     tiles = DI // LANES
@@ -119,21 +507,59 @@
         acc[...] += total
         return 0
 
-    lax.fori_loop(0, tiles // UNROLL_F, body, 0)
+    trips = tiles // UNROLL_F
+    lax.fori_loop(0, trips // 2, body, 0)
+    between(1)
+    lax.fori_loop(trips // 2, trips, body, 0)
     r = lax.rsqrt(jnp.sum(acc[...], axis=1, keepdims=True) * (1.0 / DI) + epsilon)
     rb = jnp.broadcast_to(r, (T, LANES))
     rstd[...] = rb
 
     def finish(j, _):
         lanes = pl.ds(pl.multiple_of(j * LANES, LANES), LANES)
-        mixed[:, lanes] = (gated[:, lanes] * rb * dpar[1:2, lanes]).astype(bf16)
+        mixed[lanes, :] = (gated[:, lanes] * rb * dpar[1:2, lanes]).T.astype(bf16)
         return 0
 
     lax.fori_loop(0, tiles, finish, 0)
-
-
-def mix_backward(dims, steps, proj, dmixed, ssd, rstd, cpar, hpar, dpar, dproj, small,
-                 cacc, dacc, hacc, pad, dpad, colb, rowb, mask, scores, acc, dtp, dscores, dlog, csum, bcs):
+    if net_of is not None:
+
+        @pl.when(i == pl.num_programs(0) - 1)
+        def _():
+            net.drain()
+
+
+def mix_backward(dims, steps, net_of, proj, dmixed, ssd, rstd, cpar, hpar, dpar, *refs):
+    if net_of is None:
+        dproj, small, *refs = refs
+        between = lambda half: None
+    else:
+        mT, go, dproj, small, dow, *refs = refs
+        net, own = net_of(refs[15:])
+        N, _, r, R = mT.shape
+        w = net.own3.shape[2]
+        i = pl.program_id(0)
+
+        @pl.when(i == 0)
+        def _():
+            net.at.barrier()
+            own[0] = mT[:, net.at.c].reshape(N * r, R)
+            own[1] = mT[:, 1 - net.at.c].reshape(N * r, R)
+
+        def finish(j, v):
+            dow[:, columns(j, w)] = v
+
+        def between(half):
+            k = 2 * i + half
+
+            @pl.when(k < net.K)
+            def _():
+                net.begin(k, own, go[:, columns(k, w)])
+
+            net.step(k, finish)
+
+    (cacc, dacc, hacc, pad, dpad, colb, rowb, mask, scores, acc, dtp, dscores, dlog, csum,
+     bcs) = refs[:15]
+    between(0)
     T, DI, C, H, HD, ST, KW = (dims[k] for k in ("T", "DI", "C", "H", "HD", "ST", "KW"))
     HP = LANES // HD
     tiles = DI // LANES
@@ -246,7 +672,10 @@
         csum[...] += sums[2]
         return 0
 
-    lax.fori_loop(0, tiles // UNROLL_B, body, 0)
+    trips = tiles // UNROLL_B
+    lax.fori_loop(0, trips // 2, body, 0)
+    between(1)
+    lax.fori_loop(trips // 2, trips, body, 0)
     ds = dscores[...].astype(bf16)
     dst = dscores[...].T.astype(bf16)
     dact = (
@@ -273,6 +702,12 @@
     hacc[0:8, :] += sum8(ddt)
     hacc[8:16, :] += sum8(dsteps * step)
 
+    if net_of is not None:
+
+        @pl.when(i == steps - 1)
+        def _():
+            net.drain()
+
     @pl.when(pl.program_id(0) == steps - 1)
     def _():
         small[...] = jnp.zeros_like(small)
@@ -287,21 +722,41 @@
             )
 
 
-def run_forward(dims, proj, cpar, hpar, dpar):
+def run_forward(dims, axis, geom, proj, cpar, hpar, dpar, ow):
     T, DI, C, H, KW = dims["T"], dims["DI"], dims["C"], dims["H"], dims["KW"]
     R, E = proj.shape
+    steps = R // T
     rows = lambda w: pl.BlockSpec((T, w), lambda i: (i, 0))
     whole = lambda a: pl.BlockSpec(a.shape, lambda i: (0, 0))
+    args, net_of, outs, shapes, sems, extra = [], None, [], [], [], {}
+    if geom is not None:
+        A0, A = geom
+        r, D = ow.shape
+        w = D // (2 * steps - 4)
+        K = D // w
+
+        def net_of(wl, wfull, sems):
+            return Gather(
+                Place(axis, A0, A), K, lambda j: wl.at[:, columns(j, w)],
+                lambda j, a, p, c: wfull.at[a, p, c, :, columns(j, w)], *sems,
+            )
+
+        args = [ow]
+        outs = [pl.BlockSpec(memory_space=pl.ANY)]
+        shapes = [jax.ShapeDtypeStruct((A0, A * A, 2, r, D), bf16)]
+        sems = Gather.scratch(K, A0, A)
+        extra = dict(collective_id=3, has_side_effects=True)
     return pl.pallas_call(
-        functools.partial(mix_forward, dims),
-        grid=(R // T,),
-        in_specs=[rows(E), whole(cpar), whole(hpar), whole(dpar)],
-        out_specs=[rows(DI), rows(DI), rows(LANES)],
+        functools.partial(mix_forward, dims, net_of),
+        grid=(steps,),
+        in_specs=[rows(E), whole(cpar), whole(hpar), whole(dpar)] + [whole(a) for a in args],
+        out_specs=[pl.BlockSpec((DI, T), lambda i: (0, i)), rows(DI), rows(LANES)] + outs,
         out_shape=[
-            jax.ShapeDtypeStruct((R, DI), bf16),
+            jax.ShapeDtypeStruct((DI, R), bf16),
             jax.ShapeDtypeStruct((R, DI), f32),
             jax.ShapeDtypeStruct((R, LANES), f32),
-        ],
+        ]
+        + shapes,
         scratch_shapes=[
             pltpu.VMEM((max(2, UNROLL_F), FRONT + T, LANES), f32),
             pltpu.VMEM((T, DI), f32),
@@ -311,32 +766,54 @@
             pltpu.VMEM((T, T), f32),
             pltpu.VMEM((T, LANES), f32),
             pltpu.VMEM((T, LANES), f32),
-        ],
-        compiler_params=pltpu.CompilerParams(vmem_limit_bytes=48 << 20),
+        ]
+        + sems,
+        compiler_params=pltpu.CompilerParams(vmem_limit_bytes=48 << 20, **extra),
         cost_estimate=pl.CostEstimate(
             flops=4 * R * DI * T, bytes_accessed=R * (2 * E + 6 * DI), transcendentals=R * H * T
         ),
         name="mix_forward",
-    )(proj, cpar, hpar, dpar)
-
-
-def run_backward(dims, EP, proj, dmixed, ssd, rstd, cpar, hpar, dpar):
+    )(proj, cpar, hpar, dpar, *args)
+
+
+def run_backward(dims, axis, geom, EP, proj, dmixed, ssd, rstd, cpar, hpar, dpar, mixed, go):
     T, DI, C, H, KW, ST = (dims[k] for k in ("T", "DI", "C", "H", "KW", "ST"))
     R, E = proj.shape
+    steps = R // T
     rows = lambda w: pl.BlockSpec((T, w), lambda i: (i, 0))
-    whole = lambda s: pl.BlockSpec(s, lambda i: (0, 0))
+    whole = lambda s: pl.BlockSpec(s, lambda i: (0,) * len(s))
+    once = lambda s: pl.BlockSpec(s, lambda i: (0,) * len(s), pipeline_mode=pl.Buffered(1))
     assert KW + 4 <= 8
     sums = [(8 * (KW + 1), C), (16, DI), (16, LANES)]
+    args, net_of, ins, outs, shapes, scratch, extra = [], None, [], [], [], [], {}
+    if geom is not None:
+        A0, A = geom
+        N = A0 * A * A
+        r, D = DI // (2 * N), go.shape[1]
+        w = 2 * LANES
+        K = D // w
+        assert K + 4 <= 2 * steps
+
+        def net_of(refs):
+            return Reduce(Place(axis, A0, A), K, refs[1:15]), refs[0]
+
+        args = [mixed.reshape(N, 2, r, R), go]
+        ins = [once((N, 2, r, R)), once((R, D))]
+        outs = [once((r, D))]
+        shapes = [jax.ShapeDtypeStruct((r, D), f32)]
+        scratch = [pltpu.VMEM((2, N * r, R), bf16)] + Reduce.scratch(K, A0, A, r, w)
+        extra = dict(collective_id=4, has_side_effects=True)
     return pl.pallas_call(
-        functools.partial(mix_backward, dims, R // T),
-        grid=(R // T,),
+        functools.partial(mix_backward, dims, steps, net_of),
+        grid=(steps,),
         in_specs=[rows(E), rows(DI), rows(DI), rows(LANES)]
-        + [whole(a.shape) for a in (cpar, hpar, dpar)],
-        out_specs=[rows(EP), whole((8, C))],
+        + [whole(a.shape) for a in (cpar, hpar, dpar)] + ins,
+        out_specs=[rows(EP), whole((8, C))] + outs,
         out_shape=[
             jax.ShapeDtypeStruct((R, EP), bf16),
             jax.ShapeDtypeStruct((8, C), f32),
-        ],
+        ]
+        + shapes,
         scratch_shapes=[pltpu.VMEM(s, f32) for s in sums]
         + [
             pltpu.VMEM((max(2, UNROLL_B), FRONT + T, LANES), f32),
@@ -351,370 +828,17 @@
             pltpu.VMEM((T, LANES), f32),
             pltpu.VMEM((T, LANES), f32),
             pltpu.VMEM((2, T, ST), bf16),
-        ],
-        compiler_params=pltpu.CompilerParams(vmem_limit_bytes=56 << 20),
+        ]
+        + scratch,
+        compiler_params=pltpu.CompilerParams(vmem_limit_bytes=VMEM, **extra),
         cost_estimate=pl.CostEstimate(
             flops=8 * R * DI * T, bytes_accessed=R * (4 * E + 8 * DI), transcendentals=R * H * T
         ),
         name="mix_backward",
-    )(proj, dmixed, ssd, rstd, cpar, hpar, dpar)
-
-
-MESH = pl.DeviceIdType.MESH
-CHUNK = 512
-VMEM = 67043328
-
-
-def geometry(n):
-    chips = n // 2
-    A0 = 4 if chips % 4 == 0 else 1
-    A = math.isqrt(chips // A0)
-    return (A0, A) if n % 2 == 0 and A > 1 and A0 * A * A == chips else None
-
-
-class Place:
-    def __init__(self, axis, A0, A):
-        me = lax.axis_index(axis)
-        self.A0, self.A = A0, A
-        self.c = lax.rem(me, 2)
-        chip = lax.div(me, 2)
-        self.a2 = lax.rem(chip, A)
-        self.a1 = lax.rem(lax.div(chip, A), A)
-        self.a0 = lax.div(chip, A * A)
-        c = self.c
-        self.f = self.a1 + c * (self.a2 - self.a1)
-        self.s = self.a2 + c * (self.a1 - self.a2)
-        self.sf = A + c * (1 - A)
-        self.ss = 1 + c * (A - 1)
-
-    def pos(self, f, s):
-        return f * self.sf + s * self.ss
-
-    def device(self, a0, f, s, c):
-        return ((a0 * self.A * self.A + self.pos(f, s)) * 2 + c,)
-
-    def line(self, q):
-        return lax.rem(self.a0 + q + self.A0, self.A0)
-
-    def first(self, q):
-        return lax.rem(self.f + q + self.A, self.A)
-
-    def second(self, q):
-        return lax.rem(self.s + q + self.A, self.A)
-
-    def partner(self):
-        return self.device(self.a0, self.f, self.s, 1 - self.c)
-
-    def peers(self):
-        out = [self.partner()]
-        out += [self.device(self.line(q), self.f, self.s, self.c) for q in range(1, self.A0)]
-        out += [self.device(self.a0, self.first(q), self.s, self.c) for q in range(1, self.A)]
-        out += [self.device(self.a0, self.f, self.second(q), self.c) for q in range(1, self.A)]
-        return out
-
-    def barrier(self):
-        sem = pltpu.get_barrier_semaphore()
-        peers = self.peers()
-        for peer in peers:
-            pl.semaphore_signal(sem, inc=1, device_id=peer, device_id_type=MESH)
-        pl.semaphore_wait(sem, len(peers))
-
-
-def send(src, dst, ssem, rsem, device):
-    return pltpu.make_async_remote_copy(
-        src_ref=src, dst_ref=dst, send_sem=ssem, recv_sem=rsem,
-        device_id=device, device_id_type=MESH,
-    )
-
-
-class Gather:
-    def __init__(self, at, K, wl, buf, ssem, rsem, lsem):
-        self.at, self.K, self.wl, self.buf = at, K, wl, buf
-        self.ssem, self.rsem, self.lsem = ssem, rsem, lsem
-
-    @staticmethod
-    def sems(A0, A):
-        return (A0 - 1) + (A - 1) + (A - 1) * A + 1
-
-    def local(self, j):
-        at = self.at
-        return pltpu.make_async_copy(
-            self.wl.at[j], self.buf.at[j, at.a0, at.pos(at.f, at.s), at.c],
-            self.lsem.at[lax.rem(j, 2)],
-        )
-
-    def copies(self, stage, j, sending):
-        at, buf = self.at, self.buf
-        A0, A = at.A0, at.A
-        par = lax.rem(j, 2)
-        out = []
-
-        def add(k, src, dst, device):
-            out.append(send(src, dst, self.ssem.at[par, k], self.rsem.at[j, k], device))
-
-        if stage == 0:
-            for q in range(1, A0):
-                a = at.a0 if sending else at.line(-q)
-                add(q - 1, self.wl.at[j], buf.at[j, a, at.pos(at.f, at.s), at.c],
-                    at.device(at.line(q), at.f, at.s, at.c))
-        elif stage == 1:
-            for q in range(1, A):
-                f = at.f if sending else at.first(-q)
-                ref = buf.at[j, :, at.pos(f, at.s), at.c]
-                add(A0 - 1 + q - 1, ref, ref, at.device(at.a0, at.first(q), at.s, at.c))
-        elif stage == 2:
-            for q in range(1, A):
-                s = at.s if sending else at.second(-q)
-                for o in range(A):
-                    ref = buf.at[j, :, at.pos(o, s), at.c]
-                    add(A0 - 1 + A - 1 + (q - 1) * A + o, ref, ref,
-                        at.device(at.a0, at.f, at.second(q), at.c))
-        else:
-            ref = buf.at[j, :, :, at.c if sending else 1 - at.c]
-            add(A0 - 1 + (A - 1) * (A + 1), ref, ref, at.partner())
-        return out
-
-    def step(self, i):
-        for stage in range(5):
-            j = i - stage
-
-            @pl.when((j >= 0) & (j < self.K))
-            def _(stage=stage, j=j):
-                if stage > 0:
-                    for cp in self.copies(stage - 1, j, False):
-                        cp.wait_recv()
-                if stage < 4:
-
-                    @pl.when(j >= 2)
-                    def _():
-                        for cp in self.copies(stage, j - 2, True):
-                            cp.wait_send()
-
-                    if stage == 1:
-                        self.local(j).wait()
-                    for cp in self.copies(stage, j, True):
-                        cp.start()
-                    if stage == 0:
-                        self.local(j).start()
-
-    def drain(self):
-        for j in range(max(0, self.K - 2), self.K):
-            for stage in range(4):
-                for cp in self.copies(stage, jnp.int32(j), True):
-                    cp.wait_send()
-
-
-class Reduce:
-    def __init__(self, at, K, refs):
-        self.at, self.K = at, K
-        (self.own0, self.own1, self.own2, self.own3, self.s0, self.s1, self.s2, self.s3,
-         self.r0, self.r1, self.r2, self.r3, self.ssem, self.rsem) = refs
-
-    @staticmethod
-    def sems(A0, A):
-        return 1 + (A - 1) + (A - 1) + (A0 - 1)
-
-    @staticmethod
-    def scratch(K, A0, A, r, w):
-        N = A0 * A * A
-        NS = Reduce.sems(A0, A)
-        return [
-            pltpu.VMEM((2, N, r, w), f32),
-            pltpu.VMEM((2, A0 * A, r, w), f32),
-            pltpu.VMEM((2, A0, r, w), f32),
-            pltpu.VMEM((2, r, w), f32),
-            pltpu.VMEM((2, N, r, w), bf16),
-            pltpu.VMEM((2, A - 1, A0 * A, r, w), bf16),
-            pltpu.VMEM((2, A - 1, A0, r, w), bf16),
-            pltpu.VMEM((2, A0 - 1, r, w), bf16),
-            pltpu.VMEM((K, N, r, w), bf16),
-            pltpu.VMEM((K, A - 1, A0 * A, r, w), bf16),
-            pltpu.VMEM((K, A - 1, A0, r, w), bf16),
-            pltpu.VMEM((K, A0 - 1, r, w), bf16),
-            pltpu.SemaphoreType.DMA((2, NS)),
-            pltpu.SemaphoreType.DMA((K, NS)),
-        ]
-
-    def copies(self, stage, j):
-        at = self.at
-        A0, A = at.A0, at.A
-        par = lax.rem(j, 2)
-
-        def make(k, src, dst, device):
-            return send(src, dst, self.ssem.at[par, k], self.rsem.at[j, k], device)
-
-        if stage == 0:
-            return [make(0, self.s0.at[par], self.r0.at[j], at.partner())]
-        if stage == 1:
-            return [
-                make(q, self.s1.at[par, q - 1], self.r1.at[j, q - 1],
-                     at.device(at.a0, at.f, at.second(q), at.c))
-                for q in range(1, A)
-            ]
-        if stage == 2:
-            return [
-                make(A - 1 + q, self.s2.at[par, q - 1], self.r2.at[j, q - 1],
-                     at.device(at.a0, at.first(q), at.s, at.c))
-                for q in range(1, A)
-            ]
-        return [
-            make(2 * (A - 1) + q, self.s3.at[par, q - 1], self.r3.at[j, q - 1],
-                 at.device(at.line(q), at.f, at.s, at.c))
-            for q in range(1, A0)
-        ]
-
-    def free(self, stage, j):
-        @pl.when(j >= 2)
-        def _():
-            for cp in self.copies(stage, j - 2):
-                cp.wait_send()
-
-    def start(self, stage, j):
-        for cp in self.copies(stage, j):
-            cp.start()
-
-    def arrive(self, stage, j):
-        for cp in self.copies(stage, j):
-            cp.wait_recv()
-
-    def step(self, i, finish):
-        at = self.at
-        A0, A = at.A0, at.A
-
-        def stage1(j):
-            par = lax.rem(j, 2)
-            self.arrive(0, j)
-            self.free(1, j)
-
-            def line(a, _):
-                for o in range(A):
-                    for q in range(A):
-                        b = a * A * A + at.pos(o, at.second(q))
-                        v = self.own0[par, b] + self.r0[j, b].astype(f32)
-                        if q == 0:
-                            self.own1[par, a * A + o] = v
-                        else:
-                            self.s1[par, q - 1, a * A + o] = v.astype(bf16)
-                return 0
-
-            lax.fori_loop(0, A0, line, 0)
-            self.start(1, j)
-
-        def stage2(j):
-            par = lax.rem(j, 2)
-            self.arrive(1, j)
-            self.free(2, j)
-
-            def line(a, _):
-                for q in range(A):
-                    b = a * A + at.first(q)
-                    v = self.own1[par, b]
-                    for p in range(A - 1):
-                        v = v + self.r1[j, p, b].astype(f32)
-                    if q == 0:
-                        self.own2[par, a] = v
-                    else:
-                        self.s2[par, q - 1, a] = v.astype(bf16)
-                return 0
-
-            lax.fori_loop(0, A0, line, 0)
-            self.start(2, j)
-
-        def stage3(j):
-            par = lax.rem(j, 2)
-            self.arrive(2, j)
-            self.free(3, j)
-            for q in range(A0):
-                a = at.line(q)
-                v = self.own2[par, a]
-                for p in range(A - 1):
-                    v = v + self.r2[j, p, a].astype(f32)
-                if q == 0:
-                    self.own3[par] = v
-                else:
-                    self.s3[par, q - 1] = v.astype(bf16)
-            self.start(3, j)
-
-        def stage4(j):
-            self.arrive(3, j)
-            v = self.own3[lax.rem(j, 2)]
-            for p in range(A0 - 1):
-                v = v + self.r3[j, p].astype(f32)
-            finish(j, v)
-
-        for k, stage in ((1, stage1), (2, stage2), (3, stage3), (4, stage4)):
-            j = i - k
-
-            @pl.when((j >= 0) & (j < self.K))
-            def _(j=j, stage=stage):
-                stage(j)
-
-    def drain(self):
-        for j in range(max(0, self.K - 2), self.K):
-            for stage in range(4):
-                for cp in self.copies(stage, jnp.int32(j)):
-                    cp.wait_send()
-
-
-class SumAll:
-    def __init__(self, at, refs):
-        self.at = at
-        self.hold, self.land, self.ssem, self.rsem = refs
-
-    @staticmethod
-    def scratch(A0, A, shape):
-        slots = 2 + A + A + A0
-        return [
-            pltpu.VMEM((4,) + shape, f32),
-            pltpu.VMEM((slots,) + shape, f32),
-            pltpu.SemaphoreType.DMA((slots,)),
-            pltpu.SemaphoreType.DMA((slots,)),
-        ]
-
-    def group(self, stage):
-        at = self.at
-        A0, A = at.A0, at.A
-        chip = at.a0 * A * A + at.a1 * A + at.a2
-        if stage == 0:
-            return 0, 2, at.c, 1, chip * 2
-        if stage == 1:
-            return 2, A, at.a2, 2, (chip - at.a2) * 2 + at.c
-        if stage == 2:
-            return 2 + A, A, at.a1, 2 * A, (chip - at.a1 * A) * 2 + at.c
-        return 2 + 2 * A, A0, at.a0, 2 * A * A, (chip - at.a0 * A * A) * 2 + at.c
-
-    def copies(self, stage, sending):
-        base, size, mine, stride, origin = self.group(stage)
-        out = []
-        for q in range(1, size):
-            to = lax.rem(mine + q, size)
-            slot = mine if sending else lax.rem(mine - q + size, size)
-            out.append(
-                send(self.hold.at[stage], self.land.at[base + slot], self.ssem.at[base + q],
-                     self.rsem.at[base + q], (origin + to * stride,))
-            )
-        return out
-
-    def start(self, stage, value):
-        base, _, mine, _, _ = self.group(stage)
-        self.hold[stage] = value
-        self.land[base + mine] = value
-        for cp in self.copies(stage, True):
-            cp.start()
-
-    def finish(self, stage):
-        base, size, _, _, _ = self.group(stage)
-        for cp in self.copies(stage, False):
-            cp.wait_recv()
-        for cp in self.copies(stage, True):
-            cp.wait_send()
-        total = self.land[base]
-        for k in range(1, size):
-            total = total + self.land[base + k]
-        return total
-
-
-def gather_project(axis, geom, K, tok, wl, proj, wfull, uT, scale, buf, uh, ssem, rsem, lsem):
+    )(proj, dmixed, ssd, rstd, cpar, hpar, dpar, *args)
+
+
+def gather_project(axis, geom, K, tok, wl, proj, wfull, uT, scale, buf, uh, *sems):
     A0, A = geom
     at = Place(axis, A0, A)
     i = pl.program_id(0)
@@ -725,7 +849,7 @@
     def _():
         at.barrier()
 
-    net = Gather(at, K, wl, buf, ssem, rsem, lsem)
+    net = Gather(at, K, lambda j: wl.at[j], lambda j, a, p, c: buf.at[j, a, p, c], *sems)
     net.step(i)
 
     @pl.when(i == 4)
@@ -767,7 +891,6 @@
     A0, A = geom
     R, D = tok.shape
     K, r, w = wl.shape
-    NS = Gather.sems(A0, A)
     late = lambda i: (0, lax.rem(jnp.maximum(i - 4, 0) + K - 1, K))
     once = dict(pipeline_mode=pl.Buffered(1))
     return pl.pallas_call(
@@ -792,10 +915,8 @@
         scratch_shapes=[
             pltpu.VMEM((K, A0, A * A, 2, r, w), bf16),
             pltpu.VMEM((R, D), bf16),
-            pltpu.SemaphoreType.DMA((2, NS)),
-            pltpu.SemaphoreType.DMA((K, NS)),
-            pltpu.SemaphoreType.DMA((2,)),
-        ],
+        ]
+        + Gather.scratch(K, A0, A),
         compiler_params=pltpu.CompilerParams(
             collective_id=1, has_side_effects=True, vmem_limit_bytes=VMEM
         ),
@@ -837,14 +958,7 @@
 
     @pl.when(i < K)
     def _():
-        par = lax.rem(i, 2)
-        net.free(0, i)
-        d = dproj[...]
-        net.s0[par] = (
-            jnp.dot(own[1], d, preferred_element_type=f32).astype(bf16).reshape(N, r, w)
-        )
-        net.start(0, i)
-        net.own0[par] = jnp.dot(own[0], d, preferred_element_type=f32).reshape(N, r, w)
+        net.begin(i, own, dproj[...])
         M = 256
 
         def rows(k, _):
@@ -973,7 +1087,6 @@
     ns = norm_scale.astype(f32)
     tok = tokens.reshape(R, D)
     go = grad_out.reshape(R, D)
-    out_full = lax.all_gather(out_weight, axis, axis=0, tiled=True)
     if own:
         rows = [conv_weight.T, conv_bias[None], gate_scale[None]]
         pads = jnp.concatenate(
@@ -990,6 +1103,7 @@
         conv, gate = got[:, : KW + 1, :Cn], got[:, KW + 1, :Gn]
     else:
         EP = E
+        out_full = lax.all_gather(out_weight, axis, axis=0, tiled=True)
         wfull = lax.all_gather(in_weight, axis, axis=0, tiled=True)
         conv = lax.all_gather(jnp.concatenate([conv_weight.T, conv_bias[None]]), axis, axis=0)
         gate = lax.all_gather(gate_scale, axis, axis=0)
@@ -1006,19 +1120,26 @@
     dpar = jnp.concatenate(
         [jnp.repeat(skip_d, HD)[None], gate.reshape(1, DI).astype(f32), jnp.zeros((6, DI), f32)]
     )
-    mixed, ssd, rstd = run_forward(dims, proj, cpar, hpar, dpar)
-    output = (tok.astype(f32) + jnp.dot(mixed, out_full, preferred_element_type=f32)).astype(bf16)
-    g_out = lax.dot_general(
-        mixed, go, (((0,), (0,)), ((), ())), preferred_element_type=f32
-    ).astype(bf16)
-    g_out = lax.psum_scatter(g_out, axis, scatter_dimension=0, tiled=True)
+    net = geom if own else None
+    mixed, ssd, rstd, *got = run_forward(dims, axis, net, proj, cpar, hpar, dpar, out_weight)
+    if own:
+        out_full = got[0].reshape(DI, D)
     d_mixed = lax.dot_general(go, out_full, (((1,), (1,)), ((), ())), preferred_element_type=f32)
-    dproj, small = run_backward(dims, EP, proj, d_mixed, ssd, rstd, cpar, hpar, dpar)
+    dproj, small, *got = run_backward(
+        dims, axis, net, EP, proj, d_mixed, ssd, rstd, cpar, hpar, dpar, mixed, go
+    )
+    output = lax.dot_general(
+        mixed, out_full, (((0,), (0,)), ((), ())), preferred_element_type=f32
+    )
+    output = (tok.astype(f32) + output).astype(bf16)
     if own:
+        dow = got[0]
         dw, dns, dtok, sums = run_reduce_in(
             axis, geom, uT, dproj, wfull, in_weight, scale, tok, go, small
         )
     else:
+        g_out = jnp.dot(mixed, go, preferred_element_type=f32).astype(bf16)
+        dow = lax.psum_scatter(g_out, axis, scatter_dimension=0, tiled=True).astype(f32)
         g_in = lax.dot_general(
             uh, dproj, (((0,), (0,)), ((), ())), preferred_element_type=f32
         ).astype(bf16)
@@ -1041,7 +1162,7 @@
         sums[KW + 1, :DI].reshape(H, HD).sum(axis=1),
         dns.sum(axis=1) / ns,
         lax.dynamic_slice(sums[KW + 2], (me * Gn,), (Gn,)),
-        g_out.astype(f32),
+        dow,
     )
 
 

time: 673 us -> 502 us (0.75)
  waiting for transfers between devices: 218 us -> 0 us
  Pallas kernels: 370 us -> 447 us
  matrix products: 46.1 us -> 28.5 us
  between operations: 14.2 us -> 0.86 us
    reduce_scatter x1 -> x0, waiting for transfers between devices: 136 us -> none  [local(): g_out = lax.psum_scatter(g_out, axis, scatter_dimension=0, tiled=True)]
    all_gather x1 -> x0, waiting for transfers between devices: 81.6 us -> none  [local(): out_full = lax.all_gather(out_weight, axis, axis=0, tiled=True)]
    pallas_call x2, Pallas kernels: 130 us -> 207 us  [the longest x1 123 us: run_backward(): pl.pallas_call(functools.partial(mix_backward, dims, steps, net_of), grid...]
    dot_general x2 -> x1, matrix products: 31 us -> 16 us  [local(): lax.dot_general(mixed, out_full, (((0,), (0,)), ((), ())), preferred_elem...]
  transfers between devices with their start and end apart: 2 -> 0, of which waited for: 2 -> 0; matrix products, arithmetic and copies ran while one was open for 0% -> 0% of each run, Pallas kernels for 0% -> 0%
where the time goes in v3:
time: 502 us
  Pallas kernels  447 us (89%)
  matrix products  28.5 us (6%)
  local copies, waits for them, and re-layouts  20.2 us (4%)
  other arithmetic  5.13 us (1%)
    pallas_call x1, Pallas kernels, run_reduce_in(): pl.pallas_call(functools.partial(reduce_in, axis, geom, K, E), grid=(K +...  128 us
    pallas_call x1, Pallas kernels, run_backward(): pl.pallas_call(functools.partial(mix_backward, dims, steps, net_of), grid...  123 us
    pallas_call x1, Pallas kernels, run_gather(): pl.pallas_call(functools.partial(gather_project, axis, geom, K), grid=(K...  112 us
    pallas_call x1, Pallas kernels, run_forward(): pl.pallas_call(functools.partial(mix_forward, dims, net_of), grid=(steps,...  84.2 us
    dot_general x1, matrix products, local(): lax.dot_general(mixed, out_full, (((0,), (0,)), ((), ())), preferred_elem...  16 us
    dot_general x1, matrix products, local(): lax.dot_general(go, out_full, (((1,), (1,)), ((), ())), preferred_element...  12.5 us

profile of v3, /device:TPU:0, one launch (start us, length us, event | category | flops | bytes accessed | tf_op | source)
XLA Modules:
  0.0 501.8 jit_solution(15867522348262634440)
XLA Ops:
  0.7 0.8 fusion.6
  1.5 0.8 copy.26
  2.3 1.2 concatenate.23
  3.5 0.9 pad_maximum_fusion.wl
  4.4 112.4 %gather_project.1 = (bf16[1024,6448]{1,0:T(8,128)(2,1)}, bf16[1536,6656]{1,0:T(8,128)(2,1)}, bf16[1536,1024]{1,0:T(8,128)(2,1)}, f32[8,1536]{1,0:T(8,128)}) custom-call(bf16[1024,1536]{1,0:T(8,128)(2,1)} %bitcast.61, bf16[13,48,512]{2,1,0:T(8,128)(2,1)} %pad_maximum_fusion.wl), custom_call_target="tpu_custom_call" | custom-call | flops 20283654144 | bytes 792330240 | tf_op jit(solution)/shard_map/gather_project/pallas_call | solution.py:896
  116.9 0.8 slice.93
  117.7 0.1 convert_element_type.38
  117.9 0.7 scatter.6
  118.6 0.7 fusion.8
  119.2 0.1 scatter.9.hpar
  119.3 0.9 slice.94
  120.2 0.1 reshape.139
  120.3 0.7 broadcast_in_dim.28
  121.3 1.0 copy-done.3
  122.2 84.2 %mix_forward.1 = (bf16[3072,1024]{1,0:T(8,128)(2,1)}, f32[1024,3072]{1,0:T(8,128)}, f32[1024,128]{1,0:T(8,128)S(1)}, bf16[4,4,2,96,1536]{4,3,2,1,0:T(8,128)(2,1)}) custom-call(bf16[1024,6448]{1,0:T(8,128)(2,1)} %get-tuple-element.50.proj, f32[8,3328]{1,0:T(8,128)S(1)} %pad_convert_fusion.cpar, f32[8,128]{1,0:T(8,128)S(1)} %scatter.9.hpar, ...), custom_call_target="tpu_custom_call" | custom-call | flops 1610612736 | bytes 32079872 | tf_op jit(solution)/shard_map/mix_forward/pallas_call | solution.py:749
  206.5 16.0 %add_convert_fusion = bf16[1024,1536]{1,0:T(8,128)(2,1)} fusion(bf16[1024,1536]{1,0:T(8,128)(2,1)S(1)} %bitcast.63, bf16[3072,1024]{1,0:T(8,128)(2,1)} %get-tuple-element.52, bf16[3072,1536]{1,0:T(8,128)(2,1)} %bitcast.59), kind=kOutput, calls=%fused_computation.1 | convolution fusion | flops 9668395008 | bytes 22020096 | tf_op jit(solution)/shard_map/dot_general | solution.py:1131
  222.5 12.5 %convolution_bitcast_fusion.dmixed = f32[1024,3072]{1,0:T(8,128)} fusion(bf16[3072,1536]{1,0:T(8,128)(2,1)S(1)} %bitcast.60, bf16[1024,1536]{1,0:T(8,128)(2,1)S(1)} %bitcast.47), kind=kOutput, calls=%fused_computation | convolution fusion | flops 9663676416 | bytes 25165824 | tf_op jit(solution)/shard_map/dot_general | solution.py:1127
  235.0 122.6 %mix_backward.1 = (bf16[1024,6656]{1,0:T(8,128)(2,1)}, f32[8,3328]{1,0:T(8,128)}, f32[96,1536]{1,0:T(8,128)}) custom-call(bf16[1024,6448]{1,0:T(8,128)(2,1)} %get-tuple-element.50.proj, f32[1024,3072]{1,0:T(8,128)} %convolution_bitcast_fusion.dmixed, f32[1024,3072]{1,0:T(8,128)} %get-tuple-element.55.ssd, f32[1024,128]{1,0:T(8,128)} %copy-done.2, ...), custom_call_target="tpu_custom_call" | custom-call | flops 3221225472 | bytes 51576832 | tf_op jit(solution)/shard_map/mix_backward/pallas_call | solution.py:806
  357.6 128.0 %reduce_in.1 = (f32[48,6448]{1,0:T(8,128)}, f32[48,128]{1,0:T(8,128)}, f32[1024,1536]{1,0:T(8,128)}, f32[8,3328]{1,0:T(8,128)}) custom-call(bf16[16,2,48,1024]{3,2,1,0:T(8,128)(2,1)} %bitcast.65, bf16[1024,6656]{1,0:T(8,128)(2,1)} %get-tuple-element.57.dproj, bf16[1536,6656]{1,0:T(8,128)(2,1)} %get-tuple-element.51.wfull, bf16[48,6448]{1,0:T(8,128)(2,1)} %wl.1, ...), custom_call_target="tpu_custom_call" | custom-call | flops 40567308288 | bytes 792330240 | tf_op jit(solution)/shard_map/reduce_in/pallas_call | solution.py:1025
  485.6 0.8 constant_dynamic-slice_fusion
  486.4 0.6 slice_bitcast_fusion
  487.0 0.5 slice_bitcast_fusion.2
  487.5 1.2 slice_bitcast_fusion.1
  488.7 0.8 reduce_sum.19
  489.5 1.2 bitcast_multiply_fusion
  490.7 0.9 slice_reduce_fusion
  491.7 0.6 reduce_sum.18
  492.4 0.9 slice.90
  493.3 0.6 dynamic-slice_bitcast_fusion
  493.9 6.1 %copy.44 = f32[2,4,128,1536]{3,2,1,0:T(8,128)} copy(f32[2,4,128,1536]{3,2,1,0:T(8,128)} %bitcast.43) | data formatting | bytes 12582912
  500.0 1.0 copy.45
  501.0 0.8 copy.46
  (33 shorter events, 0.6 us)
Async XLA Ops:
  117.9 88.5 %copy-start = (f32[8,3328]{1,0:T(8,128)}, f32[8,3328]{1,0:T(8,128)S(1)}, u32[]{:S(2)}) copy-start(f32[8,3328]{1,0:T(8,128)S(1)} %pad_convert_fusion.cpar) | copy-start | bytes 319492
  119.3 87.1 %copy-start.4 = (f32[8,128]{1,0:T(8,128)}, f32[8,128]{1,0:T(8,128)S(1)}, u32[]{:S(2)}) copy-start(f32[8,128]{1,0:T(8,128)S(1)} %scatter.9.hpar) | copy-start | bytes 12292
  121.3 1.0 copy-start.3
  122.2 84.2 %copy-start.1 = (f32[8,3072]{1,0:T(8,128)}, f32[8,3072]{1,0:T(8,128)S(1)}, u32[]{:S(2)}) copy-start(f32[8,3072]{1,0:T(8,128)S(1)} %maximum_maximum_fusion.dpar) | copy-start | bytes 294916
  122.2 84.2 %copy-start.9 = (bf16[2,4,128,1536]{3,2,1,0:T(8,128)(2,1)S(1)}, bf16[2,4,128,1536]{3,2,1,0:T(8,128)(2,1)}, u32[]{:S(2)}) copy-start(bf16[2,4,128,1536]{3,2,1,0:T(8,128)(2,1)} %param.15) | copy-start | bytes 9437188
  206.4 16.0 %copy-start.2 = (f32[1024,128]{1,0:T(8,128)}, f32[1024,128]{1,0:T(8,128)S(1)}, u32[]{:S(2)}) copy-start(f32[1024,128]{1,0:T(8,128)S(1)} %get-tuple-element.56.rstd) | copy-start | bytes 1572868
  206.5 16.0 %copy-start.5 = (bf16[2,4,128,1536]{3,2,1,0:T(8,128)(2,1)S(1)}, bf16[2,4,128,1536]{3,2,1,0:T(8,128)(2,1)}, u32[]{:S(2)}) copy-start(bf16[2,4,128,1536]{3,2,1,0:T(8,128)(2,1)} %param.25) | copy-start | bytes 9437188
  206.5 16.0 %copy-start.8 = (bf16[4,4,2,96,1536]{4,3,2,1,0:T(8,128)(2,1)S(1)}, bf16[4,4,2,96,1536]{4,3,2,1,0:T(8,128)(2,1)}, u32[]{:S(2)}) copy-start(bf16[4,4,2,96,1536]{4,3,2,1,0:T(8,128)(2,1)} %get-tuple-element.53) | copy-start | bytes 28311556
  493.9 6.1 %copy-start.6 = (f32[48,6448]{1,0:T(8,128)S(1)}, f32[48,6448]{1,0:T(8,128)}, u32[]{:S(2)}) copy-start(f32[48,6448]{1,0:T(8,128)} %get-tuple-element.80) | copy-start | bytes 3714052
  493.9 7.1 %copy-start.7 = (f32[96,1536]{1,0:T(8,128)S(1)}, f32[96,1536]{1,0:T(8,128)}, u32[]{:S(2)}) copy-start(f32[96,1536]{1,0:T(8,128)} %get-tuple-element.88) | copy-start | bytes 1769476

commit v4 on v3

--- a/solution.py
+++ b/solution.py
@@ -36,10 +36,16 @@
 
 
 def step_stage(dims, proj, hpar, dtp):
-    T, DI, C, H = dims["T"], dims["DI"], dims["C"], dims["H"]
+    DI, C, H = dims["DI"], dims["C"], dims["H"]
     dtp[...] = jnp.zeros_like(dtp)
     dtp[:, 0:H] = proj[:, DI + C : DI + C + H].astype(f32)
-    v = dtp[...] + hpar[0:1, :]
+    return steps_of(dims, dtp[...], hpar)
+
+
+def steps_of(dims, dt, hpar):
+    T, H = dims["T"], dims["H"]
+    _, lane = iotas(T, LANES)
+    v = jnp.where(lane < H, dt + hpar[0:1, :], 0.0)
     e = jnp.exp(-jnp.abs(v))
     step = jnp.maximum(v, 0.0) + jnp.log1p(e)
     row, col = iotas(T, T)
@@ -51,15 +57,19 @@
     return v, e, step, ld, ld - jnp.log2(step)
 
 
-def conv_tile(dims, proj, cpar, pad, c0):
-    T, DI, KW = dims["T"], dims["DI"], dims["KW"]
+def conv_of(dims, cin, cpar, pad, c0):
+    T, KW = dims["T"], dims["KW"]
     lanes = pl.ds(c0, LANES)
-    cin = proj[:, pl.ds(DI + c0, LANES)].astype(f32)
+    cin = cin.astype(f32)
     pad[FRONT : FRONT + T, :] = cin
     out = cpar[KW : KW + 1, lanes] + cin * cpar[KW - 1 : KW, lanes]
     for k in range(KW - 1):
         out = out + pad[FRONT - KW + 1 + k : FRONT - KW + 1 + k + T, :] * cpar[k : k + 1, lanes]
     return out
+
+
+def conv_tile(dims, proj, cpar, pad, c0):
+    return conv_of(dims, proj[:, pl.ds(dims["DI"] + c0, LANES)], cpar, pad, c0)
 
 
 def stack_heads(dims, v):
@@ -226,19 +236,18 @@
 
 
 class Reduce:
+    SLOTS = 3
+
     def __init__(self, at, K, refs):
         self.at, self.K = at, K
         (self.own0, self.own1, self.own2, self.own3, self.s0, self.s1, self.s2, self.s3,
-         self.r0, self.r1, self.r2, self.r3, self.ssem, self.rsem) = refs
-
-    @staticmethod
-    def sems(A0, A):
-        return 1 + (A - 1) + (A - 1) + (A0 - 1)
+         self.r0, self.r1, self.r2, self.r3, self.ssem, self.rsem, self.credit) = refs
 
     @staticmethod
     def scratch(K, A0, A, r, w):
         N = A0 * A * A
-        NS = Reduce.sems(A0, A)
+        NS = 1 + (A - 1) + (A - 1) + (A0 - 1)
+        L = Reduce.SLOTS
         return [
             pltpu.VMEM((2, N, r, w), f32),
             pltpu.VMEM((2, A0 * A, r, w), f32),
@@ -248,41 +257,39 @@
             pltpu.VMEM((2, A - 1, A0 * A, r, w), bf16),
             pltpu.VMEM((2, A - 1, A0, r, w), bf16),
             pltpu.VMEM((2, A0 - 1, r, w), bf16),
-            pltpu.VMEM((K, N, r, w), bf16),
-            pltpu.VMEM((K, A - 1, A0 * A, r, w), bf16),
-            pltpu.VMEM((K, A - 1, A0, r, w), bf16),
-            pltpu.VMEM((K, A0 - 1, r, w), bf16),
+            pltpu.VMEM((L, N, r, w), bf16),
+            pltpu.VMEM((L, A - 1, A0 * A, r, w), bf16),
+            pltpu.VMEM((L, A - 1, A0, r, w), bf16),
+            pltpu.VMEM((L, A0 - 1, r, w), bf16),
             pltpu.SemaphoreType.DMA((2, NS)),
-            pltpu.SemaphoreType.DMA((K, NS)),
+            pltpu.SemaphoreType.DMA((L, NS)),
+            pltpu.SemaphoreType.REGULAR((NS,)),
         ]
 
-    def copies(self, stage, j):
+    def routes(self, stage):
         at = self.at
         A0, A = at.A0, at.A
-        par = lax.rem(j, 2)
-
-        def make(k, src, dst, device):
-            return send(src, dst, self.ssem.at[par, k], self.rsem.at[j, k], device)
-
         if stage == 0:
-            return [make(0, self.s0.at[par], self.r0.at[j], at.partner())]
+            return [(0, at.partner(), at.partner())]
         if stage == 1:
-            return [
-                make(q, self.s1.at[par, q - 1], self.r1.at[j, q - 1],
-                     at.device(at.a0, at.f, at.second(q), at.c))
-                for q in range(1, A)
-            ]
+            to = lambda q: at.device(at.a0, at.f, at.second(q), at.c)
+            return [(q, to(q), to(-q)) for q in range(1, A)]
         if stage == 2:
-            return [
-                make(A - 1 + q, self.s2.at[par, q - 1], self.r2.at[j, q - 1],
-                     at.device(at.a0, at.first(q), at.s, at.c))
-                for q in range(1, A)
-            ]
-        return [
-            make(2 * (A - 1) + q, self.s3.at[par, q - 1], self.r3.at[j, q - 1],
-                 at.device(at.line(q), at.f, at.s, at.c))
-            for q in range(1, A0)
-        ]
+            to = lambda q: at.device(at.a0, at.first(q), at.s, at.c)
+            return [(A - 1 + q, to(q), to(-q)) for q in range(1, A)]
+        to = lambda q: at.device(at.line(q), at.f, at.s, at.c)
+        return [(2 * (A - 1) + q, to(q), to(-q)) for q in range(1, A0)]
+
+    def copies(self, stage, j):
+        par, slot = lax.rem(j, 2), lax.rem(j, self.SLOTS)
+        src, dst = ((self.s0, self.r0), (self.s1, self.r1), (self.s2, self.r2),
+                    (self.s3, self.r3))[stage]
+        out = []
+        for q, (k, to, _) in enumerate(self.routes(stage)):
+            a = src.at[par] if stage == 0 else src.at[par, q]
+            b = dst.at[slot] if stage == 0 else dst.at[slot, q]
+            out.append(send(a, b, self.ssem.at[par, k], self.rsem.at[slot, k], to))
+        return out
 
     def free(self, stage, j):
         @pl.when(j >= 2)
@@ -291,6 +298,11 @@
                 cp.wait_send()
 
     def start(self, stage, j):
+        @pl.when(j >= self.SLOTS)
+        def _():
+            for k, _, _ in self.routes(stage):
+                pl.semaphore_wait(self.credit.at[k], 1)
+
         for cp in self.copies(stage, j):
             cp.start()
 
@@ -298,30 +310,35 @@
         for cp in self.copies(stage, j):
             cp.wait_recv()
 
+    def done(self, stage, j):
+        @pl.when(j + self.SLOTS < self.K)
+        def _():
+            for k, _, source in self.routes(stage):
+                pl.semaphore_signal(
+                    self.credit.at[k], inc=1, device_id=source, device_id_type=MESH
+                )
+
     def begin(self, j, own, right):
         N, r, w = self.own0.shape[1:]
         par = lax.rem(j, 2)
+        rows = lambda k: own[k].reshape(N * r, own.shape[3])
         self.free(0, j)
         self.s0[par] = (
-            jnp.dot(own[1], right, preferred_element_type=f32).astype(bf16).reshape(N, r, w)
+            jnp.dot(rows(1), right, preferred_element_type=f32).astype(bf16).reshape(N, r, w)
         )
         self.start(0, j)
-        self.own0[par] = jnp.dot(own[0], right, preferred_element_type=f32).reshape(N, r, w)
+        self.own0[par] = jnp.dot(rows(0), right, preferred_element_type=f32).reshape(N, r, w)
 
     def step(self, i, finish):
         at = self.at
         A0, A = at.A0, at.A
 
-        def stage1(j):
-            par = lax.rem(j, 2)
-            self.arrive(0, j)
-            self.free(1, j)
-
+        def stage1(j, par, slot):
             def line(a, _):
                 for o in range(A):
                     for q in range(A):
                         b = a * A * A + at.pos(o, at.second(q))
-                        v = self.own0[par, b] + self.r0[j, b].astype(f32)
+                        v = self.own0[par, b] + self.r0[slot, b].astype(f32)
                         if q == 0:
                             self.own1[par, a * A + o] = v
                         else:
@@ -329,19 +346,14 @@
                 return 0
 
             lax.fori_loop(0, A0, line, 0)
-            self.start(1, j)
-
-        def stage2(j):
-            par = lax.rem(j, 2)
-            self.arrive(1, j)
-            self.free(2, j)
-
+
+        def stage2(j, par, slot):
             def line(a, _):
                 for q in range(A):
                     b = a * A + at.first(q)
                     v = self.own1[par, b]
                     for p in range(A - 1):
-                        v = v + self.r1[j, p, b].astype(f32)
+                        v = v + self.r1[slot, p, b].astype(f32)
                     if q == 0:
                         self.own2[par, a] = v
                     else:
@@ -349,36 +361,36 @@
                 return 0
 
             lax.fori_loop(0, A0, line, 0)
-            self.start(2, j)
-
-        def stage3(j):
-            par = lax.rem(j, 2)
-            self.arrive(2, j)
-            self.free(3, j)
+
+        def stage3(j, par, slot):
             for q in range(A0):
                 a = at.line(q)
                 v = self.own2[par, a]
                 for p in range(A - 1):
-                    v = v + self.r2[j, p, a].astype(f32)
+                    v = v + self.r2[slot, p, a].astype(f32)
                 if q == 0:
                     self.own3[par] = v
                 else:
                     self.s3[par, q - 1] = v.astype(bf16)
-            self.start(3, j)
-
-        def stage4(j):
-            self.arrive(3, j)
-            v = self.own3[lax.rem(j, 2)]
+
+        def stage4(j, par, slot):
+            v = self.own3[par]
             for p in range(A0 - 1):
-                v = v + self.r3[j, p].astype(f32)
+                v = v + self.r3[slot, p].astype(f32)
             finish(j, v)
 
         for k, stage in ((1, stage1), (2, stage2), (3, stage3), (4, stage4)):
             j = i - k
 
             @pl.when((j >= 0) & (j < self.K))
-            def _(j=j, stage=stage):
-                stage(j)
+            def _(j=j, k=k, stage=stage):
+                self.arrive(k - 1, j)
+                if k < 4:
+                    self.free(k, j)
+                stage(j, lax.rem(j, 2), lax.rem(j, self.SLOTS))
+                self.done(k - 1, j)
+                if k < 4:
+                    self.start(k, j)
 
     def drain(self):
         for j in range(max(0, self.K - 2), self.K):
@@ -445,22 +457,8 @@
         return total
 
 
-def mix_forward(dims, net_of, proj, cpar, hpar, dpar, *refs):
-    if net_of is None:
-        mixed, ssd, rstd, *refs = refs
-        between = lambda half: None
-    else:
-        wl, mixed, ssd, rstd, wfull, *refs = refs
-        net = net_of(wl, wfull, refs[8:])
-        i = pl.program_id(0)
-
-        @pl.when(i == 0)
-        def _():
-            net.at.barrier()
-
-        between = lambda half: net.step(2 * i + half)
-    pad, gated, colb, rowb, mask, scores, acc, dtp = refs[:8]
-    between(0)
+def mix_forward(dims, proj, cpar, hpar, dpar, mixed, ssd, rstd,
+                pad, gated, colb, rowb, mask, scores, acc, dtp):
     T, DI, H, HD, ST = dims["T"], dims["DI"], dims["H"], dims["HD"], dims["ST"]
     HP = LANES // HD
     tiles = DI // LANES
@@ -507,59 +505,22 @@
         acc[...] += total
         return 0
 
-    trips = tiles // UNROLL_F
-    lax.fori_loop(0, trips // 2, body, 0)
-    between(1)
-    lax.fori_loop(trips // 2, trips, body, 0)
+    lax.fori_loop(0, tiles // UNROLL_F, body, 0)
     r = lax.rsqrt(jnp.sum(acc[...], axis=1, keepdims=True) * (1.0 / DI) + epsilon)
     rb = jnp.broadcast_to(r, (T, LANES))
     rstd[...] = rb
 
     def finish(j, _):
         lanes = pl.ds(pl.multiple_of(j * LANES, LANES), LANES)
-        mixed[lanes, :] = (gated[:, lanes] * rb * dpar[1:2, lanes]).T.astype(bf16)
+        mixed[:, lanes] = (gated[:, lanes] * rb * dpar[1:2, lanes]).astype(bf16)
         return 0
 
     lax.fori_loop(0, tiles, finish, 0)
-    if net_of is not None:
-
-        @pl.when(i == pl.num_programs(0) - 1)
-        def _():
-            net.drain()
-
-
-def mix_backward(dims, steps, net_of, proj, dmixed, ssd, rstd, cpar, hpar, dpar, *refs):
-    if net_of is None:
-        dproj, small, *refs = refs
-        between = lambda half: None
-    else:
-        mT, go, dproj, small, dow, *refs = refs
-        net, own = net_of(refs[15:])
-        N, _, r, R = mT.shape
-        w = net.own3.shape[2]
-        i = pl.program_id(0)
-
-        @pl.when(i == 0)
-        def _():
-            net.at.barrier()
-            own[0] = mT[:, net.at.c].reshape(N * r, R)
-            own[1] = mT[:, 1 - net.at.c].reshape(N * r, R)
-
-        def finish(j, v):
-            dow[:, columns(j, w)] = v
-
-        def between(half):
-            k = 2 * i + half
-
-            @pl.when(k < net.K)
-            def _():
-                net.begin(k, own, go[:, columns(k, w)])
-
-            net.step(k, finish)
-
-    (cacc, dacc, hacc, pad, dpad, colb, rowb, mask, scores, acc, dtp, dscores, dlog, csum,
-     bcs) = refs[:15]
-    between(0)
+
+
+def mix_backward(dims, steps, proj, dmixed, ssd, rstd, cpar, hpar, dpar, dproj, small,
+                 cacc, dacc, hacc, pad, dpad, colb, rowb, mask, scores, acc, dtp, dscores, dlog,
+                 csum, bcs):
     T, DI, C, H, HD, ST, KW = (dims[k] for k in ("T", "DI", "C", "H", "HD", "ST", "KW"))
     HP = LANES // HD
     tiles = DI // LANES
@@ -672,10 +633,7 @@
         csum[...] += sums[2]
         return 0
 
-    trips = tiles // UNROLL_B
-    lax.fori_loop(0, trips // 2, body, 0)
-    between(1)
-    lax.fori_loop(trips // 2, trips, body, 0)
+    lax.fori_loop(0, tiles // UNROLL_B, body, 0)
     ds = dscores[...].astype(bf16)
     dst = dscores[...].T.astype(bf16)
     dact = (
@@ -702,12 +660,6 @@
     hacc[0:8, :] += sum8(ddt)
     hacc[8:16, :] += sum8(dsteps * step)
 
-    if net_of is not None:
-
-        @pl.when(i == steps - 1)
-        def _():
-            net.drain()
-
     @pl.when(pl.program_id(0) == steps - 1)
     def _():
         small[...] = jnp.zeros_like(small)
@@ -722,41 +674,21 @@
             )
 
 
-def run_forward(dims, axis, geom, proj, cpar, hpar, dpar, ow):
+def run_forward(dims, proj, cpar, hpar, dpar):
     T, DI, C, H, KW = dims["T"], dims["DI"], dims["C"], dims["H"], dims["KW"]
     R, E = proj.shape
-    steps = R // T
     rows = lambda w: pl.BlockSpec((T, w), lambda i: (i, 0))
     whole = lambda a: pl.BlockSpec(a.shape, lambda i: (0, 0))
-    args, net_of, outs, shapes, sems, extra = [], None, [], [], [], {}
-    if geom is not None:
-        A0, A = geom
-        r, D = ow.shape
-        w = D // (2 * steps - 4)
-        K = D // w
-
-        def net_of(wl, wfull, sems):
-            return Gather(
-                Place(axis, A0, A), K, lambda j: wl.at[:, columns(j, w)],
-                lambda j, a, p, c: wfull.at[a, p, c, :, columns(j, w)], *sems,
-            )
-
-        args = [ow]
-        outs = [pl.BlockSpec(memory_space=pl.ANY)]
-        shapes = [jax.ShapeDtypeStruct((A0, A * A, 2, r, D), bf16)]
-        sems = Gather.scratch(K, A0, A)
-        extra = dict(collective_id=3, has_side_effects=True)
     return pl.pallas_call(
-        functools.partial(mix_forward, dims, net_of),
-        grid=(steps,),
-        in_specs=[rows(E), whole(cpar), whole(hpar), whole(dpar)] + [whole(a) for a in args],
-        out_specs=[pl.BlockSpec((DI, T), lambda i: (0, i)), rows(DI), rows(LANES)] + outs,
+        functools.partial(mix_forward, dims),
+        grid=(R // T,),
+        in_specs=[rows(E), whole(cpar), whole(hpar), whole(dpar)],
+        out_specs=[rows(DI), rows(DI), rows(LANES)],
         out_shape=[
-            jax.ShapeDtypeStruct((DI, R), bf16),
+            jax.ShapeDtypeStruct((R, DI), bf16),
             jax.ShapeDtypeStruct((R, DI), f32),
             jax.ShapeDtypeStruct((R, LANES), f32),
-        ]
-        + shapes,
+        ],
         scratch_shapes=[
             pltpu.VMEM((max(2, UNROLL_F), FRONT + T, LANES), f32),
             pltpu.VMEM((T, DI), f32),
@@ -766,54 +698,25 @@
             pltpu.VMEM((T, T), f32),
             pltpu.VMEM((T, LANES), f32),
             pltpu.VMEM((T, LANES), f32),
-        ]
-        + sems,
-        compiler_params=pltpu.CompilerParams(vmem_limit_bytes=48 << 20, **extra),
-        cost_estimate=pl.CostEstimate(
-            flops=4 * R * DI * T, bytes_accessed=R * (2 * E + 6 * DI), transcendentals=R * H * T
-        ),
+        ],
+        compiler_params=pltpu.CompilerParams(vmem_limit_bytes=48 << 20),
         name="mix_forward",
-    )(proj, cpar, hpar, dpar, *args)
-
-
-def run_backward(dims, axis, geom, EP, proj, dmixed, ssd, rstd, cpar, hpar, dpar, mixed, go):
+    )(proj, cpar, hpar, dpar)
+
+
+def run_backward(dims, proj, dmixed, ssd, rstd, cpar, hpar, dpar):
     T, DI, C, H, KW, ST = (dims[k] for k in ("T", "DI", "C", "H", "KW", "ST"))
     R, E = proj.shape
-    steps = R // T
     rows = lambda w: pl.BlockSpec((T, w), lambda i: (i, 0))
-    whole = lambda s: pl.BlockSpec(s, lambda i: (0,) * len(s))
-    once = lambda s: pl.BlockSpec(s, lambda i: (0,) * len(s), pipeline_mode=pl.Buffered(1))
-    assert KW + 4 <= 8
+    whole = lambda s: pl.BlockSpec(s, lambda i: (0, 0))
     sums = [(8 * (KW + 1), C), (16, DI), (16, LANES)]
-    args, net_of, ins, outs, shapes, scratch, extra = [], None, [], [], [], [], {}
-    if geom is not None:
-        A0, A = geom
-        N = A0 * A * A
-        r, D = DI // (2 * N), go.shape[1]
-        w = 2 * LANES
-        K = D // w
-        assert K + 4 <= 2 * steps
-
-        def net_of(refs):
-            return Reduce(Place(axis, A0, A), K, refs[1:15]), refs[0]
-
-        args = [mixed.reshape(N, 2, r, R), go]
-        ins = [once((N, 2, r, R)), once((R, D))]
-        outs = [once((r, D))]
-        shapes = [jax.ShapeDtypeStruct((r, D), f32)]
-        scratch = [pltpu.VMEM((2, N * r, R), bf16)] + Reduce.scratch(K, A0, A, r, w)
-        extra = dict(collective_id=4, has_side_effects=True)
     return pl.pallas_call(
-        functools.partial(mix_backward, dims, steps, net_of),
-        grid=(steps,),
+        functools.partial(mix_backward, dims, R // T),
+        grid=(R // T,),
         in_specs=[rows(E), rows(DI), rows(DI), rows(LANES)]
-        + [whole(a.shape) for a in (cpar, hpar, dpar)] + ins,
-        out_specs=[rows(EP), whole((8, C))] + outs,
-        out_shape=[
-            jax.ShapeDtypeStruct((R, EP), bf16),
-            jax.ShapeDtypeStruct((8, C), f32),
-        ]
-        + shapes,
+        + [whole(a.shape) for a in (cpar, hpar, dpar)],
+        out_specs=[rows(E), whole((8, C))],
+        out_shape=[jax.ShapeDtypeStruct((R, E), bf16), jax.ShapeDtypeStruct((8, C), f32)],
         scratch_shapes=[pltpu.VMEM(s, f32) for s in sums]
         + [
             pltpu.VMEM((max(2, UNROLL_B), FRONT + T, LANES), f32),
@@ -828,236 +731,646 @@
             pltpu.VMEM((T, LANES), f32),
             pltpu.VMEM((T, LANES), f32),
             pltpu.VMEM((2, T, ST), bf16),
-        ]
-        + scratch,
-        compiler_params=pltpu.CompilerParams(vmem_limit_bytes=VMEM, **extra),
-        cost_estimate=pl.CostEstimate(
-            flops=8 * R * DI * T, bytes_accessed=R * (4 * E + 8 * DI), transcendentals=R * H * T
-        ),
+        ],
+        compiler_params=pltpu.CompilerParams(vmem_limit_bytes=56 << 20),
         name="mix_backward",
-    )(proj, dmixed, ssd, rstd, cpar, hpar, dpar, *args)
-
-
-def gather_project(axis, geom, K, tok, wl, proj, wfull, uT, scale, buf, uh, *sems):
+    )(proj, dmixed, ssd, rstd, cpar, hpar, dpar)
+
+
+def assemble(parts, size, tiles):
+    _, lane = iotas(8, LANES)
+    out = []
+    for t in range(tiles):
+        total = None
+        for d in range(t * LANES // size, min(len(parts), -(-(t + 1) * LANES // size))):
+            shift = d * size - t * LANES
+            v = parts[d] if shift % LANES == 0 else pltpu.roll(parts[d], shift % LANES, 1)
+            keep = (lane >= max(shift, 0)) & (lane < min(shift + size, LANES))
+            v = jnp.where(keep, v, 0.0)
+            total = v if total is None else total + v
+        out.append(total)
+    return out
+
+
+def forward(dims, axis, geom, K, KO, tok, wl, ow, hpar, skip, tokc, goc,
+            proj, ssd, uT, mT, out, tabs, pars, scale, wfull, ofull,
+            uh, wv, wo, pj, gated, mixed, pad, ldtab, rowtab, scores, mask, acc, dtp, wsem, osem,
+            *sems):
+    T, DI, C, H, HD, ST, KW = (dims[k] for k in ("T", "DI", "C", "H", "HD", "ST", "KW"))
     A0, A = geom
     at = Place(axis, A0, A)
     i = pl.program_id(0)
     R, D = tok.shape
     w = wl.shape[2]
+    half = w // 2
+    S = R // T
+    HP = LANES // HD
+    TC = half // LANES
+    wo_cols = wo.shape[5]
+    net = Gather(at, K, lambda j: wl.at[j], lambda j, a, p, c: wfull.at[j, a, p, c], *sems[:3])
+    neto = Gather(
+        at, KO, lambda j: ow.at[:, columns(j, wo_cols)],
+        lambda j, a, p, c: ofull.at[a, p, c, :, columns(j, wo_cols)], *sems[3:],
+    )
 
     @pl.when(i == 0)
     def _():
         at.barrier()
 
-    net = Gather(at, K, lambda j: wl.at[j], lambda j, a, p, c: buf.at[j, a, p, c], *sems)
     net.step(i)
+    neto.step(i - K)
+
+    def fetch_w(j):
+        slot = lax.rem(j, 2)
+        return pltpu.make_async_copy(wfull.at[j], wv.at[slot], wsem.at[slot])
+
+    def fetch_o(k):
+        slot = lax.rem(k, 2)
+        return pltpu.make_async_copy(
+            ofull.at[:, :, :, :, columns(k, wo_cols)], wo.at[slot], osem.at[slot]
+        )
+
+    @pl.when((i >= 4) & (i < K + 4))
+    def _():
+        fetch_w(i - 4).start()
+
+    @pl.when((i >= K + 4) & (i < K + KO + 4))
+    def _():
+        fetch_o(i - K - 4).start()
+
+    @pl.when(i == 5)
+    def _():
+        row, col = iotas(T, T)
+        mask[...] = jnp.where(col <= row, BIG, -BIG)
+        pad[:, 0:FRONT, :] = jnp.zeros((pad.shape[0], FRONT, LANES), f32)
+        acc[...] = jnp.zeros_like(acc)
+
+        def seq(s, _):
+            rows = pl.ds(pl.multiple_of(s * T, T), T)
+            bc = []
+            for a in range(2):
+                conv = conv_of(dims, pj[0, rows, a * LANES : (a + 1) * LANES], pars, pad.at[a],
+                               DI + a * ST)
+                bc.append((conv * sigmoid(conv)).astype(bf16))
+            scores[s] = lax.dot_general(
+                bc[1], bc[0], (((1,), (1,)), ((), ())), preferred_element_type=f32
+            )
+            _, _, _, ld, ld2 = steps_of(
+                dims, pj[0, rows, 2 * LANES : 3 * LANES].astype(f32), hpar
+            )
+            ldtab[s] = ld
+            rowtab[s] = ld2.T
+            return 0
+
+        lax.fori_loop(0, S, seq, 0)
+
+    @pl.when((i >= 6) & (i < K + 5))
+    def _():
+        j = i - 5
+        slot = lax.rem(j, 2)
+        h0 = (j - 1) * TC * HP
+
+        def seq(s, _):
+            rows = pl.ds(pl.multiple_of(s * T, T), T)
+            turned = pltpu.roll(ldtab[s], LANES - h0, 1)
+            total = None
+            for u in range(TC):
+                c0 = pl.multiple_of((j - 1) * half + u * LANES, LANES)
+                conv = conv_of(
+                    dims, pj[slot, rows, half + u * LANES : half + (u + 1) * LANES], pars,
+                    pad.at[u], c0,
+                )
+                x = (conv * sigmoid(conv)).astype(bf16)
+                mix = []
+                for a in range(HP):
+                    k = u * HP + a
+                    left = jnp.broadcast_to(turned[:, k : k + 1], (T, T))
+                    expo = jnp.minimum(left - rowtab[s, pl.ds(h0 + k, 1), :], mask[...])
+                    mix.append((jnp.exp2(expo) * scores[s]).astype(bf16))
+                core = jnp.dot(
+                    jnp.concatenate(mix, axis=1), stack_heads(dims, x),
+                    preferred_element_type=f32,
+                )
+                o = core + skip[0:1, pl.ds(c0, LANES)] * x.astype(f32)
+                ssd[rows, u * LANES : (u + 1) * LANES] = o
+                gate = pj[slot, rows, u * LANES : (u + 1) * LANES].astype(f32)
+                g = o * (gate * sigmoid(gate))
+                gated[rows, pl.ds(c0, LANES)] = g
+                total = g * g if total is None else total + g * g
+            acc[rows, :] += total
+            return 0
+
+        lax.fori_loop(0, S, seq, 0)
+
+    @pl.when((i >= 4) & (i < K + 4))
+    def _():
+        fetch_w(i - 4).wait()
 
     @pl.when(i == 4)
     def _():
-        last = buf[0].reshape(D, w)[:, w - LANES :].astype(f32).T
-        scale[...] = jnp.broadcast_to(last[LANES - 1 :, :], scale.shape)
+        N = A0 * A * A * 2
+        r = D // N
+        Cn, Gn = C // N, DI // N
+        last = wv[0].reshape(D, w)[:, w - LANES :].astype(f32)
+        turned = last.T
+        scale[...] = jnp.broadcast_to(turned[LANES - 1 :, :], scale.shape)
+        parts = [last[d * r : d * r + 8, :] for d in range(N)]
+        for t, v in enumerate(assemble(parts, Cn, C // LANES)):
+            pars[0:8, t * LANES : (t + 1) * LANES] = v
+        for t, v in enumerate(assemble(parts, Gn, DI // LANES)):
+            pars[8:16, t * LANES : (t + 1) * LANES] = v
 
         def norm(k, _):
             rows = pl.ds(pl.multiple_of(k * LANES, LANES), LANES)
             u = tok[rows, :].astype(f32)
-            r = lax.rsqrt(jnp.mean(u * u, axis=-1, keepdims=True) + epsilon)
-            v = u * r * scale[0:1, :]
+            rs = lax.rsqrt(jnp.mean(u * u, axis=-1, keepdims=True) + epsilon)
+            v = u * rs * scale[0:1, :]
             uh[rows, :] = v.astype(bf16)
             uT[:, rows] = v.T.astype(bf16)
             return 0
 
         lax.fori_loop(0, R // LANES, norm, 0)
 
-    @pl.when(i >= 4)
-    def _():
-        wfull[...] = buf[i - 4].reshape(D, w)
+    @pl.when((i >= 4) & (i < K + 4))
+    def _():
+        slot = lax.rem(i, 2)
         M = 256
 
         def rows(k, _):
             at_ = pl.ds(pl.multiple_of(k * M, M), M)
-            proj[at_, :] = jnp.dot(
-                uh[at_, :], wfull[...], preferred_element_type=f32
+            v = jnp.dot(
+                uh[at_, :], wv[slot].reshape(D, w), preferred_element_type=f32
             ).astype(bf16)
+            pj[slot, at_, :] = v
+            proj[0, at_, :] = v
             return 0
 
         lax.fori_loop(0, R // M, rows, 0)
 
-    @pl.when(i == K + 3)
+    @pl.when(i == K + 5)
+    def _():
+        def seq(s, _):
+            rows = pl.ds(pl.multiple_of(s * T, T), T)
+            rs = lax.rsqrt(jnp.sum(acc[rows, :], axis=1, keepdims=True) * (1.0 / DI) + epsilon)
+            rb = jnp.broadcast_to(rs, (T, LANES))
+            tabs[0, rows, :] = rb
+
+            def tile(k, _):
+                for u in range(4):
+                    lanes = pl.ds(pl.multiple_of((k * 4 + u) * LANES, LANES), LANES)
+                    v = gated[rows, lanes] * rb * pars[8 + KW + 1 : 8 + KW + 2, lanes]
+                    mixed[rows, lanes] = v.astype(bf16)
+                    mT[lanes, rows] = v.T.astype(bf16)
+                return 0
+
+            lax.fori_loop(0, DI // LANES // 4, tile, 0)
+            return 0
+
+        lax.fori_loop(0, S, seq, 0)
+        acc[...] = jnp.zeros_like(acc)
+
+    @pl.when(i >= K + 5)
+    def _():
+        k = i - K - 5
+        slot = lax.rem(k, 2)
+        fetch_o(k).wait()
+        M = 256
+
+        def rows(m, _):
+            at_ = pl.ds(pl.multiple_of(m * M, M), M)
+            branch = jnp.dot(
+                mixed[at_, :], wo[slot].reshape(DI, wo_cols), preferred_element_type=f32
+            )
+            out[at_, :] = (tokc[at_, :].astype(f32) + branch).astype(bf16)
+            p = branch * goc[at_, :].astype(f32)
+            part = p[:, 0:LANES]
+            for q in range(1, wo_cols // LANES):
+                part = part + p[:, q * LANES : (q + 1) * LANES]
+            acc[at_, :] += part
+            return 0
+
+        lax.fori_loop(0, R // M, rows, 0)
+
+    @pl.when(i == K + KO + 4)
     def _():
         net.drain()
-
-
-def run_gather(axis, geom, tok, wl, E):
+        neto.drain()
+        mu = jnp.sum(acc[...], axis=1, keepdims=True) * (1.0 / DI)
+        rb = tabs[0]
+        tabs[1] = jnp.broadcast_to(mu, rb.shape) * rb * rb
+
+
+def run_forward_net(dims, axis, geom, tok, go, wl, ow, hpar, skip):
+    T, DI, C, H = (dims[k] for k in ("T", "DI", "C", "H"))
     A0, A = geom
     R, D = tok.shape
     K, r, w = wl.shape
-    late = lambda i: (0, lax.rem(jnp.maximum(i - 4, 0) + K - 1, K))
-    once = dict(pipeline_mode=pl.Buffered(1))
+    ro = ow.shape[0]
+    half = w // 2
+    wc = r * w // ro
+    KO = D // wc
+    S = R // T
+    steps = K + KO + 5
+    whole = lambda s: pl.BlockSpec(s, lambda i: (0,) * len(s), pipeline_mode=pl.Buffered(1))
+    late = lambda i: (0, jnp.clip(i - K - 5, 0, KO - 1))
+    hbm = pl.BlockSpec(memory_space=pl.ANY)
     return pl.pallas_call(
-        functools.partial(gather_project, axis, geom, K),
-        grid=(K + 4,),
-        in_specs=[
-            pl.BlockSpec((R, D), lambda i: (0, 0), **once),
-            pl.BlockSpec((K, r, w), lambda i: (0, 0, 0), **once),
-        ],
+        functools.partial(forward, dims, axis, geom, K, KO),
+        grid=(steps,),
+        in_specs=[whole((R, D)), whole((K, r, w)), whole((ro, D)), whole((8, LANES)),
+                  whole((8, DI)), pl.BlockSpec((R, wc), late), pl.BlockSpec((R, wc), late)],
         out_specs=[
-            pl.BlockSpec((R, w), late),
-            pl.BlockSpec((D, w), late),
-            pl.BlockSpec((D, R), lambda i: (0, 0), **once),
-            pl.BlockSpec((8, D), lambda i: (0, 0), **once),
+            pl.BlockSpec((1, R, w), lambda i: (jnp.clip(i - 4, 0, K - 1), 0, 0)),
+            pl.BlockSpec((R, half), lambda i: (0, jnp.clip(i - 6, 0, K - 2))),
+            whole((D, R)), whole((DI, R)),
+            pl.BlockSpec((R, wc), late),
+            whole((2, R, LANES)), whole((16, C)), whole((8, D)), hbm, hbm,
         ],
         out_shape=[
-            jax.ShapeDtypeStruct((R, E), bf16),
-            jax.ShapeDtypeStruct((D, K * w), bf16),
+            jax.ShapeDtypeStruct((K, R, w), bf16),
+            jax.ShapeDtypeStruct((R, DI), f32),
             jax.ShapeDtypeStruct((D, R), bf16),
+            jax.ShapeDtypeStruct((DI, R), bf16),
+            jax.ShapeDtypeStruct((R, D), bf16),
+            jax.ShapeDtypeStruct((2, R, LANES), f32),
+            jax.ShapeDtypeStruct((16, C), f32),
             jax.ShapeDtypeStruct((8, D), f32),
+            jax.ShapeDtypeStruct((K, A0, A * A, 2, r, w), bf16),
+            jax.ShapeDtypeStruct((A0, A * A, 2, ro, D), bf16),
         ],
         scratch_shapes=[
-            pltpu.VMEM((K, A0, A * A, 2, r, w), bf16),
             pltpu.VMEM((R, D), bf16),
+            pltpu.VMEM((2, A0, A * A, 2, r, w), bf16),
+            pltpu.VMEM((2, A0, A * A, 2, ro, wc), bf16),
+            pltpu.VMEM((2, R, w), bf16),
+            pltpu.VMEM((R, DI), f32),
+            pltpu.VMEM((R, DI), bf16),
+            pltpu.VMEM((half // LANES, FRONT + T, LANES), f32),
+            pltpu.VMEM((S, T, LANES), f32),
+            pltpu.VMEM((S, LANES, T), f32),
+            pltpu.VMEM((S, T, T), f32),
+            pltpu.VMEM((T, T), f32),
+            pltpu.VMEM((R, LANES), f32),
+            pltpu.VMEM((T, LANES), f32),
+            pltpu.SemaphoreType.DMA((2,)),
+            pltpu.SemaphoreType.DMA((2,)),
         ]
-        + Gather.scratch(K, A0, A),
+        + Gather.scratch(K, A0, A) + Gather.scratch(KO, A0, A),
         compiler_params=pltpu.CompilerParams(
             collective_id=1, has_side_effects=True, vmem_limit_bytes=VMEM
         ),
         cost_estimate=pl.CostEstimate(
-            flops=2 * R * D * E, bytes_accessed=2 * D * E * 40, transcendentals=0
+            flops=2 * R * D * K * w, bytes_accessed=D * K * w * 60, transcendentals=0
         ),
-        name="gather_project",
-    )(tok, wl)
-
-
-def reduce_in(axis, geom, K, E, uT, dproj, wfull, wl, scale, tok, go, small,
-              dw, dns, dtok, sums, own, *refs):
+        name="forward",
+    )(tok, wl, ow, hpar, skip, tok, go)
+
+
+def backward(dims, axis, geom, K, KO, E, proj, proj0, ssd, wo, wf, uT, mT, go, wl, tabs, pars,
+             skip, hpar, dn, outc, dns, sums,
+             uo, mo, dmx, dpj, pad, dpad, ldtab, rowtab, scores, dscores, dlog, csum, bcs, mask,
+             cacc, dacc, hacc, small, csem, *refs):
+    T, DI, C, H, HD, ST, KW = (dims[k] for k in ("T", "DI", "C", "H", "HD", "ST", "KW"))
     A0, A = geom
     at = Place(axis, A0, A)
     i = pl.program_id(0)
-    R, D = tok.shape
-    N, _, r, _ = uT.shape
-    w = dproj.shape[1]
-    net = Reduce(at, K, refs[:14])
-    total = SumAll(at, refs[14:18])
+    R = ssd.shape[0]
+    _, r, w = wl.shape
+    N = A0 * A * A
+    half = w // 2
+    S = R // T
+    HP = LANES // HD
+    TC = half // LANES
+    D = go.shape[1]
+    HF = mo.shape[0]
+    slots = dpj.shape[0]
+    net = Reduce(at, K + KO, refs[:15])
+    total = SumAll(at, refs[15:])
+
+    def fetches():
+        out = [(uT.at[:, at.c], uo.at[0]), (uT.at[:, 1 - at.c], uo.at[1])]
+        for h in range(HF):
+            out += [(mT.at[:, at.c, h], mo.at[h, 0]), (mT.at[:, 1 - at.c, h], mo.at[h, 1])]
+        return [pltpu.make_async_copy(s, d, csem.at[k]) for k, (s, d) in enumerate(out)]
 
     @pl.when(i == 0)
     def _():
+        for cp in fetches():
+            cp.start()
         at.barrier()
+        for ref in (cacc, dacc, hacc, dlog, csum, dscores, dns):
+            ref[...] = jnp.zeros_like(ref)
+        row, col = iotas(T, T)
+        mask[...] = jnp.where(row <= col, BIG, -BIG)
+        pad[:, 0:FRONT, :] = jnp.zeros((pad.shape[0], FRONT, LANES), f32)
+        dpad[:, T:, :] = jnp.zeros((dpad.shape[0], FRONT, LANES), f32)
+
+        def seq(s, _):
+            rows = pl.ds(pl.multiple_of(s * T, T), T)
+            for a in range(2):
+                conv = conv_of(dims, proj0[0, rows, a * LANES : (a + 1) * LANES], pars, pad.at[a],
+                               DI + a * ST)
+                bcs[a, rows, :] = (conv * sigmoid(conv)).astype(bf16)
+            scores[s] = lax.dot_general(
+                bcs[0, rows, :], bcs[1, rows, :], (((1,), (1,)), ((), ())),
+                preferred_element_type=f32,
+            )
+            _, _, _, ld, ld2 = steps_of(
+                dims, proj0[0, rows, 2 * LANES : 3 * LANES].astype(f32), hpar
+            )
+            ldtab[s] = ld2
+            rowtab[s] = ld.T
+            return 0
+
+        lax.fori_loop(0, S, seq, 0)
+        for cp in fetches():
+            cp.wait()
+
+    def finish(p, v):
+        inner = (p >= 2 * KO) | (lax.rem(p, 2) == 1)
+
+        @pl.when(inner)
+        def _():
+            g = jnp.where(p >= 2 * KO, p - KO, lax.div(p, 2))
+            outc[g] = v
+            q = v * wl[lax.rem(g + 1, K)].astype(f32)
+            part = q[:, 0:LANES]
+            for k in range(1, w // LANES):
+                part = part + q[:, k * LANES : (k + 1) * LANES]
+            dns[...] += part
+
+        @pl.when(jnp.logical_not(inner))
+        def _():
+            outc[K + lax.div(p, 2)] = v
+
+    @pl.when(i < KO)
+    def _():
+        h = lax.div(i, KO // HF)
+        net.begin(2 * i, mo.at[h], go[:, columns(lax.rem(i, KO // HF), w)])
+        net.step(2 * i, finish)
+
+    def conv_back(slot, rows, lane0, c0, dact, conv, sig, u):
+        lanes = pl.ds(c0, LANES)
+        dconv = dact * (sig * (1.0 + conv * (1.0 - sig)))
+        dpad[u, 0:T, :] = dconv
+        dcin = dconv * pars[KW - 1 : KW, lanes]
+        for k in range(KW - 1):
+            dcin = dcin + dpad[u, KW - 1 - k : KW - 1 - k + T, :] * pars[k : k + 1, lanes]
+        dpj[slot, rows, lane0 : lane0 + LANES] = dcin.astype(bf16)
+        for k in range(KW):
+            start = FRONT - KW + 1 + k
+            cacc[8 * k : 8 * k + 8, lanes] += sum8(dconv * pad[u, start : start + T, :])
+        cacc[8 * KW : 8 * KW + 8, lanes] += sum8(dconv)
+
+    @pl.when(i < K - 1)
+    def _():
+        slot = lax.rem(i, slots)
+        h0 = i * TC * HP
+        M = 256
+
+        def rows_of(m, _):
+            at_ = pl.ds(pl.multiple_of(m * M, M), M)
+            dmx[at_, :] = lax.dot_general(
+                go[at_, :], wo[...], (((1,), (1,)), ((), ())), preferred_element_type=f32
+            )
+            return 0
+
+        lax.fori_loop(0, R // M, rows_of, 0)
+
+        def seq(s, _):
+            rows = pl.ds(pl.multiple_of(s * T, T), T)
+            turned = pltpu.roll(ldtab[s], LANES - h0, 1)
+            rb, mb = tabs[0, rows, :], tabs[1, rows, :]
+            parts = None
+            for u in range(TC):
+                c0 = pl.multiple_of(i * half + u * LANES, LANES)
+                lanes = pl.ds(c0, LANES)
+                here = slice(u * LANES, (u + 1) * LANES)
+                there = slice(half + u * LANES, half + (u + 1) * LANES)
+                conv = conv_of(dims, proj[0, rows, there], pars, pad.at[u], c0)
+                sig = sigmoid(conv)
+                x = (conv * sig).astype(bf16)
+                xf = x.astype(f32)
+                gate = proj[0, rows, here].astype(f32)
+                gs = sigmoid(gate)
+                act = gate * gs
+                o = ssd[rows, here]
+                dm = dmx[rows, here]
+                gated = o * act
+                dgated = rb * (dm * pars[8 + KW + 1 : 8 + KW + 2, lanes]) - gated * mb
+                dacc[8:16, lanes] += sum8(dm * (gated * rb))
+                dssd = dgated * act
+                dpj[slot, rows, here] = (
+                    dgated * o * (gs * (1.0 + gate * (1.0 - gs)))
+                ).astype(bf16)
+                low = dssd.astype(bf16)
+                dacc[0:8, lanes] += sum8(dssd * xf)
+                lows = stack_heads(dims, low)
+                dmix = lax.dot_general(
+                    x, lows, (((1,), (1,)), ((), ())), preferred_element_type=f32
+                )
+                mix = []
+                part = None
+                for a in range(HP):
+                    k = u * HP + a
+                    right = jnp.broadcast_to(turned[:, k : k + 1], (T, T))
+                    decay = jnp.exp2(
+                        jnp.minimum(rowtab[s, pl.ds(h0 + k, 1), :] - right, mask[...])
+                    )
+                    mix.append((decay * scores[s]).astype(bf16))
+                    term = dmix[:, a * T : (a + 1) * T] * decay
+                    part = term if part is None else part + term
+                core = jnp.dot(
+                    jnp.concatenate(mix, axis=1), lows, preferred_element_type=f32
+                )
+                sk = skip[0:1, lanes]
+                from_cols = xf * core
+                diff = low.astype(f32) * (o - sk * xf) - from_cols
+                prow, pcol = iotas(LANES, LANES)
+                place = (pcol == h0 + u * HP + prow // HD).astype(bf16)
+                both = jnp.concatenate([diff, from_cols], axis=0)
+                hi = both.astype(bf16)
+                lo = (both - hi.astype(f32)).astype(bf16)
+                by_head = jnp.dot(
+                    jnp.concatenate([hi, lo], axis=1),
+                    jnp.concatenate([place, place], axis=0), preferred_element_type=f32,
+                )
+                conv_back(slot, rows, half + u * LANES, c0, core + sk * dssd, conv, sig, u)
+                new = (part, by_head)
+                parts = new if parts is None else tuple(p + q for p, q in zip(parts, new))
+            dscores[s] += parts[0]
+            dlog[rows, :] += parts[1][0:T]
+            csum[rows, :] += parts[1][T:]
+            return 0
+
+        lax.fori_loop(0, S, seq, 0)
+
+    @pl.when(i == K - 1)
+    def _():
+        slot = lax.rem(i, slots)
+        row, col = iotas(T, T)
+        upper = (row <= col).astype(f32)
+
+        def seq(s, _):
+            rows = pl.ds(pl.multiple_of(s * T, T), T)
+            ds = dscores[s]
+            dact = (
+                jnp.dot(ds.astype(bf16), bcs[1, rows, :], preferred_element_type=f32),
+                jnp.dot(ds.T.astype(bf16), bcs[0, rows, :], preferred_element_type=f32),
+            )
+            for a in range(2):
+                conv = conv_of(dims, proj0[0, rows, a * LANES : (a + 1) * LANES], pars, pad.at[a],
+                               DI + a * ST)
+                conv_back(slot, rows, a * LANES, DI + a * ST, dact[a], conv, sigmoid(conv), a)
+            v, e, step, _, _ = steps_of(
+                dims, proj0[0, rows, 2 * LANES : 3 * LANES].astype(f32), hpar
+            )
+            dsteps = jnp.dot(
+                upper, dlog[rows, :], precision=lax.Precision.HIGHEST,
+                preferred_element_type=f32,
+            )
+            sg = jnp.where(v >= 0.0, 1.0, e) / (1.0 + e)
+            ratio = jnp.where(step > 1e-30, sg / jnp.maximum(step, 1e-30), 1.0)
+            ddt = csum[rows, :] * ratio + dsteps * hpar[1:2, :] * sg
+            _, lane = iotas(T, LANES)
+            ddt = jnp.where(lane < H, ddt, 0.0)
+            dpj[slot, rows, 2 * LANES : 3 * LANES] = ddt.astype(bf16)
+            dpj[slot, rows, 3 * LANES :] = jnp.zeros((T, w - 3 * LANES), bf16)
+            hacc[0:8, :] += sum8(ddt)
+            hacc[8:16, :] += sum8(dsteps * step)
+            return 0
+
+        lax.fori_loop(0, S, seq, 0)
+        small[...] = jnp.zeros_like(small)
+        for k in range(KW + 1):
+            small[k : k + 1, :] = jnp.sum(cacc[8 * k : 8 * k + 8, :], axis=0, keepdims=True)
+        for k in range(2):
+            small[KW + 1 + k : KW + 2 + k, 0:DI] = jnp.sum(
+                dacc[8 * k : 8 * k + 8, :], axis=0, keepdims=True
+            )
+            small[KW + 3 : KW + 4, k * LANES : (k + 1) * LANES] = jnp.sum(
+                hacc[8 * k : 8 * k + 8, :], axis=0, keepdims=True
+            )
         total.start(0, small[...])
-        own[0] = uT[:, at.c].reshape(N * r, R)
-        own[1] = uT[:, 1 - at.c].reshape(N * r, R)
-        dns[...] = jnp.zeros_like(dns)
 
     for stage in range(1, 4):
 
-        @pl.when(i == stage)
+        @pl.when(i == K - 1 + stage)
         def _(stage=stage):
             total.start(stage, total.finish(stage - 1))
 
-    @pl.when(i == 4)
+    @pl.when(i == K + 3)
     def _():
         sums[...] = total.finish(3)
 
+    p = jnp.where(i < KO, 2 * i + 1, i + KO)
+
     @pl.when(i < K)
     def _():
-        net.begin(i, own, dproj[...])
+        net.begin(p, uo, dpj[lax.rem(i, slots)])
+
+    net.step(p, finish)
+
+    lag = slots - 1
+
+    @pl.when(i >= lag)
+    def _():
+        slot = lax.rem(i - lag, slots)
         M = 256
 
-        def rows(k, _):
-            at_ = pl.ds(pl.multiple_of(k * M, M), M)
+        def rows_of(m, _):
+            at_ = pl.ds(pl.multiple_of(m * M, M), M)
             part = lax.dot_general(
-                dproj[at_, :], wfull[...], (((1,), (1,)), ((), ())), preferred_element_type=f32
-            )
-
-            @pl.when(i == 0)
+                dpj[slot, at_, :], wf[0], (((1,), (1,)), ((), ())), preferred_element_type=f32
+            )
+
+            @pl.when(i == lag)
             def _():
-                dtok[at_, :] = part
-
-            @pl.when(i > 0)
+                dn[at_, :] = part
+
+            @pl.when(i > lag)
             def _():
-                dtok[at_, :] += part
+                dn[at_, :] += part
 
             return 0
 
-        lax.fori_loop(0, R // M, rows, 0)
-
-    def finish(j, v):
-        dw[...] = v
-        _, col = iotas(r, w)
-        p = jnp.where(col < E - j * w, v * wl[:, pl.ds(0, w)].astype(f32), 0.0)
-        part = p[:, 0:LANES]
-        for k in range(1, w // LANES):
-            part = part + p[:, k * LANES : (k + 1) * LANES]
-        dns[...] += part
-
-    net.step(i, finish)
-
-    @pl.when((i >= K) & (i < K + 4))
-    def _():
-        M = R // 4
-
-        def tail(k, _):
-            at_ = pl.ds(pl.multiple_of((i - K) * M + k * 64, 64), 64)
-            u = tok[at_, :].astype(f32)
-            rs = lax.rsqrt(jnp.mean(u * u, axis=-1, keepdims=True) + epsilon)
-            u = u * rs
-            d = dtok[at_, :] * scale[0:1, :]
-            m = jnp.mean(d * u, axis=-1, keepdims=True)
-            dtok[at_, :] = go[at_, :].astype(f32) + rs * (d - u * m)
-            return 0
-
-        lax.fori_loop(0, M // 64, tail, 0)
+        lax.fori_loop(0, R // M, rows_of, 0)
 
     @pl.when(i == K + 3)
     def _():
         net.drain()
 
 
-def run_reduce_in(axis, geom, uT, dproj, wfull, wl, scale, tok, go, small):
+def run_backward_net(dims, axis, geom, E, proj, ssd, ofull, wfull, uT, mT, go, wl, tabs, pars,
+                     skip, hpar):
+    T, DI, C, H, KW, ST = (dims[k] for k in ("T", "DI", "C", "H", "KW", "ST"))
     A0, A = geom
-    R, D = tok.shape
-    r, E = wl.shape
-    w = CHUNK
-    K = dproj.shape[1] // w
     N = A0 * A * A
-    once = dict(pipeline_mode=pl.Buffered(1))
-    late = lambda i: (0, jnp.clip(i - 4, 0, K - 1))
-    early = lambda i: (0, jnp.minimum(i, K - 1))
-    whole = lambda i: (0, 0)
+    K, R, w = proj.shape
+    r = wl.shape[1]
+    D = go.shape[1]
+    ro = DI // (2 * N)
+    HF = ro // r
+    half = w // 2
+    S = R // T
+    KO = HF * (D // w)
+    assert KO <= K - 1 and HF * r == ro and D % w == 0
+    slots = 5
+    whole = lambda s: pl.BlockSpec(s, lambda i: (0,) * len(s), pipeline_mode=pl.Buffered(1))
+    tile = lambda i: jnp.clip(i, 0, K - 2)
+    hbm = pl.BlockSpec(memory_space=pl.ANY)
+    lagged = lambda i: (lax.rem(jnp.clip(i - slots + 1, 0, K - 1) + 1, K), 0, 0)
     return pl.pallas_call(
-        functools.partial(reduce_in, axis, geom, K, E),
+        functools.partial(backward, dims, axis, geom, K, KO, E),
         grid=(K + 4,),
         in_specs=[
-            pl.BlockSpec((N, 2, r, R), lambda i: (0, 0, 0, 0), **once),
-            pl.BlockSpec((R, w), early),
-            pl.BlockSpec((D, w), early),
-            pl.BlockSpec((r, w), late),
-            pl.BlockSpec((8, D), whole, **once),
-            pl.BlockSpec((R, D), whole, **once),
-            pl.BlockSpec((R, D), whole, **once),
-            pl.BlockSpec(small.shape, whole, **once),
+            pl.BlockSpec((1, R, w), lambda i: (tile(i) + 1, 0, 0)),
+            whole((1, R, w)),
+            pl.BlockSpec((R, half), lambda i: (0, tile(i))),
+            pl.BlockSpec((half, D), lambda i: (tile(i), 0)),
+            pl.BlockSpec((1, D, w), lagged),
+            hbm, hbm, whole((R, D)), whole((K, r, w)), whole((2, R, LANES)), whole((16, C)),
+            whole((8, DI)), whole((8, LANES)),
         ],
-        out_specs=[
-            pl.BlockSpec((r, w), late),
-            pl.BlockSpec((r, LANES), whole, **once),
-            pl.BlockSpec((R, D), whole, **once),
-            pl.BlockSpec(small.shape, whole, **once),
+        out_specs=[whole((R, D)), whole((K + KO, r, w)), whole((r, LANES)), whole((8, C))],
+        out_shape=[
+            jax.ShapeDtypeStruct((R, D), f32),
+            jax.ShapeDtypeStruct((K + KO, r, w), f32),
+            jax.ShapeDtypeStruct((r, LANES), f32),
+            jax.ShapeDtypeStruct((8, C), f32),
         ],
-        out_shape=[
-            jax.ShapeDtypeStruct((r, E), f32),
-            jax.ShapeDtypeStruct((r, LANES), f32),
-            jax.ShapeDtypeStruct((R, D), f32),
-            jax.ShapeDtypeStruct(small.shape, f32),
-        ],
-        scratch_shapes=[pltpu.VMEM((2, N * r, R), bf16)]
-        + Reduce.scratch(K, A0, A, r, w)
-        + SumAll.scratch(A0, A, small.shape),
+        scratch_shapes=[
+            pltpu.VMEM((2, N, r, R), bf16),
+            pltpu.VMEM((HF, 2, N, r, R), bf16),
+            pltpu.VMEM((R, half), f32),
+            pltpu.VMEM((slots, R, w), bf16),
+            pltpu.VMEM((2, FRONT + T, LANES), f32),
+            pltpu.VMEM((2, FRONT + T, LANES), f32),
+            pltpu.VMEM((S, T, LANES), f32),
+            pltpu.VMEM((S, LANES, T), f32),
+            pltpu.VMEM((S, T, T), f32),
+            pltpu.VMEM((S, T, T), f32),
+            pltpu.VMEM((R, LANES), f32),
+            pltpu.VMEM((R, LANES), f32),
+            pltpu.VMEM((2, R, ST), bf16),
+            pltpu.VMEM((T, T), f32),
+            pltpu.VMEM((8 * (KW + 1), C), f32),
+            pltpu.VMEM((16, DI), f32),
+            pltpu.VMEM((16, LANES), f32),
+            pltpu.VMEM((8, C), f32),
+            pltpu.SemaphoreType.DMA((2 + 2 * HF,)),
+        ]
+        + Reduce.scratch(K + KO, A0, A, r, w)
+        + SumAll.scratch(A0, A, (8, C)),
         compiler_params=pltpu.CompilerParams(
             collective_id=2, has_side_effects=True, vmem_limit_bytes=VMEM
         ),
         cost_estimate=pl.CostEstimate(
-            flops=4 * R * D * E, bytes_accessed=2 * D * E * 40, transcendentals=0
+            flops=6 * R * D * K * w, bytes_accessed=D * K * w * 90, transcendentals=0
         ),
-        name="reduce_in",
-    )(uT.reshape(N, 2, r, R), dproj, wfull, wl, scale, tok, go, small)
+        name="backward",
+    )(proj, proj, ssd, ofull.reshape(DI, D), wfull.reshape(K, D, w), uT.reshape(N, 2, r, R),
+      mT.reshape(N, 2, HF, r, R), go, wl, tabs, pars, skip, hpar)
 
 
 def local(axis, n, tokens, in_weight, conv_weight, conv_bias, dt_bias, a_log, skip_d,
@@ -1075,18 +1388,19 @@
     assert LANES % HD == 0 and ST == LANES and DI % (LANES * 2) == 0 and T % 16 == 0
     geom = geometry(n)
     w = CHUNK
-    K = -(-E // w)
-    EP = K * w
-    Gn = DI // n
+    Gn, ro = DI // n, out_weight.shape[0]
     own = (
-        geom is not None and r % 16 == 0 and EP - LANES >= E and max(Cn, Gn) < LANES
-        and KW + 2 <= r
+        geom is not None and r % 16 == 0 and ro % r == 0 and D % w == 0 and DI % (w // 2) == 0
+        and w == 2 * ST + 2 * LANES and E == 2 * DI + 2 * ST + H and H <= LANES
+        and max(Cn, Gn) < LANES and 6 <= KW + 2 <= 8 and ro // r * (D // w) < DI * 2 // w
     )
     me = lax.axis_index(axis)
-
-    ns = norm_scale.astype(f32)
     tok = tokens.reshape(R, D)
     go = grad_out.reshape(R, D)
+    rate = -jnp.exp(a_log)
+    hpar = jnp.pad(jnp.stack([dt_bias, rate]), ((0, 6), (0, LANES - H)))
+    skip = jnp.broadcast_to(jnp.repeat(skip_d, HD)[None], (8, DI))
+    ns = norm_scale.astype(f32)
     if own:
         rows = [conv_weight.T, conv_bias[None], gate_scale[None]]
         pads = jnp.concatenate(
@@ -1094,61 +1408,55 @@
             + [jnp.zeros((r - KW - 2, LANES - 1), bf16)],
             axis=0,
         )
-        wl = jnp.concatenate(
-            [in_weight, jnp.zeros((r, EP - LANES - E), bf16), pads, norm_scale[:, None]], axis=1
+        first = jnp.concatenate(
+            [in_weight[:, 2 * DI :], jnp.zeros((r, LANES - H), bf16), pads, norm_scale[:, None]],
+            axis=1,
         )
-        wl = jnp.roll(wl.reshape(r, K, w).transpose(1, 0, 2), 1, axis=0)
-        proj, wfull, uT, scale = run_gather(axis, geom, tok, wl, E)
-        got = wfull.reshape(n, r, EP)[:, : KW + 2, EP - LANES :]
-        conv, gate = got[:, : KW + 1, :Cn], got[:, KW + 1, :Gn]
+        K = DI * 2 // w + 1
+        rest = in_weight[:, : 2 * DI].reshape(r, 2, K - 1, w // 2).transpose(2, 0, 1, 3)
+        wl = jnp.concatenate([first[None], rest.reshape(K - 1, r, w)], axis=0)
+        proj, ssd, uT, mT, output, tabs, pars, scale, wfull, ofull = run_forward_net(
+            dims, axis, geom, tok, go, wl, out_weight, hpar, skip
+        )
+        dn, outc, dns, sums = run_backward_net(
+            dims, axis, geom, E, proj, ssd, ofull, wfull, uT, mT, go, wl, tabs, pars, skip, hpar
+        )
+        scale = scale[0:1]
+        rest = outc[: K - 1].reshape(K - 1, r, 2, w // 2).transpose(1, 2, 0, 3)
+        dw = jnp.concatenate([rest.reshape(r, 2 * DI), outc[K - 1][:, : E - 2 * DI]], axis=1)
+        dow = outc[K:].reshape(ro // r, D // w, r, w).transpose(0, 2, 1, 3).reshape(ro, D)
     else:
-        EP = E
         out_full = lax.all_gather(out_weight, axis, axis=0, tiled=True)
         wfull = lax.all_gather(in_weight, axis, axis=0, tiled=True)
         conv = lax.all_gather(jnp.concatenate([conv_weight.T, conv_bias[None]]), axis, axis=0)
-        gate = lax.all_gather(gate_scale, axis, axis=0)
+        conv = conv.transpose(1, 0, 2).reshape(KW + 1, C).astype(f32)
+        gate = lax.all_gather(gate_scale, axis, axis=0).reshape(1, DI).astype(f32)
         scale = lax.all_gather(norm_scale, axis, axis=0).reshape(1, D).astype(f32)
         u = tok.astype(f32)
-        rs = lax.rsqrt(jnp.mean(u * u, axis=-1, keepdims=True) + epsilon)
-        uh = (u * rs * scale).astype(bf16)
+        u = u * lax.rsqrt(jnp.mean(u * u, axis=-1, keepdims=True) + epsilon)
+        uh = (u * scale).astype(bf16)
         proj = jnp.dot(uh, wfull, preferred_element_type=f32).astype(bf16)
-    conv = conv.transpose(1, 0, 2).reshape(KW + 1, C).astype(f32)
-
-    rate = -jnp.exp(a_log)
-    cpar = jnp.concatenate([conv, jnp.zeros((8 - KW - 1, C), f32)], axis=0)
-    hpar = jnp.zeros((8, LANES), f32).at[0, :H].set(dt_bias).at[1, :H].set(rate)
-    dpar = jnp.concatenate(
-        [jnp.repeat(skip_d, HD)[None], gate.reshape(1, DI).astype(f32), jnp.zeros((6, DI), f32)]
-    )
-    net = geom if own else None
-    mixed, ssd, rstd, *got = run_forward(dims, axis, net, proj, cpar, hpar, dpar, out_weight)
-    if own:
-        out_full = got[0].reshape(DI, D)
-    d_mixed = lax.dot_general(go, out_full, (((1,), (1,)), ((), ())), preferred_element_type=f32)
-    dproj, small, *got = run_backward(
-        dims, axis, net, EP, proj, d_mixed, ssd, rstd, cpar, hpar, dpar, mixed, go
-    )
-    output = lax.dot_general(
-        mixed, out_full, (((0,), (0,)), ((), ())), preferred_element_type=f32
-    )
-    output = (tok.astype(f32) + output).astype(bf16)
-    if own:
-        dow = got[0]
-        dw, dns, dtok, sums = run_reduce_in(
-            axis, geom, uT, dproj, wfull, in_weight, scale, tok, go, small
+        cpar = jnp.pad(conv, ((0, 8 - KW - 1), (0, 0)))
+        dpar = jnp.concatenate([skip[:1], gate, skip[2:]], axis=0)
+        mixed, ssd, rstd = run_forward(dims, proj, cpar, hpar, dpar)
+        output = jnp.dot(mixed, out_full, preferred_element_type=f32)
+        output = (tok.astype(f32) + output).astype(bf16)
+        d_mixed = lax.dot_general(
+            go, out_full, (((1,), (1,)), ((), ())), preferred_element_type=f32
         )
-    else:
-        g_out = jnp.dot(mixed, go, preferred_element_type=f32).astype(bf16)
+        dproj, small = run_backward(dims, proj, d_mixed, ssd, rstd, cpar, hpar, dpar)
+        left = (((0,), (0,)), ((), ()))
+        g_out = lax.dot_general(mixed, go, left, preferred_element_type=f32).astype(bf16)
         dow = lax.psum_scatter(g_out, axis, scatter_dimension=0, tiled=True).astype(f32)
-        g_in = lax.dot_general(
-            uh, dproj, (((0,), (0,)), ((), ())), preferred_element_type=f32
-        ).astype(bf16)
+        g_in = lax.dot_general(uh, dproj, left, preferred_element_type=f32).astype(bf16)
         dw = lax.psum_scatter(g_in, axis, scatter_dimension=0, tiled=True).astype(f32)
         dns = dw * in_weight.astype(f32)
-        d = lax.dot_general(dproj, wfull, (((1,), (1,)), ((), ())), preferred_element_type=f32)
-        u, d = u * rs, d * scale
-        dtok = go.astype(f32) + rs * (d - u * jnp.mean(d * u, axis=-1, keepdims=True))
+        dn = lax.dot_general(dproj, wfull, (((1,), (1,)), ((), ())), preferred_element_type=f32)
         sums = lax.psum(small, axis)
+    u = tok.astype(f32)
+    rs = lax.rsqrt(jnp.mean(u * u, axis=-1, keepdims=True) + epsilon)
+    u, d = u * rs, dn * scale
+    dtok = go.astype(f32) + rs * (d - u * jnp.mean(d * u, axis=-1, keepdims=True))
     dconv = lax.dynamic_slice(sums, (0, me * Cn), (KW + 1, Cn))
     heads = sums[KW + 3]
     return (

time: 502 us -> 459 us (0.914)
  Pallas kernels: 447 us -> 413 us
  matrix products: 28.5 us -> 0 us
  other arithmetic: 5.13 us -> 21.1 us
    pallas_call x4 -> x2, Pallas kernels: 447 us -> 413 us  [the longest x1 236 us: run_backward_net(): pl.pallas_call(functools.partial(backward, dims, axis, geom, K, KO, E), g...]
    dot_general x2 -> x0, matrix products: 28.5 us -> none  [the longest x1 16 us: local(): lax.dot_general(mixed, out_full, (((0,), (0,)), ((), ())), preferred_elem...]
    reduce_sum x0 -> x2, other arithmetic: none -> 7.45 us  [the longest x1 4.88 us: local(): jnp.mean(d * u, axis=-1, keepdims=True)]
    add x0 -> x1, other arithmetic: none -> 5.13 us  [local(): go.astype(f32) + rs * (d - u * jnp.mean(d * u, axis=-1, keepdims=True))]
where the time goes in v4:
time: 459 us; the launch traced here: 458 us
  Pallas kernels  413 us (90%)
  local copies, waits for them, and re-layouts  22.9 us (5%)
  other arithmetic  21.1 us (5%)
    pallas_call x1, Pallas kernels, run_backward_net(): pl.pallas_call(functools.partial(backward, dims, axis, geom, K, KO, E), g...  236 us
    pallas_call x1, Pallas kernels, run_forward_net(): pl.pallas_call(functools.partial(forward, dims, axis, geom, K, KO), grid=...  177 us

profile of v4, /device:TPU:0, one launch (start us, length us, event | category | flops | bytes accessed | tf_op | source)
XLA Modules:
  0.0 457.9 jit_solution(16609291716902994506)
XLA Ops:
  0.6 0.7 fusion.18
  1.4 1.3 select_maximum_fusion.hpar
  2.7 2.6 multiply_reduce_fusion.1
  5.2 0.6 add_rsqrt_fusion
  5.8 0.8 copy.26
  6.6 0.7 broadcast_in_dim.36
  7.4 0.8 slice.48
  8.2 0.8 maximum_bitcast_fusion
  9.0 0.6 broadcast_in_dim.38.skip
  9.6 1.1 slice.49
  12.0 0.9 pad_maximum_fusion.1.wl
  12.9 177.3 %forward.1 = (bf16[13,1024,512]{2,1,0:T(8,128)(2,1)}, f32[1024,3072]{1,0:T(8,128)}, bf16[1536,1024]{1,0:T(8,128)(2,1)}, bf16[3072,1024]{1,0:T(8,128)(2,1)}, bf16...) custom-call(bf16[1024,1536]{1,0:T(8,128)(2,1)} %bitcast.42, ...), custom_call_target="tpu_custom_call" | custom-call | flops 20937965568 | bytes 613416960 | tf_op jit(solution)/shard_map/forward/pallas_call | solution.py:977
  190.2 1.4 slice_reduce_fusion.1
  191.6 235.8 %backward.1 = (f32[1024,1536]{1,0:T(8,128)}, f32[19,48,512]{2,1,0:T(8,128)}, f32[48,128]{1,0:T(8,128)}, f32[8,3328]{1,0:T(8,128)}) custom-call(bf16[13,1024,512]{2,1,0:T(8,128)(2,1)} %get-tuple-element.26.proj.proj0, bf16[13,1024,512]{2,1,0:T(8,128)(2,1)} %get-tuple-element.26.proj.proj0, f32[1024,3072]{1,0:T(8,128)} %get-tuple-element.27.ssd, ...), custom_call_target="tpu_custom_call" | custom-call | flops 62813896704 | bytes 920125440 | tf_op jit(solution)/shard_map/backward/pallas_call | solution.py:1323
  427.5 1.0 reduce_sum.39
  428.5 1.3 slice_bitcast_fusion.2
  429.9 1.6 bitcast_multiply_fusion
  431.4 0.8 constant_dynamic-slice_fusion
  433.3 4.9 %multiply_reduce_fusion = f32[1024]{0:T(1024)S(1)} fusion(f32[1024,1536]{1,0:T(8,128)} %get-tuple-element.34, f32[1536]{0:T(1024)} %slice_reduce_fusion.1, f32[1024]{0:T(1024)} %bitcast.53, bf16[2,4,128,1536]{3,2,1,0:T(8,128)(2,1)} %param.11), kind=kLoop, calls=%fused_computation.1 | loop fusion | flops 7863296 | bytes 9451520 | tf_op jit(solution)/shard_map/reduce_sum | solution.py:1459
  438.2 5.1 %multiply_add_fusion = f32[1024,1536]{1,0:T(8,128)} fusion(f32[1024,1536]{1,0:T(8,128)S(1)} %copy-done.1, f32[1024]{0:T(1024)S(1)} %broadcast_multiply_fusion, f32[1536]{0:T(1024)S(1)} %copy-done.2, f32[1024]{0:T(1024)S(1)} %bitcast.54, bf16[2,4,128,1536]{3,2,1,0:T(8,128)(2,1)} %param.21, bf16[2,4,128,1536]{3,2,1,0:T(8,128)(2,1)S(1)} %copy-done), kind=kLoop, calls=%fused_computation | loop fusion | flops 12582912 | bytes 18888704 | tf_op jit(solution)/shard_map/add | solution.py:1459
  443.4 0.9 slice_reduce_fusion
  444.3 0.9 slice.61
  445.2 0.6 dynamic-slice_bitcast_fusion
  445.9 0.6 reduce_sum.38
  446.5 0.9 slice_bitcast_fusion
  447.4 1.1 slice.62
  448.5 1.4 slice.51
  449.9 0.8 reshape.99
  451.1 1.0 copy.30
  452.1 0.7 copy.32
  453.1 1.1 pad_maximum_fusion
  454.2 3.8 copy.34
  (22 shorter events, 3.3 us)
Async XLA Ops:
  427.5 10.7 %copy-start = (bf16[2,4,128,1536]{3,2,1,0:T(8,128)(2,1)S(1)}, bf16[2,4,128,1536]{3,2,1,0:T(8,128)(2,1)}, u32[]{:S(2)}) copy-start(bf16[2,4,128,1536]{3,2,1,0:T(8,128)(2,1)} %param.11) | copy-start | bytes 9437188
  427.5 10.7 %copy-start.2 = (f32[1536]{0:T(1024)S(1)}, f32[1536]{0:T(1024)}, u32[]{:S(2)}) copy-start(f32[1536]{0:T(1024)} %slice_reduce_fusion.1) | copy-start | bytes 18436
  427.5 10.7 %copy-start.3 = (f32[2,4,128]{2,1,0:T(4,128)S(1)}, f32[2,4,128]{2,1,0:T(4,128)}, u32[]{:S(2)}) copy-start(f32[2,4,128]{2,1,0:T(4,128)} %add_rsqrt_fusion) | copy-start | bytes 12292
  428.5 9.7 %copy-start.1 = (f32[1024,1536]{1,0:T(8,128)S(1)}, f32[1024,1536]{1,0:T(8,128)}, u32[]{:S(2)}) copy-start(f32[1024,1536]{1,0:T(8,128)} %get-tuple-element.34) | copy-start | bytes 18874372

commit v5 on v4

--- a/solution.py
+++ b/solution.py
@@ -84,6 +84,7 @@
 MESH = pl.DeviceIdType.MESH
 CHUNK = 512
 VMEM = 67043328
+ROWS = 512
 
 
 def geometry(n):
@@ -153,90 +154,117 @@
 
 
 class Gather:
-    def __init__(self, at, K, mine, whole, ssem, rsem, lsem):
-        self.at, self.K, self.mine, self.whole = at, K, mine, whole
+    LAG = 2
+    DEEP = 4
+    ORDER = (0, 4, 3, 2, 1)
+    WARM = 2
+
+    def __init__(self, at, K, mine, whole, ssem, rsem, lsem, warm=0):
+        self.at, self.K, self.mine, self.whole, self.warm = at, K, mine, whole, warm
         self.ssem, self.rsem, self.lsem = ssem, rsem, lsem
 
     @staticmethod
     def scratch(K, A0, A):
-        NS = (A0 - 1) + (A - 1) + (A - 1) * A + 1
+        NS = (A0 - 1) * A + (A - 1) + (A - 1) * A + 1
         return [
-            pltpu.SemaphoreType.DMA((2, NS)),
+            pltpu.SemaphoreType.DMA((Gather.DEEP, NS)),
             pltpu.SemaphoreType.DMA((K, NS)),
-            pltpu.SemaphoreType.DMA((2,)),
+            pltpu.SemaphoreType.DMA((Gather.DEEP,)),
         ]
 
     def local(self, j):
         at = self.at
         return pltpu.make_async_copy(
             self.mine(j), self.whole(j, at.a0, at.pos(at.f, at.s), at.c),
-            self.lsem.at[lax.rem(j, 2)],
+            self.lsem.at[lax.rem(j, self.DEEP)],
         )
 
-    def copies(self, stage, j, sending):
+    def copies(self, stage, j, sending, late):
         at, whole = self.at, self.whole
         A0, A = at.A0, at.A
-        par = lax.rem(j, 2)
+        par = lax.rem(j, self.DEEP)
+        line0, first0 = 0, (A0 - 1) * A
+        second0 = first0 + A - 1
         every = slice(None)
         out = []
 
         def add(k, src, dst, device):
             out.append(send(src, dst, self.ssem.at[par, k], self.rsem.at[j, k], device))
 
-        if stage == 0:
+        if stage == 0 and not late:
             for q in range(1, A0):
                 a = at.a0 if sending else at.line(-q)
-                add(q - 1, self.mine(j), whole(j, a, at.pos(at.f, at.s), at.c),
+                add(line0 + q - 1, self.mine(j), whole(j, a, at.pos(at.f, at.s), at.c),
                     at.device(at.line(q), at.f, at.s, at.c))
-        elif stage == 1:
+        elif stage == 1 and late:
+            for q in range(1, A0):
+                a = at.a0 if sending else at.line(-q)
+                for o in range(A):
+                    ref = whole(j, a, at.pos(o, at.s), at.c)
+                    add(line0 + (q - 1) * A + o, ref, ref,
+                        at.device(at.line(q), at.f, at.s, at.c))
+        elif stage < 2:
             for q in range(1, A):
                 f = at.f if sending else at.first(-q)
-                ref = whole(j, every, at.pos(f, at.s), at.c)
-                add(A0 - 1 + q - 1, ref, ref, at.device(at.a0, at.first(q), at.s, at.c))
+                ref = whole(j, at.a0 if late else every, at.pos(f, at.s), at.c)
+                add(first0 + q - 1, self.mine(j) if late else ref, ref,
+                    at.device(at.a0, at.first(q), at.s, at.c))
         elif stage == 2:
             for q in range(1, A):
                 s = at.s if sending else at.second(-q)
                 for o in range(A):
                     ref = whole(j, every, at.pos(o, s), at.c)
-                    add(A0 - 1 + A - 1 + (q - 1) * A + o, ref, ref,
+                    add(second0 + (q - 1) * A + o, ref, ref,
                         at.device(at.a0, at.f, at.second(q), at.c))
         else:
             ref = whole(j, every, every, at.c if sending else 1 - at.c)
-            add(A0 - 1 + (A - 1) * (A + 1), ref, ref, at.partner())
+            add(second0 + (A - 1) * A, ref, ref, at.partner())
         return out
 
+    def each(self, stage, j, sending, act):
+        def run(late):
+            for cp in self.copies(stage, j, sending, late):
+                act(cp)
+
+        if stage >= 2:
+            run(False)
+            return
+        late = lax.rem(j, 3) == 2
+        pl.when(late)(lambda: run(True))
+        pl.when(jnp.logical_not(late))(lambda: run(False))
+
     def step(self, i):
-        for stage in range(5):
+        for stage in self.ORDER:
             j = i - stage
-
-            @pl.when((j >= 0) & (j < self.K))
+            early = (j >= 0) & (j < self.warm)
+            j = jnp.where(early, j, i - stage * self.LAG)
+
+            @pl.when(early | ((j >= self.warm) & (j < self.K)))
             def _(stage=stage, j=j):
                 if stage > 0:
-                    for cp in self.copies(stage - 1, j, False):
-                        cp.wait_recv()
+                    self.each(stage - 1, j, False, lambda cp: cp.wait_recv())
                 if stage < 4:
 
-                    @pl.when(j >= 2)
+                    @pl.when(j >= self.DEEP)
                     def _():
-                        for cp in self.copies(stage, j - 2, True):
-                            cp.wait_send()
+                        self.each(stage, j - self.DEEP, True, lambda cp: cp.wait_send())
 
                     if stage == 1:
                         self.local(j).wait()
-                    for cp in self.copies(stage, j, True):
-                        cp.start()
+                    self.each(stage, j, True, lambda cp: cp.start())
                     if stage == 0:
                         self.local(j).start()
 
     def drain(self):
-        for j in range(max(0, self.K - 2), self.K):
+        for j in range(max(0, self.K - self.DEEP), self.K):
             for stage in range(4):
-                for cp in self.copies(stage, jnp.int32(j), True):
+                for cp in self.copies(stage, jnp.int32(j), True, j % 3 == 2):
                     cp.wait_send()
 
 
 class Reduce:
     SLOTS = 3
+    LAG = 2
 
     def __init__(self, at, K, refs):
         self.at, self.K = at, K
@@ -379,8 +407,8 @@
                 v = v + self.r3[slot, p].astype(f32)
             finish(j, v)
 
-        for k, stage in ((1, stage1), (2, stage2), (3, stage3), (4, stage4)):
-            j = i - k
+        for k, stage in ((4, stage4), (3, stage3), (2, stage2), (1, stage1)):
+            j = i - k * self.LAG
 
             @pl.when((j >= 0) & (j < self.K))
             def _(j=j, k=k, stage=stage):
@@ -752,8 +780,8 @@
     return out
 
 
-def forward(dims, axis, geom, K, KO, tok, wl, ow, hpar, skip, tokc, goc,
-            proj, ssd, uT, mT, out, tabs, pars, scale, wfull, ofull,
+def forward(dims, axis, geom, K, KO, skip, tok, inw, taps, bias, gains, ns, dtb, alog, ow,
+            tokc, goc, proj, ssd, uT, mT, out, tabs, pars, scale, wl, hpar, wfull, ofull,
             uh, wv, wo, pj, gated, mixed, pad, ldtab, rowtab, scores, mask, acc, dtp, wsem, osem,
             *sems):
     T, DI, C, H, HD, ST, KW = (dims[k] for k in ("T", "DI", "C", "H", "HD", "ST", "KW"))
@@ -767,22 +795,54 @@
     HP = LANES // HD
     TC = half // LANES
     wo_cols = wo.shape[5]
-    net = Gather(at, K, lambda j: wl.at[j], lambda j, a, p, c: wfull.at[j, a, p, c], *sems[:3])
+    place = lambda j: lax.rem(j + K - 1, K)
+    part = lambda j: columns(lax.rem(j, 2), half)
+    net = Gather(
+        at, 2 * K, lambda j: wl.at[lax.div(j, 2), :, part(j)],
+        lambda j, a, p, c: wfull.at[place(lax.div(j, 2)), a, p, c, :, part(j)], *sems[:3],
+        warm=Gather.WARM,
+    )
     neto = Gather(
-        at, KO, lambda j: ow.at[:, columns(j, wo_cols)],
-        lambda j, a, p, c: ofull.at[a, p, c, :, columns(j, wo_cols)], *sems[3:],
+        at, 2 * KO, lambda j: ow.at[:, columns(j, wo_cols // 2)],
+        lambda j, a, p, c: ofull.at[a, p, c, :, columns(j, wo_cols // 2)], *sems[3:],
     )
 
     @pl.when(i == 0)
     def _():
+        r, E = inw.shape
+        Cn, Gn = bias.shape[1], gains.shape[1]
+        zero = jnp.zeros((LANES, LANES), f32)
+        dtp[...] = zero
+        dtp[0:1, 0:r] = ns[...].astype(f32)
+        column = pltpu.roll(dtp[...].T, LANES - 1, 1)
+        dtp[...] = column
+        dtp[0:KW, 0:Cn] = taps[...].astype(f32)
+        dtp[KW : KW + 1, 0:Cn] = bias[...].astype(f32)
+        dtp[KW + 1 : KW + 2, 0:Gn] = gains[...].astype(f32)
+        wl[0, :, 0 : half] = inw[:, 2 * DI : 2 * DI + half]
+        wl[0, :, half : half + LANES] = jnp.concatenate(
+            [inw[:, 2 * DI + half : E], jnp.zeros((r, LANES - H), bf16)], axis=1
+        )
+        wl[0, :, half + LANES :] = dtp[0:r, :].astype(bf16)
+        for j in range(1, K):
+            wl[j, :, 0:half] = inw[:, (j - 1) * half : j * half]
+            wl[j, :, half:] = inw[:, DI + (j - 1) * half : DI + j * half]
+        hpar[...] = jnp.zeros_like(hpar)
+        hpar[0:1, 0:H] = dtb[...]
+        hpar[1:2, 0:H] = -jnp.exp(alog[...])
         at.barrier()
 
-    net.step(i)
-    neto.step(i - K)
+    def travel(q):
+        net.step(q)
+        neto.step(q - 2 * K)
+
+    trip = 2 * i
+    i = i - 1
+    travel(trip)
 
     def fetch_w(j):
         slot = lax.rem(j, 2)
-        return pltpu.make_async_copy(wfull.at[j], wv.at[slot], wsem.at[slot])
+        return pltpu.make_async_copy(wfull.at[place(j)], wv.at[slot], wsem.at[slot])
 
     def fetch_o(k):
         slot = lax.rem(k, 2)
@@ -790,15 +850,18 @@
             ofull.at[:, :, :, :, columns(k, wo_cols)], wo.at[slot], osem.at[slot]
         )
 
-    @pl.when((i >= 4) & (i < K + 4))
-    def _():
-        fetch_w(i - 4).start()
+    ready = (i == 2) | ((i >= 5) & (i < K + 4))
+    chunk = jnp.maximum(i - 4, 0)
+
+    @pl.when(ready)
+    def _():
+        fetch_w(chunk).start()
 
     @pl.when((i >= K + 4) & (i < K + KO + 4))
     def _():
         fetch_o(i - K - 4).start()
 
-    @pl.when(i == 5)
+    @pl.when(i == 3)
     def _():
         row, col = iotas(T, T)
         mask[...] = jnp.where(col <= row, BIG, -BIG)
@@ -851,7 +914,7 @@
                     jnp.concatenate(mix, axis=1), stack_heads(dims, x),
                     preferred_element_type=f32,
                 )
-                o = core + skip[0:1, pl.ds(c0, LANES)] * x.astype(f32)
+                o = core + pars[8:9, pl.ds(c0, LANES)] * x.astype(f32)
                 ssd[rows, u * LANES : (u + 1) * LANES] = o
                 gate = pj[slot, rows, u * LANES : (u + 1) * LANES].astype(f32)
                 g = o * (gate * sigmoid(gate))
@@ -862,11 +925,15 @@
 
         lax.fori_loop(0, S, seq, 0)
 
-    @pl.when((i >= 4) & (i < K + 4))
-    def _():
-        fetch_w(i - 4).wait()
-
-    @pl.when(i == 4)
+    @pl.when(i < K + 5)
+    def _():
+        travel(trip + 1)
+
+    @pl.when(ready)
+    def _():
+        fetch_w(chunk).wait()
+
+    @pl.when(i == 2)
     def _():
         N = A0 * A * A * 2
         r = D // N
@@ -879,6 +946,12 @@
             pars[0:8, t * LANES : (t + 1) * LANES] = v
         for t, v in enumerate(assemble(parts, Gn, DI // LANES)):
             pars[8:16, t * LANES : (t + 1) * LANES] = v
+        _, lane = iotas(1, LANES)
+        for t in range(DI // LANES):
+            v = jnp.zeros((1, LANES), f32)
+            for q in range(HP):
+                v = jnp.where(lane // HD == q, skip[t * HP + q], v)
+            pars[8:9, t * LANES : (t + 1) * LANES] = v
 
         def norm(k, _):
             rows = pl.ds(pl.multiple_of(k * LANES, LANES), LANES)
@@ -891,10 +964,10 @@
 
         lax.fori_loop(0, R // LANES, norm, 0)
 
-    @pl.when((i >= 4) & (i < K + 4))
+    @pl.when(ready)
     def _():
         slot = lax.rem(i, 2)
-        M = 256
+        M = min(R, ROWS)
 
         def rows(k, _):
             at_ = pl.ds(pl.multiple_of(k * M, M), M)
@@ -920,7 +993,6 @@
                     lanes = pl.ds(pl.multiple_of((k * 4 + u) * LANES, LANES), LANES)
                     v = gated[rows, lanes] * rb * pars[8 + KW + 1 : 8 + KW + 2, lanes]
                     mixed[rows, lanes] = v.astype(bf16)
-                    mT[lanes, rows] = v.T.astype(bf16)
                 return 0
 
             lax.fori_loop(0, DI // LANES // 4, tile, 0)
@@ -928,6 +1000,10 @@
 
         lax.fori_loop(0, S, seq, 0)
         acc[...] = jnp.zeros_like(acc)
+
+    @pl.when(i >= K + 5)
+    def _():
+        travel(trip + 1)
 
     @pl.when(i >= K + 5)
     def _():
@@ -951,6 +1027,17 @@
 
         lax.fori_loop(0, R // M, rows, 0)
 
+        share = DI // LANES // KO
+
+        def turn(m, _):
+            for u in range(share):
+                lanes = pl.ds(pl.multiple_of((k * share + u) * LANES, LANES), LANES)
+                rows = pl.ds(pl.multiple_of(m * LANES, LANES), LANES)
+                mT[lanes, rows] = mixed[rows, lanes].T
+            return 0
+
+        lax.fori_loop(0, R // LANES, turn, 0)
+
     @pl.when(i == K + KO + 4)
     def _():
         net.drain()
@@ -960,31 +1047,34 @@
         tabs[1] = jnp.broadcast_to(mu, rb.shape) * rb * rb
 
 
-def run_forward_net(dims, axis, geom, tok, go, wl, ow, hpar, skip):
-    T, DI, C, H = (dims[k] for k in ("T", "DI", "C", "H"))
+def run_forward_net(dims, axis, geom, K, w, skip, tok, go, inw, smalls, ow):
+    T, DI, C = (dims[k] for k in ("T", "DI", "C"))
     A0, A = geom
     R, D = tok.shape
-    K, r, w = wl.shape
+    r = inw.shape[0]
     ro = ow.shape[0]
     half = w // 2
     wc = r * w // ro
     KO = D // wc
     S = R // T
-    steps = K + KO + 5
+    assert DI // LANES % KO == 0
+    steps = K + KO + 6
     whole = lambda s: pl.BlockSpec(s, lambda i: (0,) * len(s), pipeline_mode=pl.Buffered(1))
-    late = lambda i: (0, jnp.clip(i - K - 5, 0, KO - 1))
+    late = lambda i: (0, jnp.clip(i - K - 6, 0, KO - 1))
     hbm = pl.BlockSpec(memory_space=pl.ANY)
     return pl.pallas_call(
         functools.partial(forward, dims, axis, geom, K, KO),
         grid=(steps,),
-        in_specs=[whole((R, D)), whole((K, r, w)), whole((ro, D)), whole((8, LANES)),
-                  whole((8, DI)), pl.BlockSpec((R, wc), late), pl.BlockSpec((R, wc), late)],
+        in_specs=[pl.BlockSpec(memory_space=pltpu.SMEM), whole((R, D)), whole(inw.shape)]
+        + [whole(a.shape) for a in smalls]
+        + [whole((ro, D)), pl.BlockSpec((R, wc), late), pl.BlockSpec((R, wc), late)],
         out_specs=[
-            pl.BlockSpec((1, R, w), lambda i: (jnp.clip(i - 4, 0, K - 1), 0, 0)),
-            pl.BlockSpec((R, half), lambda i: (0, jnp.clip(i - 6, 0, K - 2))),
+            pl.BlockSpec((1, R, w), lambda i: (jnp.clip(i - 5, 0, K - 1), 0, 0)),
+            pl.BlockSpec((R, half), lambda i: (0, jnp.clip(i - 7, 0, K - 2))),
             whole((D, R)), whole((DI, R)),
             pl.BlockSpec((R, wc), late),
-            whole((2, R, LANES)), whole((16, C)), whole((8, D)), hbm, hbm,
+            whole((2, R, LANES)), whole((16, C)), whole((8, D)), whole((K, r, w)),
+            whole((8, LANES)), hbm, hbm,
         ],
         out_shape=[
             jax.ShapeDtypeStruct((K, R, w), bf16),
@@ -995,6 +1085,8 @@
             jax.ShapeDtypeStruct((2, R, LANES), f32),
             jax.ShapeDtypeStruct((16, C), f32),
             jax.ShapeDtypeStruct((8, D), f32),
+            jax.ShapeDtypeStruct((K, r, w), bf16),
+            jax.ShapeDtypeStruct((8, LANES), f32),
             jax.ShapeDtypeStruct((K, A0, A * A, 2, r, w), bf16),
             jax.ShapeDtypeStruct((A0, A * A, 2, ro, D), bf16),
         ],
@@ -1015,7 +1107,7 @@
             pltpu.SemaphoreType.DMA((2,)),
             pltpu.SemaphoreType.DMA((2,)),
         ]
-        + Gather.scratch(K, A0, A) + Gather.scratch(KO, A0, A),
+        + Gather.scratch(2 * K, A0, A) + Gather.scratch(2 * KO, A0, A),
         compiler_params=pltpu.CompilerParams(
             collective_id=1, has_side_effects=True, vmem_limit_bytes=VMEM
         ),
@@ -1023,13 +1115,13 @@
             flops=2 * R * D * K * w, bytes_accessed=D * K * w * 60, transcendentals=0
         ),
         name="forward",
-    )(tok, wl, ow, hpar, skip, tok, go)
+    )(skip, tok, inw, *smalls, ow, tok, go)
 
 
 def backward(dims, axis, geom, K, KO, E, proj, proj0, ssd, wo, wf, uT, mT, go, wl, tabs, pars,
-             skip, hpar, dn, outc, dns, sums,
+             hpar, dn, outc, dns, sums,
              uo, mo, dmx, dpj, pad, dpad, ldtab, rowtab, scores, dscores, dlog, csum, bcs, mask,
-             cacc, dacc, hacc, small, csem, *refs):
+             cacc, dacc, hacc, small, wv, csem, wsem, *refs):
     T, DI, C, H, HD, ST, KW = (dims[k] for k in ("T", "DI", "C", "H", "HD", "ST", "KW"))
     A0, A = geom
     at = Place(axis, A0, A)
@@ -1042,20 +1134,23 @@
     HP = LANES // HD
     TC = half // LANES
     D = go.shape[1]
-    HF = mo.shape[0]
-    slots = dpj.shape[0]
+    HF = mT.shape[2]
+    each = KO // HF
+    pairs = (K + 1) // 2
     net = Reduce(at, K + KO, refs[:15])
     total = SumAll(at, refs[15:])
 
     def fetches():
         out = [(uT.at[:, at.c], uo.at[0]), (uT.at[:, 1 - at.c], uo.at[1])]
-        for h in range(HF):
-            out += [(mT.at[:, at.c, h], mo.at[h, 0]), (mT.at[:, 1 - at.c, h], mo.at[h, 1])]
         return [pltpu.make_async_copy(s, d, csem.at[k]) for k, (s, d) in enumerate(out)]
 
+    def fetch_half(h):
+        out = [(mT.at[:, at.c, h], mo.at[0]), (mT.at[:, 1 - at.c, h], mo.at[1])]
+        return [pltpu.make_async_copy(s, d, csem.at[2 + k]) for k, (s, d) in enumerate(out)]
+
     @pl.when(i == 0)
     def _():
-        for cp in fetches():
+        for cp in fetches() + fetch_half(0):
             cp.start()
         at.barrier()
         for ref in (cacc, dacc, hacc, dlog, csum, dscores, dns):
@@ -1083,15 +1178,27 @@
             return 0
 
         lax.fori_loop(0, S, seq, 0)
-        for cp in fetches():
+        for cp in fetches() + fetch_half(0):
             cp.wait()
 
+    for h in range(1, HF):
+
+        @pl.when(i == 2 * h * each - 1)
+        def _(h=h):
+            for cp in fetch_half(h):
+                cp.start()
+
+        @pl.when(i == 2 * h * each)
+        def _(h=h):
+            for cp in fetch_half(h):
+                cp.wait()
+
     def finish(p, v):
-        inner = (p >= 2 * KO) | (lax.rem(p, 2) == 1)
+        inner = (p >= 3 * KO) | (lax.rem(p, 3) > 0)
 
         @pl.when(inner)
         def _():
-            g = jnp.where(p >= 2 * KO, p - KO, lax.div(p, 2))
+            g = jnp.where(p >= 3 * KO, p - KO, p - 1 - lax.div(p, 3))
             outc[g] = v
             q = v * wl[lax.rem(g + 1, K)].astype(f32)
             part = q[:, 0:LANES]
@@ -1101,22 +1208,44 @@
 
         @pl.when(jnp.logical_not(inner))
         def _():
-            outc[K + lax.div(p, 2)] = v
-
-    @pl.when(i < KO)
-    def _():
-        h = lax.div(i, KO // HF)
-        net.begin(2 * i, mo.at[h], go[:, columns(lax.rem(i, KO // HF), w)])
-        net.step(2 * i, finish)
-
-    def conv_back(slot, rows, lane0, c0, dact, conv, sig, u):
+            outc[K + lax.div(p, 3)] = v
+
+    def send_out():
+        k = lax.div(i, 2)
+
+        @pl.when((lax.rem(i, 2) == 0) & (k < KO))
+        def _():
+            net.step(3 * k, finish)
+            net.begin(3 * k, mo, go[:, columns(lax.rem(k, each), w)])
+
+    def fetch(t, q):
+        return pltpu.make_async_copy(
+            wf.at[2 * t + q], wv.at[:, q * w : (q + 1) * w], wsem.at[q]
+        )
+
+    def fetch_pair(t, act):
+        act(fetch(t, 0))
+
+        @pl.when(2 * t + 1 < K)
+        def _():
+            act(fetch(t, 1))
+
+    @pl.when(i == 0)
+    def _():
+        fetch_pair(0, lambda cp: cp.start())
+
+    slot = lax.rem(lax.div(i, 2), dpj.shape[0])
+    off = lax.rem(i, 2) * w
+    here_of = lambda lane: pl.ds(pl.multiple_of(off + lane, LANES), LANES)
+
+    def conv_back(rows, lane0, c0, dact, conv, sig, u):
         lanes = pl.ds(c0, LANES)
         dconv = dact * (sig * (1.0 + conv * (1.0 - sig)))
         dpad[u, 0:T, :] = dconv
         dcin = dconv * pars[KW - 1 : KW, lanes]
         for k in range(KW - 1):
             dcin = dcin + dpad[u, KW - 1 - k : KW - 1 - k + T, :] * pars[k : k + 1, lanes]
-        dpj[slot, rows, lane0 : lane0 + LANES] = dcin.astype(bf16)
+        dpj[slot, rows, here_of(lane0)] = dcin.astype(bf16)
         for k in range(KW):
             start = FRONT - KW + 1 + k
             cacc[8 * k : 8 * k + 8, lanes] += sum8(dconv * pad[u, start : start + T, :])
@@ -1124,18 +1253,10 @@
 
     @pl.when(i < K - 1)
     def _():
-        slot = lax.rem(i, slots)
         h0 = i * TC * HP
-        M = 256
-
-        def rows_of(m, _):
-            at_ = pl.ds(pl.multiple_of(m * M, M), M)
-            dmx[at_, :] = lax.dot_general(
-                go[at_, :], wo[...], (((1,), (1,)), ((), ())), preferred_element_type=f32
-            )
-            return 0
-
-        lax.fori_loop(0, R // M, rows_of, 0)
+        dmx[...] = lax.dot_general(
+            go[...], wo[...], (((1,), (1,)), ((), ())), preferred_element_type=f32
+        )
 
         def seq(s, _):
             rows = pl.ds(pl.multiple_of(s * T, T), T)
@@ -1160,7 +1281,7 @@
                 dgated = rb * (dm * pars[8 + KW + 1 : 8 + KW + 2, lanes]) - gated * mb
                 dacc[8:16, lanes] += sum8(dm * (gated * rb))
                 dssd = dgated * act
-                dpj[slot, rows, here] = (
+                dpj[slot, rows, here_of(u * LANES)] = (
                     dgated * o * (gs * (1.0 + gate * (1.0 - gs)))
                 ).astype(bf16)
                 low = dssd.astype(bf16)
@@ -1183,7 +1304,7 @@
                 core = jnp.dot(
                     jnp.concatenate(mix, axis=1), lows, preferred_element_type=f32
                 )
-                sk = skip[0:1, lanes]
+                sk = pars[8:9, lanes]
                 from_cols = xf * core
                 diff = low.astype(f32) * (o - sk * xf) - from_cols
                 prow, pcol = iotas(LANES, LANES)
@@ -1195,7 +1316,7 @@
                     jnp.concatenate([hi, lo], axis=1),
                     jnp.concatenate([place, place], axis=0), preferred_element_type=f32,
                 )
-                conv_back(slot, rows, half + u * LANES, c0, core + sk * dssd, conv, sig, u)
+                conv_back(rows, half + u * LANES, c0, core + sk * dssd, conv, sig, u)
                 new = (part, by_head)
                 parts = new if parts is None else tuple(p + q for p, q in zip(parts, new))
             dscores[s] += parts[0]
@@ -1203,11 +1324,12 @@
             csum[rows, :] += parts[1][T:]
             return 0
 
-        lax.fori_loop(0, S, seq, 0)
+        lax.fori_loop(0, S // 2, seq, 0)
+        send_out()
+        lax.fori_loop(S // 2, S, seq, 0)
 
     @pl.when(i == K - 1)
     def _():
-        slot = lax.rem(i, slots)
         row, col = iotas(T, T)
         upper = (row <= col).astype(f32)
 
@@ -1221,7 +1343,7 @@
             for a in range(2):
                 conv = conv_of(dims, proj0[0, rows, a * LANES : (a + 1) * LANES], pars, pad.at[a],
                                DI + a * ST)
-                conv_back(slot, rows, a * LANES, DI + a * ST, dact[a], conv, sigmoid(conv), a)
+                conv_back(rows, a * LANES, DI + a * ST, dact[a], conv, sigmoid(conv), a)
             v, e, step, _, _ = steps_of(
                 dims, proj0[0, rows, 2 * LANES : 3 * LANES].astype(f32), hpar
             )
@@ -1234,8 +1356,8 @@
             ddt = csum[rows, :] * ratio + dsteps * hpar[1:2, :] * sg
             _, lane = iotas(T, LANES)
             ddt = jnp.where(lane < H, ddt, 0.0)
-            dpj[slot, rows, 2 * LANES : 3 * LANES] = ddt.astype(bf16)
-            dpj[slot, rows, 3 * LANES :] = jnp.zeros((T, w - 3 * LANES), bf16)
+            dpj[slot, rows, here_of(2 * LANES)] = ddt.astype(bf16)
+            dpj[slot, rows, here_of(3 * LANES)] = jnp.zeros((T, LANES), bf16)
             hacc[0:8, :] += sum8(ddt)
             hacc[8:16, :] += sum8(dsteps * step)
             return 0
@@ -1263,38 +1385,53 @@
     def _():
         sums[...] = total.finish(3)
 
-    p = jnp.where(i < KO, 2 * i + 1, i + KO)
+    p = jnp.where(i < K, i + jnp.minimum(lax.div(i, 2) + 1, KO), 2 * i - K + KO)
+    net.step(p, finish)
 
     @pl.when(i < K)
     def _():
-        net.begin(p, uo, dpj[lax.rem(i, slots)])
-
-    net.step(p, finish)
-
-    lag = slots - 1
-
-    @pl.when(i >= lag)
-    def _():
-        slot = lax.rem(i - lag, slots)
-        M = 256
-
-        def rows_of(m, _):
-            at_ = pl.ds(pl.multiple_of(m * M, M), M)
-            part = lax.dot_general(
-                dpj[slot, at_, :], wf[0], (((1,), (1,)), ((), ())), preferred_element_type=f32
-            )
-
-            @pl.when(i == lag)
+        net.begin(p, uo, dpj[slot, :, pl.ds(pl.multiple_of(off, w), w)])
+
+    @pl.when(i >= K)
+    def _():
+        net.step(p + 1, finish)
+
+    tail = pairs - dpj.shape[0] + i - K
+    t = jnp.where(i < K, lax.div(i - 7, 2), tail)
+    turn = jnp.where(
+        i < K, (i >= 7) & (lax.rem(i, 2) == 1) & (t < pairs - dpj.shape[0]), t >= 0
+    )
+
+    @pl.when(turn)
+    def _():
+        fetch_pair(t, lambda cp: cp.wait())
+        mine = lax.rem(t, dpj.shape[0])
+
+        def add(part):
+            @pl.when(t == 0)
             def _():
-                dn[at_, :] = part
-
-            @pl.when(i > lag)
+                dn[...] = part()
+
+            @pl.when(t > 0)
             def _():
-                dn[at_, :] += part
-
-            return 0
-
-        lax.fori_loop(0, R // M, rows_of, 0)
+                dn[...] += part()
+
+        @pl.when(2 * t + 1 < K)
+        def _():
+            add(lambda: lax.dot_general(
+                dpj[mine], wv[...], (((1,), (1,)), ((), ())), preferred_element_type=f32
+            ))
+
+        @pl.when(2 * t + 1 >= K)
+        def _():
+            add(lambda: lax.dot_general(
+                dpj[mine, :, 0:w], wv[:, 0:w], (((1,), (1,)), ((), ())),
+                preferred_element_type=f32,
+            ))
+
+        @pl.when(t + 1 < pairs)
+        def _():
+            fetch_pair(t + 1, lambda cp: cp.start())
 
     @pl.when(i == K + 3)
     def _():
@@ -1302,7 +1439,7 @@
 
 
 def run_backward_net(dims, axis, geom, E, proj, ssd, ofull, wfull, uT, mT, go, wl, tabs, pars,
-                     skip, hpar):
+                     hpar):
     T, DI, C, H, KW, ST = (dims[k] for k in ("T", "DI", "C", "H", "KW", "ST"))
     A0, A = geom
     N = A0 * A * A
@@ -1314,12 +1451,10 @@
     half = w // 2
     S = R // T
     KO = HF * (D // w)
-    assert KO <= K - 1 and HF * r == ro and D % w == 0
-    slots = 5
+    assert 2 * KO <= K + 1 and HF * r == ro and D % w == 0
     whole = lambda s: pl.BlockSpec(s, lambda i: (0,) * len(s), pipeline_mode=pl.Buffered(1))
     tile = lambda i: jnp.clip(i, 0, K - 2)
     hbm = pl.BlockSpec(memory_space=pl.ANY)
-    lagged = lambda i: (lax.rem(jnp.clip(i - slots + 1, 0, K - 1) + 1, K), 0, 0)
     return pl.pallas_call(
         functools.partial(backward, dims, axis, geom, K, KO, E),
         grid=(K + 4,),
@@ -1328,9 +1463,8 @@
             whole((1, R, w)),
             pl.BlockSpec((R, half), lambda i: (0, tile(i))),
             pl.BlockSpec((half, D), lambda i: (tile(i), 0)),
-            pl.BlockSpec((1, D, w), lagged),
-            hbm, hbm, whole((R, D)), whole((K, r, w)), whole((2, R, LANES)), whole((16, C)),
-            whole((8, DI)), whole((8, LANES)),
+            hbm, hbm, hbm, whole((R, D)), whole((K, r, w)), whole((2, R, LANES)), whole((16, C)),
+            whole((8, LANES)),
         ],
         out_specs=[whole((R, D)), whole((K + KO, r, w)), whole((r, LANES)), whole((8, C))],
         out_shape=[
@@ -1341,9 +1475,9 @@
         ],
         scratch_shapes=[
             pltpu.VMEM((2, N, r, R), bf16),
-            pltpu.VMEM((HF, 2, N, r, R), bf16),
+            pltpu.VMEM((2, N, r, R), bf16),
             pltpu.VMEM((R, half), f32),
-            pltpu.VMEM((slots, R, w), bf16),
+            pltpu.VMEM((4, R, 2 * w), bf16),
             pltpu.VMEM((2, FRONT + T, LANES), f32),
             pltpu.VMEM((2, FRONT + T, LANES), f32),
             pltpu.VMEM((S, T, LANES), f32),
@@ -1358,7 +1492,9 @@
             pltpu.VMEM((16, DI), f32),
             pltpu.VMEM((16, LANES), f32),
             pltpu.VMEM((8, C), f32),
-            pltpu.SemaphoreType.DMA((2 + 2 * HF,)),
+            pltpu.VMEM((D, 2 * w), bf16),
+            pltpu.SemaphoreType.DMA((4,)),
+            pltpu.SemaphoreType.DMA((2,)),
         ]
         + Reduce.scratch(K + KO, A0, A, r, w)
         + SumAll.scratch(A0, A, (8, C)),
@@ -1370,7 +1506,82 @@
         ),
         name="backward",
     )(proj, proj, ssd, ofull.reshape(DI, D), wfull.reshape(K, D, w), uT.reshape(N, 2, r, R),
-      mT.reshape(N, 2, HF, r, R), go, wl, tabs, pars, skip, hpar)
+      mT.reshape(N, 2, HF, r, R), go, wl, tabs, pars, hpar)
+
+
+def conclude(dims, axis, K, E, dn, tok, go, out, scale, outc, dns, sums, ns, hpar,
+             dtok, outs, dw, dow, dtaps, dbias, ddtb, dalog, dskip, dnorm, dgain, tmp):
+    T, DI, C, H, HD, KW = (dims[k] for k in ("T", "DI", "C", "H", "HD", "KW"))
+    outs[...] = out[...]
+    u = tok[...].astype(f32)
+    rs = lax.rsqrt(jnp.mean(u * u, axis=-1, keepdims=True) + epsilon)
+    u = u * rs
+    d = dn[...] * scale[0:1, :]
+    m = jnp.mean(d * u, axis=-1, keepdims=True)
+    dtok[...] = go[...].astype(f32) + rs * (d - u * m)
+
+    @pl.when(pl.program_id(0) == 0)
+    def _():
+        me = lax.axis_index(axis)
+        r, w = outc.shape[1:]
+        half = w // 2
+        for g in range(K - 1):
+            dw[:, g * half : (g + 1) * half] = outc[g, :, 0:half]
+            dw[:, DI + g * half : DI + (g + 1) * half] = outc[g, :, half:]
+        dw[:, 2 * DI :] = outc[K - 1, :, 0 : E - 2 * DI]
+        cols = dow.shape[1] // w
+        for k in range(outc.shape[0] - K):
+            h, c = k // cols, k % cols
+            dow[h * r : (h + 1) * r, c * w : (c + 1) * w] = outc[K + k]
+
+        def window(size):
+            start = me * size
+            base = jnp.minimum(lax.div(start, LANES), C // LANES - 2) * LANES
+            v = sums[:, pl.ds(pl.multiple_of(base, LANES), 2 * LANES)]
+            return pltpu.roll(v, lax.rem(2 * LANES - (start - base), 2 * LANES), 1)
+
+        Cn, Gn = dbias.shape[0], dgain.shape[0]
+        v = window(Cn)[:, 0:LANES]
+        tmp[...] = jnp.zeros_like(tmp)
+        tmp[0:8, :] = v
+        dtaps[...] = tmp[...].T[0:Cn, 0:KW]
+        dbias[...] = v[KW, 0:Cn]
+        dgain[...] = window(Gn)[KW + 2, 0:Gn]
+        ddtb[...] = sums[KW + 3, 0:H]
+        dalog[...] = sums[KW + 3 : KW + 4, LANES : 2 * LANES][0, 0:H] * hpar[1, 0:H]
+        tmp[0:r, :] = dns[...]
+        tmp[r:, :] = jnp.zeros((LANES - r, LANES), f32)
+        dnorm[...] = jnp.sum(tmp[...].T, axis=0)[0:r] / ns[0, :].astype(f32)
+        tiles = DI // LANES
+        tmp[...] = jnp.zeros_like(tmp)
+        for t in range(tiles):
+            tmp[t : t + 1, :] = sums[KW + 1 : KW + 2, t * LANES : (t + 1) * LANES]
+        row, col = iotas(LANES, LANES)
+        HP = LANES // HD
+        fold = (row // HD == lax.rem(col, HP)).astype(f32)
+        v = jnp.dot(tmp[...], fold, precision=lax.Precision.HIGHEST, preferred_element_type=f32)
+        dskip[...] = jnp.sum(jnp.where(col // HP == row, v, 0.0), axis=0)[0:H]
+
+
+def run_conclude(dims, axis, K, E, dn, tok, go, out, scale, outc, dns, sums, ns, hpar, ro):
+    T, DI, C, H, KW = (dims[k] for k in ("T", "DI", "C", "H", "KW"))
+    R, D = tok.shape
+    r = outc.shape[1]
+    n = D // r
+    rows = pl.BlockSpec((T, D), lambda i: (i, 0))
+    whole = lambda s: pl.BlockSpec(s, lambda i: (0,) * len(s))
+    shapes = [(r, E), (ro, D), (C // n, KW), (C // n,), (H,), (H,), (H,), (r,), (DI // n,)]
+    return pl.pallas_call(
+        functools.partial(conclude, dims, axis, K, E),
+        grid=(R // T,),
+        in_specs=[rows, rows, rows, rows]
+        + [whole(a.shape) for a in (scale, outc, dns, sums, ns, hpar)],
+        out_specs=[rows, rows] + [whole(x) for x in shapes],
+        out_shape=[jax.ShapeDtypeStruct((R, D), f32), jax.ShapeDtypeStruct((R, D), bf16)]
+        + [jax.ShapeDtypeStruct(x, f32) for x in shapes],
+        scratch_shapes=[pltpu.VMEM((LANES, LANES), f32)],
+        name="conclude",
+    )(dn, tok, go, out, scale, outc, dns, sums, ns, hpar)
 
 
 def local(axis, n, tokens, in_weight, conv_weight, conv_bias, dt_bias, a_log, skip_d,
@@ -1392,67 +1603,62 @@
     own = (
         geom is not None and r % 16 == 0 and ro % r == 0 and D % w == 0 and DI % (w // 2) == 0
         and w == 2 * ST + 2 * LANES and E == 2 * DI + 2 * ST + H and H <= LANES
-        and max(Cn, Gn) < LANES and 6 <= KW + 2 <= 8 and ro // r * (D // w) < DI * 2 // w
+        and max(Cn, Gn) < LANES and 6 <= KW + 2 <= 8 and 2 * (ro // r) * (D // w) <= DI * 2 // w + 2
     )
     me = lax.axis_index(axis)
     tok = tokens.reshape(R, D)
     go = grad_out.reshape(R, D)
+    if own:
+        row = lambda v: v.reshape(1, -1)
+        K = DI * 2 // w + 1
+        smalls = [conv_weight.T] + [
+            row(v) for v in (conv_bias, gate_scale, norm_scale, dt_bias, a_log)
+        ]
+        proj, ssd, uT, mT, output, tabs, pars, scale, wl, hpar, wfull, ofull = run_forward_net(
+            dims, axis, geom, K, w, skip_d, tok, go, in_weight, smalls, out_weight
+        )
+        dn, outc, dns, sums = run_backward_net(
+            dims, axis, geom, E, proj, ssd, ofull, wfull, uT, mT, go, wl, tabs, pars, hpar
+        )
+        dtok, output, dw, dow, dtaps, dbias, ddtb, dalog, dskip, dnorm, dgain = run_conclude(
+            dims, axis, K, E, dn, tok, go, output, scale, outc, dns, sums, row(norm_scale), hpar,
+            ro,
+        )
+        return (
+            output.reshape(tokens.shape), dtok.reshape(tokens.shape), dw, dtaps, dbias, ddtb,
+            dalog, dskip, dnorm, dgain, dow,
+        )
     rate = -jnp.exp(a_log)
     hpar = jnp.pad(jnp.stack([dt_bias, rate]), ((0, 6), (0, LANES - H)))
     skip = jnp.broadcast_to(jnp.repeat(skip_d, HD)[None], (8, DI))
     ns = norm_scale.astype(f32)
-    if own:
-        rows = [conv_weight.T, conv_bias[None], gate_scale[None]]
-        pads = jnp.concatenate(
-            [jnp.pad(v, ((0, 0), (0, LANES - 1 - v.shape[1]))) for v in rows]
-            + [jnp.zeros((r - KW - 2, LANES - 1), bf16)],
-            axis=0,
-        )
-        first = jnp.concatenate(
-            [in_weight[:, 2 * DI :], jnp.zeros((r, LANES - H), bf16), pads, norm_scale[:, None]],
-            axis=1,
-        )
-        K = DI * 2 // w + 1
-        rest = in_weight[:, : 2 * DI].reshape(r, 2, K - 1, w // 2).transpose(2, 0, 1, 3)
-        wl = jnp.concatenate([first[None], rest.reshape(K - 1, r, w)], axis=0)
-        proj, ssd, uT, mT, output, tabs, pars, scale, wfull, ofull = run_forward_net(
-            dims, axis, geom, tok, go, wl, out_weight, hpar, skip
-        )
-        dn, outc, dns, sums = run_backward_net(
-            dims, axis, geom, E, proj, ssd, ofull, wfull, uT, mT, go, wl, tabs, pars, skip, hpar
-        )
-        scale = scale[0:1]
-        rest = outc[: K - 1].reshape(K - 1, r, 2, w // 2).transpose(1, 2, 0, 3)
-        dw = jnp.concatenate([rest.reshape(r, 2 * DI), outc[K - 1][:, : E - 2 * DI]], axis=1)
-        dow = outc[K:].reshape(ro // r, D // w, r, w).transpose(0, 2, 1, 3).reshape(ro, D)
-    else:
-        out_full = lax.all_gather(out_weight, axis, axis=0, tiled=True)
-        wfull = lax.all_gather(in_weight, axis, axis=0, tiled=True)
-        conv = lax.all_gather(jnp.concatenate([conv_weight.T, conv_bias[None]]), axis, axis=0)
-        conv = conv.transpose(1, 0, 2).reshape(KW + 1, C).astype(f32)
-        gate = lax.all_gather(gate_scale, axis, axis=0).reshape(1, DI).astype(f32)
-        scale = lax.all_gather(norm_scale, axis, axis=0).reshape(1, D).astype(f32)
-        u = tok.astype(f32)
-        u = u * lax.rsqrt(jnp.mean(u * u, axis=-1, keepdims=True) + epsilon)
-        uh = (u * scale).astype(bf16)
-        proj = jnp.dot(uh, wfull, preferred_element_type=f32).astype(bf16)
-        cpar = jnp.pad(conv, ((0, 8 - KW - 1), (0, 0)))
-        dpar = jnp.concatenate([skip[:1], gate, skip[2:]], axis=0)
-        mixed, ssd, rstd = run_forward(dims, proj, cpar, hpar, dpar)
-        output = jnp.dot(mixed, out_full, preferred_element_type=f32)
-        output = (tok.astype(f32) + output).astype(bf16)
-        d_mixed = lax.dot_general(
-            go, out_full, (((1,), (1,)), ((), ())), preferred_element_type=f32
-        )
-        dproj, small = run_backward(dims, proj, d_mixed, ssd, rstd, cpar, hpar, dpar)
-        left = (((0,), (0,)), ((), ()))
-        g_out = lax.dot_general(mixed, go, left, preferred_element_type=f32).astype(bf16)
-        dow = lax.psum_scatter(g_out, axis, scatter_dimension=0, tiled=True).astype(f32)
-        g_in = lax.dot_general(uh, dproj, left, preferred_element_type=f32).astype(bf16)
-        dw = lax.psum_scatter(g_in, axis, scatter_dimension=0, tiled=True).astype(f32)
-        dns = dw * in_weight.astype(f32)
-        dn = lax.dot_general(dproj, wfull, (((1,), (1,)), ((), ())), preferred_element_type=f32)
-        sums = lax.psum(small, axis)
+    out_full = lax.all_gather(out_weight, axis, axis=0, tiled=True)
+    wfull = lax.all_gather(in_weight, axis, axis=0, tiled=True)
+    conv = lax.all_gather(jnp.concatenate([conv_weight.T, conv_bias[None]]), axis, axis=0)
+    conv = conv.transpose(1, 0, 2).reshape(KW + 1, C).astype(f32)
+    gate = lax.all_gather(gate_scale, axis, axis=0).reshape(1, DI).astype(f32)
+    scale = lax.all_gather(norm_scale, axis, axis=0).reshape(1, D).astype(f32)
+    u = tok.astype(f32)
+    u = u * lax.rsqrt(jnp.mean(u * u, axis=-1, keepdims=True) + epsilon)
+    uh = (u * scale).astype(bf16)
+    proj = jnp.dot(uh, wfull, preferred_element_type=f32).astype(bf16)
+    cpar = jnp.pad(conv, ((0, 8 - KW - 1), (0, 0)))
+    dpar = jnp.concatenate([skip[:1], gate, skip[2:]], axis=0)
+    mixed, ssd, rstd = run_forward(dims, proj, cpar, hpar, dpar)
+    output = jnp.dot(mixed, out_full, preferred_element_type=f32)
+    output = (tok.astype(f32) + output).astype(bf16)
+    d_mixed = lax.dot_general(
+        go, out_full, (((1,), (1,)), ((), ())), preferred_element_type=f32
+    )
+    dproj, small = run_backward(dims, proj, d_mixed, ssd, rstd, cpar, hpar, dpar)
+    left = (((0,), (0,)), ((), ()))
+    g_out = lax.dot_general(mixed, go, left, preferred_element_type=f32).astype(bf16)
+    dow = lax.psum_scatter(g_out, axis, scatter_dimension=0, tiled=True).astype(f32)
+    g_in = lax.dot_general(uh, dproj, left, preferred_element_type=f32).astype(bf16)
+    dw = lax.psum_scatter(g_in, axis, scatter_dimension=0, tiled=True).astype(f32)
+    dns = dw * in_weight.astype(f32)
+    dn = lax.dot_general(dproj, wfull, (((1,), (1,)), ((), ())), preferred_element_type=f32)
+    sums = lax.psum(small, axis)
     u = tok.astype(f32)
     rs = lax.rsqrt(jnp.mean(u * u, axis=-1, keepdims=True) + epsilon)
     u, d = u * rs, dn * scale

time: 459 us -> 389 us (0.85)
  Pallas kernels: 413 us -> 386 us
  local copies, waits for them, and re-layouts: 22.9 us -> 1.46 us
  other arithmetic: 21.1 us -> 0 us
    pallas_call x1, Pallas kernels: 236 us -> 195 us  [run_backward_net(): pl.pallas_call(functools.partial(backward, dims, axis, geom, K, KO, E), g...]
    pallas_call x0 -> x1, Pallas kernels: none -> 13.4 us  [run_conclude(): pl.pallas_call(functools.partial(conclude, dims, axis, K, E), grid=(R //...]
    reduce_sum x4 -> x0, other arithmetic: 9.08 us -> none  [the longest x1 4.88 us: local(): jnp.mean(d * u, axis=-1, keepdims=True)]
    slice x9 -> x0, local copies, waits for them, and re-layouts: 8.98 us -> none  [the longest x1 1.42 us: local(): scale = scale[0:1]]
    add x1 -> x0, other arithmetic: 5.13 us -> none  [local(): go.astype(f32) + rs * (d - u * jnp.mean(d * u, axis=-1, keepdims=True))]
where the time goes in v5:
time: 389 us; the launch traced here: 388 us
  Pallas kernels  386 us (99%)
    pallas_call x1, Pallas kernels, run_backward_net(): pl.pallas_call(functools.partial(backward, dims, axis, geom, K, KO, E), g...  195 us
    pallas_call x1, Pallas kernels, run_forward_net(): pl.pallas_call(functools.partial(forward, dims, axis, geom, K, KO), grid=...  178 us
    pallas_call x1, Pallas kernels, run_conclude(): pl.pallas_call(functools.partial(conclude, dims, axis, K, E), grid=(R //...  13.4 us

profile of v5, /device:TPU:0, one launch (start us, length us, event | category | flops | bytes accessed | tf_op | source)
XLA Modules:
  0.0 388.4 jit_solution(16111147554005867125)
XLA Ops:
  0.6 178.0 %forward.1 = (bf16[13,1024,512]{2,1,0:T(8,128)(2,1)}, f32[1024,3072]{1,0:T(8,128)}, bf16[1536,1024]{1,0:T(8,128)(2,1)}, bf16[3072,1024]{1,0:T(8,128)(2,1)}, bf16...) custom-call(f32[48]{0:T(128)} %skip.1, ...), custom_call_target="tpu_custom_call" | custom-call | flops 20937965568 | bytes 613416960 | tf_op jit(solution)/shard_map/forward/pallas_call | solution.py:1065
  178.7 194.8 %backward.1 = (f32[1024,1536]{1,0:T(8,128)}, f32[19,48,512]{2,1,0:T(8,128)}, f32[48,128]{1,0:T(8,128)}, f32[8,3328]{1,0:T(8,128)}) custom-call(bf16[13,1024,512]{2,1,0:T(8,128)(2,1)} %get-tuple-element.38.proj.proj0, bf16[13,1024,512]{2,1,0:T(8,128)(2,1)} %get-tuple-element.38.proj.proj0, f32[1024,3072]{1,0:T(8,128)} %get-tuple-element.39.ssd, ...), custom_call_target="tpu_custom_call" | custom-call | flops 62813896704 | bytes 920125440 | tf_op jit(solution)/shard_map/backward/pallas_call | solution.py:1458
  373.5 13.4 %conclude.1 = (f32[1024,1536]{1,0:T(8,128)}, bf16[1024,1536]{1,0:T(8,128)(2,1)}, f32[48,6448]{1,0:T(8,128)}, f32[96,1536]{1,0:T(8,128)}, f32[104,4]{1,0:T(8,128)...) custom-call(f32[1024,1536]{1,0:T(8,128)} %get-tuple-element.48.dn, ...), custom_call_target="tpu_custom_call" | custom-call | tf_op jit(solution)/shard_map/conclude/pallas_call | solution.py:1574
  386.9 1.5 copy.22

commit v6 on v5

--- a/solution.py
+++ b/solution.py
@@ -85,6 +85,8 @@
 CHUNK = 512
 VMEM = 67043328
 ROWS = 512
+SEQ_F = 2
+SEQ_B = 2
 
 
 def geometry(n):
@@ -134,12 +136,14 @@
         out += [self.device(self.a0, self.f, self.second(q), self.c) for q in range(1, self.A)]
         return out
 
-    def barrier(self):
-        sem = pltpu.get_barrier_semaphore()
-        peers = self.peers()
-        for peer in peers:
-            pl.semaphore_signal(sem, inc=1, device_id=peer, device_id_type=MESH)
-        pl.semaphore_wait(sem, len(peers))
+    def greet(self):
+        for peer in self.peers():
+            pl.semaphore_signal(
+                pltpu.get_barrier_semaphore(), inc=1, device_id=peer, device_id_type=MESH
+            )
+
+    def meet(self):
+        pl.semaphore_wait(pltpu.get_barrier_semaphore(), len(self.peers()))
 
 
 def columns(j, w):
@@ -154,13 +158,13 @@
 
 
 class Gather:
-    LAG = 2
-    DEEP = 4
+    AFTER = (0, 2, 4, 6, 7)
+    DEEP = 5
     ORDER = (0, 4, 3, 2, 1)
-    WARM = 2
-
-    def __init__(self, at, K, mine, whole, ssem, rsem, lsem, warm=0):
-        self.at, self.K, self.mine, self.whole, self.warm = at, K, mine, whole, warm
+    TURN = 0
+
+    def __init__(self, at, K, mine, whole, ssem, rsem, lsem):
+        self.at, self.K, self.mine, self.whole = at, K, mine, whole
         self.ssem, self.rsem, self.lsem = ssem, rsem, lsem
 
     @staticmethod
@@ -229,17 +233,15 @@
         if stage >= 2:
             run(False)
             return
-        late = lax.rem(j, 3) == 2
+        late = lax.rem(j, 3) == self.TURN
         pl.when(late)(lambda: run(True))
         pl.when(jnp.logical_not(late))(lambda: run(False))
 
     def step(self, i):
         for stage in self.ORDER:
-            j = i - stage
-            early = (j >= 0) & (j < self.warm)
-            j = jnp.where(early, j, i - stage * self.LAG)
-
-            @pl.when(early | ((j >= self.warm) & (j < self.K)))
+            j = i - self.AFTER[stage]
+
+            @pl.when((j >= 0) & (j < self.K))
             def _(stage=stage, j=j):
                 if stage > 0:
                     self.each(stage - 1, j, False, lambda cp: cp.wait_recv())
@@ -258,7 +260,7 @@
     def drain(self):
         for j in range(max(0, self.K - self.DEEP), self.K):
             for stage in range(4):
-                for cp in self.copies(stage, jnp.int32(j), True, j % 3 == 2):
+                for cp in self.copies(stage, jnp.int32(j), True, j % 3 == self.TURN):
                     cp.wait_send()
 
 
@@ -266,8 +268,8 @@
     SLOTS = 3
     LAG = 2
 
-    def __init__(self, at, K, refs):
-        self.at, self.K = at, K
+    def __init__(self, at, K, begun, refs):
+        self.at, self.K, self.begun = at, K, begun
         (self.own0, self.own1, self.own2, self.own3, self.s0, self.s1, self.s2, self.s3,
          self.r0, self.r1, self.r2, self.r3, self.ssem, self.rsem, self.credit) = refs
 
@@ -408,9 +410,9 @@
             finish(j, v)
 
         for k, stage in ((4, stage4), (3, stage3), (2, stage2), (1, stage1)):
-            j = i - k * self.LAG
-
-            @pl.when((j >= 0) & (j < self.K))
+            valid, j = self.begun(i - k * self.LAG)
+
+            @pl.when(valid)
             def _(j=j, k=k, stage=stage):
                 self.arrive(k - 1, j)
                 if k < 4:
@@ -765,6 +767,17 @@
     )(proj, dmixed, ssd, rstd, cpar, hpar, dpar)
 
 
+def several(count, width, body):
+    width = math.gcd(width, count)
+
+    def trip(m, _):
+        for q in range(width):
+            body(m * width + q, q)
+        return 0
+
+    lax.fori_loop(0, count // width, trip, 0)
+
+
 def assemble(parts, size, tiles):
     _, lane = iotas(8, LANES)
     out = []
@@ -800,7 +813,6 @@
     net = Gather(
         at, 2 * K, lambda j: wl.at[lax.div(j, 2), :, part(j)],
         lambda j, a, p, c: wfull.at[place(lax.div(j, 2)), a, p, c, :, part(j)], *sems[:3],
-        warm=Gather.WARM,
     )
     neto = Gather(
         at, 2 * KO, lambda j: ow.at[:, columns(j, wo_cols // 2)],
@@ -809,6 +821,7 @@
 
     @pl.when(i == 0)
     def _():
+        at.greet()
         r, E = inw.shape
         Cn, Gn = bias.shape[1], gains.shape[1]
         zero = jnp.zeros((LANES, LANES), f32)
@@ -830,14 +843,14 @@
         hpar[...] = jnp.zeros_like(hpar)
         hpar[0:1, 0:H] = dtb[...]
         hpar[1:2, 0:H] = -jnp.exp(alog[...])
-        at.barrier()
+        at.meet()
 
     def travel(q):
         net.step(q)
         neto.step(q - 2 * K)
 
     trip = 2 * i
-    i = i - 1
+    i = i - ((Gather.AFTER[4] + 2) // 2 - 4)
     travel(trip)
 
     def fetch_w(j):
@@ -850,7 +863,7 @@
             ofull.at[:, :, :, :, columns(k, wo_cols)], wo.at[slot], osem.at[slot]
         )
 
-    ready = (i == 2) | ((i >= 5) & (i < K + 4))
+    ready = (i >= 4) & (i < K + 4)
     chunk = jnp.maximum(i - 4, 0)
 
     @pl.when(ready)
@@ -861,7 +874,7 @@
     def _():
         fetch_o(i - K - 4).start()
 
-    @pl.when(i == 3)
+    @pl.when(i == 5)
     def _():
         row, col = iotas(T, T)
         mask[...] = jnp.where(col <= row, BIG, -BIG)
@@ -893,7 +906,7 @@
         slot = lax.rem(j, 2)
         h0 = (j - 1) * TC * HP
 
-        def seq(s, _):
+        def seq(s, q):
             rows = pl.ds(pl.multiple_of(s * T, T), T)
             turned = pltpu.roll(ldtab[s], LANES - h0, 1)
             total = None
@@ -901,7 +914,7 @@
                 c0 = pl.multiple_of((j - 1) * half + u * LANES, LANES)
                 conv = conv_of(
                     dims, pj[slot, rows, half + u * LANES : half + (u + 1) * LANES], pars,
-                    pad.at[u], c0,
+                    pad.at[q * TC + u], c0,
                 )
                 x = (conv * sigmoid(conv)).astype(bf16)
                 mix = []
@@ -921,9 +934,8 @@
                 gated[rows, pl.ds(c0, LANES)] = g
                 total = g * g if total is None else total + g * g
             acc[rows, :] += total
-            return 0
-
-        lax.fori_loop(0, S, seq, 0)
+
+        several(S, SEQ_F, seq)
 
     @pl.when(i < K + 5)
     def _():
@@ -933,7 +945,7 @@
     def _():
         fetch_w(chunk).wait()
 
-    @pl.when(i == 2)
+    @pl.when(i == 4)
     def _():
         N = A0 * A * A * 2
         r = D // N
@@ -1058,9 +1070,10 @@
     KO = D // wc
     S = R // T
     assert DI // LANES % KO == 0
-    steps = K + KO + 6
+    shift = (Gather.AFTER[4] + 2) // 2 - 4
+    steps = K + KO + 5 + shift
     whole = lambda s: pl.BlockSpec(s, lambda i: (0,) * len(s), pipeline_mode=pl.Buffered(1))
-    late = lambda i: (0, jnp.clip(i - K - 6, 0, KO - 1))
+    late = lambda i: (0, jnp.clip(i - K - 5 - shift, 0, KO - 1))
     hbm = pl.BlockSpec(memory_space=pl.ANY)
     return pl.pallas_call(
         functools.partial(forward, dims, axis, geom, K, KO),
@@ -1069,8 +1082,8 @@
         + [whole(a.shape) for a in smalls]
         + [whole((ro, D)), pl.BlockSpec((R, wc), late), pl.BlockSpec((R, wc), late)],
         out_specs=[
-            pl.BlockSpec((1, R, w), lambda i: (jnp.clip(i - 5, 0, K - 1), 0, 0)),
-            pl.BlockSpec((R, half), lambda i: (0, jnp.clip(i - 7, 0, K - 2))),
+            pl.BlockSpec((1, R, w), lambda i: (jnp.clip(i - 4 - shift, 0, K - 1), 0, 0)),
+            pl.BlockSpec((R, half), lambda i: (0, jnp.clip(i - 6 - shift, 0, K - 2))),
             whole((D, R)), whole((DI, R)),
             pl.BlockSpec((R, wc), late),
             whole((2, R, LANES)), whole((16, C)), whole((8, D)), whole((K, r, w)),
@@ -1097,7 +1110,7 @@
             pltpu.VMEM((2, R, w), bf16),
             pltpu.VMEM((R, DI), f32),
             pltpu.VMEM((R, DI), bf16),
-            pltpu.VMEM((half // LANES, FRONT + T, LANES), f32),
+            pltpu.VMEM((SEQ_F * half // LANES, FRONT + T, LANES), f32),
             pltpu.VMEM((S, T, LANES), f32),
             pltpu.VMEM((S, LANES, T), f32),
             pltpu.VMEM((S, T, T), f32),
@@ -1137,7 +1150,16 @@
     HF = mT.shape[2]
     each = KO // HF
     pairs = (K + 1) // 2
-    net = Reduce(at, K + KO, refs[:15])
+
+    def begun(t):
+        step = lax.div(t, 2)
+        ends = lax.rem(t, 2) == 1
+        outer = (lax.rem(step, 2) == 0) & (step < 2 * KO)
+        valid = (t >= 0) & ((ends & (step < K)) | (jnp.logical_not(ends) & outer))
+        done = jnp.minimum(lax.div(step + 1, 2), KO)
+        return valid, step + done + (ends & outer).astype(jnp.int32)
+
+    net = Reduce(at, K + KO, begun, refs[:15])
     total = SumAll(at, refs[15:])
 
     def fetches():
@@ -1150,9 +1172,9 @@
 
     @pl.when(i == 0)
     def _():
+        at.greet()
         for cp in fetches() + fetch_half(0):
             cp.start()
-        at.barrier()
         for ref in (cacc, dacc, hacc, dlog, csum, dscores, dns):
             ref[...] = jnp.zeros_like(ref)
         row, col = iotas(T, T)
@@ -1180,6 +1202,7 @@
         lax.fori_loop(0, S, seq, 0)
         for cp in fetches() + fetch_half(0):
             cp.wait()
+        at.meet()
 
     for h in range(1, HF):
 
@@ -1212,10 +1235,10 @@
 
     def send_out():
         k = lax.div(i, 2)
+        net.step(2 * i, finish)
 
         @pl.when((lax.rem(i, 2) == 0) & (k < KO))
         def _():
-            net.step(3 * k, finish)
             net.begin(3 * k, mo, go[:, columns(lax.rem(k, each), w)])
 
     def fetch(t, q):
@@ -1258,7 +1281,7 @@
             go[...], wo[...], (((1,), (1,)), ((), ())), preferred_element_type=f32
         )
 
-        def seq(s, _):
+        def seq(s, q):
             rows = pl.ds(pl.multiple_of(s * T, T), T)
             turned = pltpu.roll(ldtab[s], LANES - h0, 1)
             rb, mb = tabs[0, rows, :], tabs[1, rows, :]
@@ -1268,7 +1291,7 @@
                 lanes = pl.ds(c0, LANES)
                 here = slice(u * LANES, (u + 1) * LANES)
                 there = slice(half + u * LANES, half + (u + 1) * LANES)
-                conv = conv_of(dims, proj[0, rows, there], pars, pad.at[u], c0)
+                conv = conv_of(dims, proj[0, rows, there], pars, pad.at[q * TC + u], c0)
                 sig = sigmoid(conv)
                 x = (conv * sig).astype(bf16)
                 xf = x.astype(f32)
@@ -1316,17 +1339,17 @@
                     jnp.concatenate([hi, lo], axis=1),
                     jnp.concatenate([place, place], axis=0), preferred_element_type=f32,
                 )
-                conv_back(rows, half + u * LANES, c0, core + sk * dssd, conv, sig, u)
+                conv_back(rows, half + u * LANES, c0, core + sk * dssd, conv, sig,
+                          q * TC + u)
                 new = (part, by_head)
                 parts = new if parts is None else tuple(p + q for p, q in zip(parts, new))
             dscores[s] += parts[0]
             dlog[rows, :] += parts[1][0:T]
             csum[rows, :] += parts[1][T:]
-            return 0
-
-        lax.fori_loop(0, S // 2, seq, 0)
+
+        several(S // 2, SEQ_B, seq)
         send_out()
-        lax.fori_loop(S // 2, S, seq, 0)
+        several(S // 2, SEQ_B, lambda s, q: seq(S // 2 + s, q))
 
     @pl.when(i == K - 1)
     def _():
@@ -1375,27 +1398,6 @@
             )
         total.start(0, small[...])
 
-    for stage in range(1, 4):
-
-        @pl.when(i == K - 1 + stage)
-        def _(stage=stage):
-            total.start(stage, total.finish(stage - 1))
-
-    @pl.when(i == K + 3)
-    def _():
-        sums[...] = total.finish(3)
-
-    p = jnp.where(i < K, i + jnp.minimum(lax.div(i, 2) + 1, KO), 2 * i - K + KO)
-    net.step(p, finish)
-
-    @pl.when(i < K)
-    def _():
-        net.begin(p, uo, dpj[slot, :, pl.ds(pl.multiple_of(off, w), w)])
-
-    @pl.when(i >= K)
-    def _():
-        net.step(p + 1, finish)
-
     tail = pairs - dpj.shape[0] + i - K
     t = jnp.where(i < K, lax.div(i - 7, 2), tail)
     turn = jnp.where(
@@ -1432,6 +1434,26 @@
         @pl.when(t + 1 < pairs)
         def _():
             fetch_pair(t + 1, lambda cp: cp.start())
+
+    @pl.when(i >= K - 1)
+    def _():
+        net.step(2 * i, finish)
+
+    net.step(2 * i + 1, finish)
+
+    @pl.when(i < K)
+    def _():
+        net.begin(begun(2 * i + 1)[1], uo, dpj[slot, :, pl.ds(pl.multiple_of(off, w), w)])
+
+    for stage in range(1, 4):
+
+        @pl.when(i == K - 1 + stage)
+        def _(stage=stage):
+            total.start(stage, total.finish(stage - 1))
+
+    @pl.when(i == K + 3)
+    def _():
+        sums[...] = total.finish(3)
 
     @pl.when(i == K + 3)
     def _():
@@ -1478,8 +1500,8 @@
             pltpu.VMEM((2, N, r, R), bf16),
             pltpu.VMEM((R, half), f32),
             pltpu.VMEM((4, R, 2 * w), bf16),
-            pltpu.VMEM((2, FRONT + T, LANES), f32),
-            pltpu.VMEM((2, FRONT + T, LANES), f32),
+            pltpu.VMEM((2 * SEQ_B, FRONT + T, LANES), f32),
+            pltpu.VMEM((2 * SEQ_B, FRONT + T, LANES), f32),
             pltpu.VMEM((S, T, LANES), f32),
             pltpu.VMEM((S, LANES, T), f32),
             pltpu.VMEM((S, T, T), f32),

time: 389 us -> 367 us (0.943)
  Pallas kernels: 386 us -> 365 us
    pallas_call x1, Pallas kernels: 178 us -> 167 us  [run_forward_net(): pl.pallas_call(functools.partial(forward, dims, axis, geom, K, KO), grid=...]
    pallas_call x1, Pallas kernels: 195 us -> 184 us  [run_backward_net(): pl.pallas_call(functools.partial(backward, dims, axis, geom, K, KO, E), g...]
where the time goes in v6:
time: 367 us
  Pallas kernels  365 us (99%)
    pallas_call x1, Pallas kernels, run_backward_net(): pl.pallas_call(functools.partial(backward, dims, axis, geom, K, KO, E), g...  184 us
    pallas_call x1, Pallas kernels, run_forward_net(): pl.pallas_call(functools.partial(forward, dims, axis, geom, K, KO), grid=...  167 us
    pallas_call x1, Pallas kernels, run_conclude(): pl.pallas_call(functools.partial(conclude, dims, axis, K, E), grid=(R //...  13.4 us

profile of v6, /device:TPU:0, one launch (start us, length us, event | category | flops | bytes accessed | tf_op | source)
XLA Modules:
  0.0 366.7 jit_solution(15461281052187829087)
XLA Ops:
  0.6 166.9 %forward.1 = (bf16[13,1024,512]{2,1,0:T(8,128)(2,1)}, f32[1024,3072]{1,0:T(8,128)}, bf16[1536,1024]{1,0:T(8,128)(2,1)}, bf16[3072,1024]{1,0:T(8,128)(2,1)}, bf16...) custom-call(f32[48]{0:T(128)} %skip.1, ...), custom_call_target="tpu_custom_call" | custom-call | flops 20937965568 | bytes 613416960 | tf_op jit(solution)/shard_map/forward/pallas_call | solution.py:1078
  167.6 184.3 %backward.1 = (f32[1024,1536]{1,0:T(8,128)}, f32[19,48,512]{2,1,0:T(8,128)}, f32[48,128]{1,0:T(8,128)}, f32[8,3328]{1,0:T(8,128)}) custom-call(bf16[13,1024,512]{2,1,0:T(8,128)(2,1)} %get-tuple-element.38.proj.proj0, bf16[13,1024,512]{2,1,0:T(8,128)(2,1)} %get-tuple-element.38.proj.proj0, f32[1024,3072]{1,0:T(8,128)} %get-tuple-element.39.ssd, ...), custom_call_target="tpu_custom_call" | custom-call | flops 62813896704 | bytes 920125440 | tf_op jit(solution)/shard_map/backward/pallas_call | solution.py:1480
  351.9 13.4 %conclude.1 = (f32[1024,1536]{1,0:T(8,128)}, bf16[1024,1536]{1,0:T(8,128)(2,1)}, f32[48,6448]{1,0:T(8,128)}, f32[96,1536]{1,0:T(8,128)}, f32[104,4]{1,0:T(8,128)...) custom-call(f32[1024,1536]{1,0:T(8,128)} %get-tuple-element.48.dn, ...), custom_call_target="tpu_custom_call" | custom-call | tf_op jit(solution)/shard_map/conclude/pallas_call | solution.py:1596
  365.2 1.5 copy.22

commit v7 on v6

--- a/solution.py
+++ b/solution.py
@@ -84,8 +84,9 @@
 MESH = pl.DeviceIdType.MESH
 CHUNK = 512
 VMEM = 67043328
-ROWS = 512
+ROWS = 1024
 SEQ_F = 2
+BLOCK = 256
 SEQ_B = 2
 
 
@@ -158,7 +159,7 @@
 
 
 class Gather:
-    AFTER = (0, 2, 4, 6, 7)
+    AFTER = (0, 3, 6, 9, 12)
     DEEP = 5
     ORDER = (0, 4, 3, 2, 1)
     TURN = 0
@@ -1022,7 +1023,7 @@
         k = i - K - 5
         slot = lax.rem(k, 2)
         fetch_o(k).wait()
-        M = 256
+        M = min(R, ROWS)
 
         def rows(m, _):
             at_ = pl.ds(pl.multiple_of(m * M, M), M)
@@ -1590,6 +1591,7 @@
     R, D = tok.shape
     r = outc.shape[1]
     n = D // r
+    T = math.gcd(R, BLOCK)
     rows = pl.BlockSpec((T, D), lambda i: (i, 0))
     whole = lambda s: pl.BlockSpec(s, lambda i: (0,) * len(s))
     shapes = [(r, E), (ro, D), (C // n, KW), (C // n,), (H,), (H,), (H,), (r,), (DI // n,)]

time: 367 us -> 354 us (0.965)
  Pallas kernels: 365 us -> 351 us
    pallas_call x1, Pallas kernels: 167 us -> 154 us  [run_forward_net(): pl.pallas_call(functools.partial(forward, dims, axis, geom, K, KO), grid=...]
where the time goes in v7:
time: 354 us; the launch traced here: 353 us
  Pallas kernels  351 us (99%)
    pallas_call x1, Pallas kernels, run_backward_net(): pl.pallas_call(functools.partial(backward, dims, axis, geom, K, KO, E), g...  185 us
    pallas_call x1, Pallas kernels, run_forward_net(): pl.pallas_call(functools.partial(forward, dims, axis, geom, K, KO), grid=...  154 us
    pallas_call x1, Pallas kernels, run_conclude(): pl.pallas_call(functools.partial(conclude, dims, axis, K, E), grid=(R //...  11.9 us

profile of v7, /device:TPU:0, one launch (start us, length us, event | category | flops | bytes accessed | tf_op | source)
XLA Modules:
  0.0 353.4 jit_solution(6847779466776057836)
XLA Ops:
  0.6 153.9 %forward.1 = (bf16[13,1024,512]{2,1,0:T(8,128)(2,1)}, f32[1024,3072]{1,0:T(8,128)}, bf16[1536,1024]{1,0:T(8,128)(2,1)}, bf16[3072,1024]{1,0:T(8,128)(2,1)}, bf16...) custom-call(f32[48]{0:T(128)} %skip.1, ...), custom_call_target="tpu_custom_call" | custom-call | flops 20937965568 | bytes 613416960 | tf_op jit(solution)/shard_map/forward/pallas_call | solution.py:1079
  154.6 185.4 %backward.1 = (f32[1024,1536]{1,0:T(8,128)}, f32[19,48,512]{2,1,0:T(8,128)}, f32[48,128]{1,0:T(8,128)}, f32[8,3328]{1,0:T(8,128)}) custom-call(bf16[13,1024,512]{2,1,0:T(8,128)(2,1)} %get-tuple-element.38.proj.proj0, bf16[13,1024,512]{2,1,0:T(8,128)(2,1)} %get-tuple-element.38.proj.proj0, f32[1024,3072]{1,0:T(8,128)} %get-tuple-element.39.ssd, ...), custom_call_target="tpu_custom_call" | custom-call | flops 62813896704 | bytes 920125440 | tf_op jit(solution)/shard_map/backward/pallas_call | solution.py:1481
  340.0 11.9 %conclude.1 = (f32[1024,1536]{1,0:T(8,128)}, bf16[1024,1536]{1,0:T(8,128)(2,1)}, f32[48,6448]{1,0:T(8,128)}, f32[96,1536]{1,0:T(8,128)}, f32[104,4]{1,0:T(8,128)...) custom-call(f32[1024,1536]{1,0:T(8,128)} %get-tuple-element.48.dn, ...), custom_call_target="tpu_custom_call" | custom-call | tf_op jit(solution)/shard_map/conclude/pallas_call | solution.py:1598
  351.9 1.5 copy.22
